TPU v7x, 256 devices: a whole 4x4x8 slice. The times are simulated.
256 devices in a mesh: pair: 32 (over x, z_hi, core), aux: 8 (over z_lo, y).
Axes of the slice: x: 4, y: 4, z: 8 (z_hi: 4, z_lo: 2; z = z_hi * 2 + z_lo), core: 2. Of those that a mesh axis runs over, the one named last changes fastest.
Arguments:
- integrals: float32 [32, 640, 4096], P(None, 'aux', 'pair'), may hold values from -6 to 6
- factor: float32 [4096, 4096], P('aux', 'pair'), may hold values from -1 to 2, as said below
- diag_inverse: float32 [8, 512, 512], P('aux'), may hold values from -1 to 1, as said below
Outputs:
- transformed: float32 [32, 640, 4096], P('pair', None, 'aux')
Inputs may be any that keep to these rules, and one draw needn't show every extreme that they name: factor is zero above its diagonal. diag_inverse[j] is the inverse, up to rounding, of the factor's j-th diagonal block of 512 x 512.
All inputs are finite; a program needn't handle non-finite values.
Results may differ from a plain program's by a relative error of at most 0.0001.
Values sent between devices are 32-bit elements; how exact they have to be, the bound alone decides.
No kernel may reach another device: no remote copies, remote signals or barrier semaphores. Data moves between devices by JAX's collectives and lax.ppermute only.
A program may use at most 128 MiB of HBM per device.

v0:
```python
import jax
import jax.numpy as jnp
from jax import lax
from jax.experimental import pallas as pl
from jax.experimental.pallas import tpu as pltpu
from jax.sharding import PartitionSpec as P


NX, NY, NZ = 4, 4, 8
ALL = ("pair", "aux")
EARLY, LATE = 4, 3
SLOTS = EARLY + LATE
PANELS, PANEL, LANES, ROWS = 8, 512, 128, 80


def device_id(x, y, z, core):
    return ((x * NZ // 2 + z // 2) * 2 + core) * 8 + (z % 2) * NY + y


def shift(value, dx=0, dy=0, dz=0, core=0):
    pairs = [
        (device_id(x, y, z, c), device_id((x + dx) % NX, (y + dy) % NY, (z + dz) % NZ, (c + core) % 2))
        for x in range(NX)
        for y in range(NY)
        for z in range(NZ)
        for c in range(2)
    ]
    return lax.ppermute(value, ALL, pairs)


def along(axis):
    return lambda value, d: shift(value, **{axis: d})


def ring_of_eight(piece):
    near = [shift(piece, dz=d) for d in (1, -1, 2, -2)]
    one, minus_one, two, minus_two = lax.optimization_barrier(near)
    three, minus_three = shift(two, dz=1), shift(minus_two, dz=-1)
    four = jnp.concatenate([shift(two[:EARLY], dz=2), shift(minus_two[EARLY:], dz=-2)])
    return jnp.stack([piece, one, two, three, four, minus_three, minus_two, minus_one])


def spread(factor, pair):
    halves = factor.reshape(2, 8, 32, LANES)
    halves = jnp.where(pair < 16, halves, halves[::-1]).reshape(16, 32, LANES)
    groups = [[8 * p + a for p in (low, 31 - low) for a in range(8)] for low in range(16)]
    return lax.all_to_all(halves, ALL, 0, 0, axis_index_groups=groups, tiled=True)


def share(both, column):
    least = jnp.minimum(column, 7 - column)
    held = []
    for slot in range(SLOTS):
        paired = (slot + 9) // 2 if slot % 2 else 8 + (slot + 8) // 2
        index = jnp.where(slot < 7 - 2 * least, slot + least + 1, paired)
        held.append(lax.dynamic_index_in_dim(both, index, 0, keepdims=False))
    return jnp.stack(held)


def start(factor, diag_inverse, pair):
    half = lax.dynamic_slice(diag_inverse[0], (256 * (pair % 2), 0), (256, PANEL))
    neighbour = lax.ppermute(half, "aux", [(a, (a + 4) % 8) for a in range(8)])
    both = spread(factor, pair)
    both, neighbour = lax.optimization_barrier((both, neighbour))
    own = jnp.stack([half, neighbour])
    up, down = shift(own, dy=1), shift(own, dy=-1)
    column = ring_of_eight(share(both, pair // 4))
    column, up, down = lax.optimization_barrier((column, up, down))
    return column, [own, up, down]


def swap(values):
    return [shift(value, core=1) for value in values]


def gather(column, diagonals, integrals):
    blocks = [column[:, :EARLY], column[:, EARLY:]]
    first = [along("dx"), along("dy")]
    second = [along("dy"), along("dx")]
    near = [(one(block, 1), one(block, -1)) for one, block in zip(first, blocks)]
    near, diagonals = lax.optimization_barrier((near, diagonals))
    far = [(one(up[:4], 1), one(down[4:], -1)) for one, (up, down) in zip(first, near)]
    ends = jnp.stack([shift(diagonals[1][0], dy=1), shift(diagonals[2][1], dy=-1)])
    whole = [jnp.concatenate([block, up, down, *ends]) for block, (up, down), ends in zip(blocks, near, far)]
    whole, ends, integrals = lax.optimization_barrier((whole, ends, integrals))
    near = [(two(block, 1), two(block, -1)) for two, block in zip(second, whole)]
    swapped = swap(whole)
    swapped, diagonals, ends = lax.optimization_barrier((swapped, diagonals, ends))
    rows = lax.all_to_all(integrals, "pair", 0, 0, tiled=True)
    diagonals = jnp.stack([*diagonals, ends])
    swapped += swap([diagonals])
    near, swapped, rows = lax.optimization_barrier((near, swapped, rows))
    far = [(two(up[:16], 1), two(down[16:], -1)) for two, (up, down) in zip(second, near)]
    swapped_near = [swap(values) for values in near]
    far, swapped_near = lax.optimization_barrier((far, swapped_near))
    gathered = []
    for color in range(2):
        gathered += [whole[color], *near[color], *far[color]]
        gathered += [swapped[color], *swapped_near[color], *swap(far[color])]
    return rows, (diagonals, swapped[2]), gathered


LAYOUT = ((0, 0, 4), (1, 0, 4), (2, 0, 4), (3, 0, 2), (3, 2, 2))


def position(delta):
    delta = lax.rem(delta + 4, 4)
    return jnp.where(delta == 3, 1, jnp.where(delta == 0, 0, delta + 1))


def kernel(*refs):
    place_ref, x_ref = refs[:2]
    diagonals, arrays = refs[2:4], refs[4:24]
    out_ref, held, inverses, remain, parts, inverse_sem, early_sem, late_sem = refs[24:]
    x, y, z, core = (place_ref[i] for i in range(4))

    for other in range(2):
        pltpu.make_async_copy(diagonals[other], inverses.at[other], inverse_sem).start()
    for other in range(2):
        for number, (second, block, count) in enumerate(LAYOUT):
            ref = arrays[5 * other + number]
            to = held.at[other, second, pl.ds(block, count), :, pl.ds(0, EARLY)]
            pltpu.make_async_copy(ref, to, early_sem).start()
    for other in range(2):
        for number, (second, block, count) in enumerate(LAYOUT):
            ref = arrays[10 + 5 * other + number]
            to = held.at[other, pl.ds(block, count), second, :, pl.ds(EARLY, LATE)]
            pltpu.make_async_copy(ref, to, late_sem).start()
    y_positions = [position(sy - y) for sy in range(NY)]

    def slab(p, slot):
        x_position = position(lax.div(p, 8) - x)
        other = lax.rem(p + core, 2)
        sz = 2 * lax.rem(lax.div(p, 2), 4)
        rows = []
        for z_lo in range(2):
            d = lax.rem(z - sz - z_lo + NZ, NZ)
            rows += [held[other, y_positions[sy], x_position, d, slot] for sy in range(NY)]
        return jnp.concatenate(rows)

    def product(left, load):
        halves = []
        for half in range(2):
            total = None
            for side in range(2):
                weight = load(half, side)
                high = weight.astype(jnp.bfloat16)
                low = (weight - high.astype(jnp.float32)).astype(jnp.bfloat16)
                part = left[:, 256 * side : 256 * (side + 1)]
                dims = (((1,), (1,)), ((), ()))
                twice = lax.dot_general(part, high, dims, preferred_element_type=jnp.float32)
                once = lax.dot_general(part[:ROWS], low, dims, preferred_element_type=jnp.float32)
                piece = twice[:ROWS] + (twice[ROWS:] + once)
                total = piece if total is None else total + piece
            halves.append(total)
        return jnp.concatenate(halves, axis=1)

    def split(value):
        high = value.astype(jnp.bfloat16)
        low = (value - high.astype(jnp.float32)).astype(jnp.bfloat16)
        return jnp.concatenate([high, low], axis=0)

    def panel(j, carry):
        @pl.when(j == EARLY + 1)
        def _():
            late = held.at[:, :, :, :, pl.ds(EARLY, LATE)]
            pltpu.make_async_copy(late, late, late_sem).wait()

        remain[...] = jnp.concatenate([x_ref[4 * j + s] for s in range(4)], axis=1)

        def update(k, carry):
            low_slot = jnp.where(j < 8 - k, j - k - 1, 2 * j - 9)
            slot = jnp.where(k < 4, low_slot, 2 * j - 8)

            def load(half, side):
                columns = [4 * k + 2 * side + s for s in range(2)]
                return jnp.concatenate([slab(31 - p if half else p, slot) for p in columns], axis=1)

            remain[...] -= product(parts[k], load)
            return carry

        lax.fori_loop(0, j, update, 0)

        def load(half, side):
            other, z_lo = lax.rem(core + half, 2), lax.rem(z + lax.div(j, 4), 2)
            at = position(lax.rem(j, 4) - y)
            return inverses[other, at, z_lo, :, 256 * side : 256 * (side + 1)]

        solved = product(split(remain[...]), load)
        out_ref[j] = solved
        parts[j] = split(solved)
        return carry

    pltpu.make_async_copy(inverses, inverses, inverse_sem).wait()
    early = held.at[:, :, :, :, pl.ds(0, EARLY)]
    pltpu.make_async_copy(early, early, early_sem).wait()
    lax.fori_loop(0, PANELS, panel, 0)


def solve(place, rows, diagonals, arrays):
    arrays = [v.reshape(-1, NZ, *v.shape[1:]) for v in arrays]
    return pl.pallas_call(
        kernel,
        out_shape=jax.ShapeDtypeStruct((PANELS, ROWS, PANEL), jnp.float32),
        in_specs=[pl.BlockSpec(memory_space=pltpu.SMEM), pl.BlockSpec(memory_space=pltpu.VMEM)]
        + [pl.BlockSpec(memory_space=pl.ANY)] * (len(diagonals) + len(arrays)),
        out_specs=pl.BlockSpec(memory_space=pltpu.VMEM),
        scratch_shapes=[
            pltpu.VMEM((2, 4, 4, NZ, SLOTS, 32, LANES), jnp.float32),
            pltpu.VMEM((2, 4, 2, 256, PANEL), jnp.float32),
            pltpu.VMEM((ROWS, PANEL), jnp.float32),
            pltpu.VMEM((PANELS, 2 * ROWS, PANEL), jnp.bfloat16),
            pltpu.SemaphoreType.DMA,
            pltpu.SemaphoreType.DMA,
            pltpu.SemaphoreType.DMA,
        ],
        compiler_params=pltpu.CompilerParams(vmem_limit_bytes=48 * 2**20),
        cost_estimate=pl.CostEstimate(flops=16 * 10**9, bytes_accessed=40 * 10**6, transcendentals=0),
    )(place, rows, *diagonals, *arrays)


def local(integrals, factor, diag_inverse):
    pair, aux = lax.axis_index("pair"), lax.axis_index("aux")
    x, z, core = pair // 8, (pair // 2) % 4 * 2 + aux // NY, pair % 2
    place = jnp.stack([x, aux % NY, z, core]).astype(jnp.int32)

    column, diagonals = start(factor, diag_inverse, pair)
    rows, diagonals, gathered = gather(column, diagonals, integrals)
    solved = solve(place, rows, diagonals, gathered)
    result = lax.all_to_all(solved, "aux", 0, 0, tiled=True)
    return result.reshape(1, 8 * ROWS, PANEL)


def solution(mesh):
    in_specs = (P(None, "aux", "pair"), P("aux", "pair"), P("aux", None, None))
    out_specs = P("pair", None, "aux")
    return jax.shard_map(local, mesh=mesh, in_specs=in_specs, out_specs=out_specs, check_vma=False)
```

profile of v0, /device:TPU:56, one launch (start us, length us, event | category | flops | bytes accessed | tf_op | source)
XLA Modules:
  0.0 281.3 jit_solution(18153352362292947772)
XLA Ops:
  1.5 1.8 reverse_select_fusion
  3.2 12.3 %all-to-all-start = ((f32[16,32,128]{2,1,0:T(8,128)}), f32[16,32,128]{2,1,0:T(8,128)S(1)}, u32[]{:S(2)}, u32[]{:S(2)}) async-start(f32[16,32,128]{2,1,0:T(8,128)} %bitcast.5), calls=%async_computation | async-start | bytes 524288 | tf_op jit(solution)/shard_map/all_to_all | solution.py:47
  15.5 9.9 %all-to-all-done = f32[16,32,128]{2,1,0:T(8,128)S(1)} async-done(((f32[16,32,128]{2,1,0:T(8,128)}), f32[16,32,128]{2,1,0:T(8,128)S(1)}, u32[]{:S(2)}, u32[]{:S(2)}) %all-to-all-start) | async-done | bytes 262176 | tf_op jit(solution)/shard_map/all_to_all | solution.py:47
  28.5 2.0 collective-permute-start.1
  31.8 1.8 collective-permute-done.4
  34.9 1.8 collective-permute-done.3
  37.3 2.4 collective-permute-start.8
  41.8 4.2 %collective-permute-done.5 = f32[7,32,128]{2,1,0:T(8,128)S(1)} collective-permute-done((f32[7,32,128]{2,1,0:T(8,128)S(1)}, f32[7,32,128]{2,1,0:T(8,128)S(1)}, u32[]{:S(2)}, u32[]{:S(2)}) %collective-permute-start.5) | collective-permute-done | bytes 114720 | tf_op jit(solution)/shard_map/ppermute | solution.py:28
  47.5 5.6 %collective-permute-done.6 = f32[4,32,128]{2,1,0:T(8,128)S(1)} collective-permute-done((f32[4,32,128]{2,1,0:T(8,128)S(1)}, f32[4,32,128]{2,1,0:T(8,128)S(1)}, u32[]{:S(2)}, u32[]{:S(2)}) %collective-permute-start.6) | collective-permute-done | bytes 65568 | tf_op jit(solution)/shard_map/ppermute | solution.py:28
  53.2 5.4 %collective-permute-done.10 = f32[2,256,512]{2,1,0:T(8,128)S(1)} collective-permute-done((f32[2,256,512]{2,1,0:T(8,128)S(1)}, f32[2,256,512]{2,1,0:T(8,128)S(1)}, u32[]{:S(2)}, u32[]{:S(2)}) %collective-permute-start.10) | collective-permute-done | bytes 1048608 | tf_op jit(solution)/shard_map/ppermute | solution.py:28
  62.7 2.2 collective-permute-start.13
  64.9 8.6 %collective-permute-done.14 = f32[8,3,32,128]{3,2,1,0:T(8,128)S(1)} collective-permute-done((f32[8,3,32,128]{3,2,1,0:T(8,128)S(1)}, f32[8,3,32,128]{3,2,1,0:T(8,128)S(1)}, u32[]{:S(2)}, u32[]{:S(2)}) %collective-permute-start.14) | collective-permute-done | bytes 393248 | tf_op jit(solution)/shard_map/ppermute | solution.py:28
  76.3 2.0 collective-permute-start.17
  78.9 3.2 %collective-permute-start.19 = (f32[256,512]{1,0:T(8,128)S(1)}, f32[256,512]{1,0:T(8,128)S(1)}, u32[]{:S(2)}, u32[]{:S(2)}) collective-permute-start(f32[256,512]{1,0:T(8,128)S(1)} %slice_bitcast_fusion.1), channel_id=1, source_target_pairs={{0,1},{8,9},{4,5},{12,13},{16,17},{24,25},{20,21},{28,29},{32,33},... | collective-permute-start | bytes 1572872 | tf_op jit(solution)/shard_map/ppermute | solution.py:28
  82.2 1.8 collective-permute-done.17
  85.9 4.6 %collective-permute-done.16 = f32[4,4,32,128]{3,2,1,0:T(8,128)S(1)} collective-permute-done((f32[4,4,32,128]{3,2,1,0:T(8,128)S(1)}, f32[4,4,32,128]{3,2,1,0:T(8,128)S(1)}, u32[]{:S(2)}, u32[]{:S(2)}) %collective-permute-start.16) | collective-permute-done | bytes 262176 | tf_op jit(solution)/shard_map/ppermute | solution.py:28
  90.4 2.7 collective-permute-done.20
  93.8 5.9 %collective-permute-done.26 = f32[32,3,32,128]{3,2,1,0:T(8,128)S(1)} collective-permute-done((f32[32,3,32,128]{3,2,1,0:T(8,128)S(1)}, f32[32,3,32,128]{3,2,1,0:T(8,128)S(1)}, u32[]{:S(2)}, u32[]{:S(2)}) %collective-permute-start.26) | collective-permute-done | bytes 1572896 | tf_op jit(solution)/shard_map/ppermute | solution.py:28
  101.5 2.7 pad_maximum_fusion.refs_2_
  104.4 7.1 %all-to-all-start.1 = ((f32[32,80,128]{2,1,0:T(8,128)}), f32[32,80,128]{2,1,0:T(8,128)S(1)}, u32[]{:S(2)}, u32[]{:S(2)}) async-start(f32[32,80,128]{2,1,0:T(8,128)} %param.3), calls=%async_computation.1 | async-start | bytes 2621440 | tf_op jit(solution)/shard_map/all_to_all | solution.py:89
  111.8 3.0 %collective-permute-start.21 = (f32[32,4,32,128]{3,2,1,0:T(8,128)}, f32[32,4,32,128]{3,2,1,0:T(8,128)}, u32[]{:S(2)}, u32[]{:S(2)}) collective-permute-start(f32[32,4,32,128]{3,2,1,0:T(8,128)} %copy-done.8), channel_id=1, source_target_pairs={{0,1},{8,9},{4,5},{12,13},{16,17},{24,25},{20,21},{28,29},{32,33},... | collective-permute-start | bytes 6291464 | tf_op jit(solution)/shard_map/ppermute | solution.py:28
  114.8 3.0 %collective-permute-start.24 = (f32[32,3,32,128]{3,2,1,0:T(8,128)}, f32[32,3,32,128]{3,2,1,0:T(8,128)S(1)}, u32[]{:S(2)}, u32[]{:S(2)}) collective-permute-start(f32[32,3,32,128]{3,2,1,0:T(8,128)} %copy-done.9), channel_id=1, source_target_pairs={{0,192},{8,200},{4,196},{12,204},{16,208},{24,216},{20,212},{28,22... | collective-permute-start | bytes 4718600 | tf_op jit(solution)/shard_map/ppermute | solution.py:28
  117.9 44.3 %collective-permute-done.24 = f32[32,3,32,128]{3,2,1,0:T(8,128)S(1)} collective-permute-done((f32[32,3,32,128]{3,2,1,0:T(8,128)}, f32[32,3,32,128]{3,2,1,0:T(8,128)S(1)}, u32[]{:S(2)}, u32[]{:S(2)}) %collective-permute-start.24) | collective-permute-done | bytes 1572896 | tf_op jit(solution)/shard_map/ppermute | solution.py:28
  162.2 2.3 collective-permute-done.23
  168.7 1.8 collective-permute-start.31
  173.1 14.1 %collective-permute-done.31 = f32[16,3,32,128]{3,2,1,0:T(8,128)} collective-permute-done((f32[16,3,32,128]{3,2,1,0:T(8,128)S(1)}, f32[16,3,32,128]{3,2,1,0:T(8,128)}, u32[]{:S(2)}, u32[]{:S(2)}) %collective-permute-start.31) | collective-permute-done | bytes 786464 | tf_op jit(solution)/shard_map/ppermute | solution.py:28
  187.2 4.3 %collective-permute-done.30 = f32[16,3,32,128]{3,2,1,0:T(8,128)} collective-permute-done((f32[16,3,32,128]{3,2,1,0:T(8,128)S(1)}, f32[16,3,32,128]{3,2,1,0:T(8,128)}, u32[]{:S(2)}, u32[]{:S(2)}) %collective-permute-start.30) | collective-permute-done | bytes 786464 | tf_op jit(solution)/shard_map/ppermute | solution.py:28
  192.9 4.4 %collective-permute-done.29 = f32[16,4,32,128]{3,2,1,0:T(8,128)S(1)} collective-permute-done((f32[16,4,32,128]{3,2,1,0:T(8,128)S(1)}, f32[16,4,32,128]{3,2,1,0:T(8,128)S(1)}, u32[]{:S(2)}, u32[]{:S(2)}) %collective-permute-start.29) | collective-permute-done | bytes 1048608 | tf_op jit(solution)/shard_map/ppermute | solution.py:28
  198.3 21.7 %collective-permute-done.28 = f32[16,4,32,128]{3,2,1,0:T(8,128)S(1)} collective-permute-done((f32[16,4,32,128]{3,2,1,0:T(8,128)S(1)}, f32[16,4,32,128]{3,2,1,0:T(8,128)S(1)}, u32[]{:S(2)}, u32[]{:S(2)}) %collective-permute-start.28) | collective-permute-done | bytes 1048608 | tf_op jit(solution)/shard_map/ppermute | solution.py:28
  223.6 3.2 %collective-permute-done.38 = f32[16,3,32,128]{3,2,1,0:T(8,128)} collective-permute-done((f32[16,3,32,128]{3,2,1,0:T(8,128)}, f32[16,3,32,128]{3,2,1,0:T(8,128)}, u32[]{:S(2)}, u32[]{:S(2)}) %collective-permute-start.38) | collective-permute-done | bytes 786464 | tf_op jit(solution)/shard_map/ppermute | solution.py:28
  228.0 28.4 %shard_map.37 = f32[8,80,512]{2,1,0:T(8,128)} custom-call(s32[4]{0:T(128)S(1)} %pad_add_fusion.refs_0_, f32[32,80,128]{2,1,0:T(8,128)} %copy-done.1, f32[4,2,256,512]{3,2,1,0:T(8,128)} %pad_maximum_fusion.refs_2_, f32[4,2,256,512]{3,2,1,0:T(8,128)} %collective-permute-done.27.refs_3_, f32[4,8,4,32,128]{4,3,2,1,0:T(8,128)} %bitcast.72, ...), custom_call_target="tpu_custom_call" | custom-call | flops 16000000000 | bytes 40000000 | tf_op jit(solution)/shard_map/pallas_call | solution.py:202
  256.4 23.8 %all_to_all.15 = f32[8,80,512]{2,1,0:T(8,128)S(1)} all-to-all(f32[8,80,512]{2,1,0:T(8,128)} %shard_map.37), channel_id=1, replica_groups=mesh['pair'=32,'aux'=8] {'aux'}, dimensions={0} | all-to-all | bytes 2621440 | tf_op jit(solution)/shard_map/all_to_all | solution.py:230
  (131 shorter events, 38.3 us)
Async XLA Ops:
  1.3 24.1 %collective-permute-start = (f32[256,512]{1,0:T(8,128)S(1)}, f32[256,512]{1,0:T(8,128)S(1)}, u32[]{:S(2)}, u32[]{:S(2)}) collective-permute-start(f32[256,512]{1,0:T(8,128)S(1)} %fusion.2), channel_id=1, source_target_pairs={{0,4},{1,5},{2,6},{3,7},{4,0},{5,1},{6,2},{7,3},{8,12},{9,13},{10,... | collective-permute-start | bytes 1572872 | tf_op jit(solution)/shard_map/ppermute | solution.py:62
  3.2 22.2 %all-to-all-start = ((f32[16,32,128]{2,1,0:T(8,128)}), f32[16,32,128]{2,1,0:T(8,128)S(1)}, u32[]{:S(2)}, u32[]{:S(2)}) async-start(f32[16,32,128]{2,1,0:T(8,128)} %bitcast.5), calls=%async_computation | async-start | bytes 524288 | tf_op jit(solution)/shard_map/all_to_all | solution.py:47
  25.5 8.1 %collective-permute-start.4 = (f32[7,32,128]{2,1,0:T(8,128)S(1)}, f32[7,32,128]{2,1,0:T(8,128)S(1)}, u32[]{:S(2)}, u32[]{:S(2)}) collective-permute-start(f32[7,32,128]{2,1,0:T(8,128)S(1)} %constant_dynamic-update-slice_fusion), channel_id=1, source_target_pairs={{0,48},{8,56},{4,52},{12,60},{16,0},{24,8},{20,4},{28,12},{32,16},... | collective-permute-start | bytes 344072 | tf_op jit(solution)/shard_map/ppermute | solution.py:28
  27.0 9.7 %collective-permute-start.3 = (f32[7,32,128]{2,1,0:T(8,128)S(1)}, f32[7,32,128]{2,1,0:T(8,128)S(1)}, u32[]{:S(2)}, u32[]{:S(2)}) collective-permute-start(f32[7,32,128]{2,1,0:T(8,128)S(1)} %constant_dynamic-update-slice_fusion), channel_id=1, source_target_pairs={{0,16},{8,24},{4,20},{12,28},{16,32},{24,40},{20,36},{28,44},{32,4... | collective-permute-start | bytes 344072 | tf_op jit(solution)/shard_map/ppermute | solution.py:28
  28.5 8.1 %collective-permute-start.2 = (f32[7,32,128]{2,1,0:T(8,128)S(1)}, f32[7,32,128]{2,1,0:T(8,128)S(1)}, u32[]{:S(2)}, u32[]{:S(2)}) collective-permute-start(f32[7,32,128]{2,1,0:T(8,128)S(1)} %constant_dynamic-update-slice_fusion), channel_id=1, source_target_pairs={{0,52},{8,60},{4,0},{12,8},{16,4},{24,12},{20,16},{28,24},{32,20},... | collective-permute-start | bytes 344072 | tf_op jit(solution)/shard_map/ppermute | solution.py:28
  28.5 8.8 %collective-permute-start.1 = (f32[7,32,128]{2,1,0:T(8,128)S(1)}, f32[7,32,128]{2,1,0:T(8,128)S(1)}, u32[]{:S(2)}, u32[]{:S(2)}) collective-permute-start(f32[7,32,128]{2,1,0:T(8,128)S(1)} %constant_dynamic-update-slice_fusion), channel_id=1, source_target_pairs={{0,4},{8,12},{4,16},{12,24},{16,20},{24,28},{20,32},{28,40},{32,36... | collective-permute-start | bytes 344072 | tf_op jit(solution)/shard_map/ppermute | solution.py:28
  30.6 28.0 %collective-permute-start.10 = (f32[2,256,512]{2,1,0:T(8,128)S(1)}, f32[2,256,512]{2,1,0:T(8,128)S(1)}, u32[]{:S(2)}, u32[]{:S(2)}) collective-permute-start(f32[2,256,512]{2,1,0:T(8,128)S(1)} %pad_maximum_fusion.1), channel_id=1, source_target_pairs={{0,3},{8,11},{4,7},{12,15},{16,19},{24,27},{20,23},{28,31},{32,35}... | collective-permute-start | bytes 3145736 | tf_op jit(solution)/shard_map/ppermute | solution.py:28
  33.6 25.7 %collective-permute-start.9 = (f32[2,256,512]{2,1,0:T(8,128)S(1)}, f32[2,256,512]{2,1,0:T(8,128)S(1)}, u32[]{:S(2)}, u32[]{:S(2)}) collective-permute-start(f32[2,256,512]{2,1,0:T(8,128)S(1)} %pad_maximum_fusion.1), channel_id=1, source_target_pairs={{0,1},{8,9},{4,5},{12,13},{16,17},{24,25},{20,21},{28,29},{32,33},... | collective-permute-start | bytes 3145736 | tf_op jit(solution)/shard_map/ppermute | solution.py:28
  37.3 15.8 %collective-permute-start.8 = (f32[7,32,128]{2,1,0:T(8,128)S(1)}, f32[7,32,128]{2,1,0:T(8,128)S(1)}, u32[]{:S(2)}, u32[]{:S(2)}) collective-permute-start(f32[7,32,128]{2,1,0:T(8,128)S(1)} %collective-permute-done.4), channel_id=1, source_target_pairs={{0,52},{8,60},{4,0},{12,8},{16,4},{24,12},{20,16},{28,24},{32,20},... | collective-permute-start | bytes 344072 | tf_op jit(solution)/shard_map/ppermute | solution.py:28
  39.8 7.7 %collective-permute-start.7 = (f32[3,32,128]{2,1,0:T(8,128)S(1)}, f32[3,32,128]{2,1,0:T(8,128)S(1)}, u32[]{:S(2)}, u32[]{:S(2)}) collective-permute-start(f32[3,32,128]{2,1,0:T(8,128)S(1)} %slice.43), channel_id=1, source_target_pairs={{0,48},{8,56},{4,52},{12,60},{16,0},{24,8},{20,4},{28,12},{32,16},... | collective-permute-start | bytes 147464 | tf_op jit(solution)/shard_map/ppermute | solution.py:28
  59.4 14.1 %collective-permute-start.12 = (f32[8,4,32,128]{3,2,1,0:T(8,128)S(1)}, f32[8,4,32,128]{3,2,1,0:T(8,128)S(1)}, u32[]{:S(2)}, u32[]{:S(2)}) collective-permute-start(f32[8,4,32,128]{3,2,1,0:T(8,128)S(1)} %get-tuple-element.91), channel_id=1, source_target_pairs={{0,192},{8,200},{4,196},{12,204},{16,208},{24,216},{20,212},{28,22... | collective-permute-start | bytes 1572872 | tf_op jit(solution)/shard_map/ppermute | solution.py:28
  60.6 14.2 %collective-permute-start.11 = (f32[8,4,32,128]{3,2,1,0:T(8,128)S(1)}, f32[8,4,32,128]{3,2,1,0:T(8,128)S(1)}, u32[]{:S(2)}, u32[]{:S(2)}) collective-permute-start(f32[8,4,32,128]{3,2,1,0:T(8,128)S(1)} %get-tuple-element.91), channel_id=1, source_target_pairs={{0,64},{8,72},{4,68},{12,76},{16,80},{24,88},{20,84},{28,92},{32,9... | collective-permute-start | bytes 1572872 | tf_op jit(solution)/shard_map/ppermute | solution.py:28
  61.6 11.9 %collective-permute-start.14 = (f32[8,3,32,128]{3,2,1,0:T(8,128)S(1)}, f32[8,3,32,128]{3,2,1,0:T(8,128)S(1)}, u32[]{:S(2)}, u32[]{:S(2)}) collective-permute-start(f32[8,3,32,128]{3,2,1,0:T(8,128)S(1)} %get-tuple-element.90), channel_id=1, source_target_pairs={{0,3},{8,11},{4,7},{12,15},{16,19},{24,27},{20,23},{28,31},{32,35}... | collective-permute-start | bytes 1179656 | tf_op jit(solution)/shard_map/ppermute | solution.py:28
  62.7 10.8 %collective-permute-start.13 = (f32[8,3,32,128]{3,2,1,0:T(8,128)S(1)}, f32[8,3,32,128]{3,2,1,0:T(8,128)S(1)}, u32[]{:S(2)}, u32[]{:S(2)}) collective-permute-start(f32[8,3,32,128]{3,2,1,0:T(8,128)S(1)} %get-tuple-element.90), channel_id=1, source_target_pairs={{0,1},{8,9},{4,5},{12,13},{16,17},{24,25},{20,21},{28,29},{32,33},... | collective-permute-start | bytes 1179656 | tf_op jit(solution)/shard_map/ppermute | solution.py:28
  74.9 10.2 %collective-permute-start.18 = (f32[4,3,32,128]{3,2,1,0:T(8,128)S(1)}, f32[4,3,32,128]{3,2,1,0:T(8,128)S(1)}, u32[]{:S(2)}, u32[]{:S(2)}) collective-permute-start(f32[4,3,32,128]{3,2,1,0:T(8,128)S(1)} %slice.49), channel_id=1, source_target_pairs={{0,3},{8,11},{4,7},{12,15},{16,19},{24,27},{20,23},{28,31},{32,35}... | collective-permute-start | bytes 589832 | tf_op jit(solution)/shard_map/ppermute | solution.py:28
  76.3 7.8 %collective-permute-start.17 = (f32[4,3,32,128]{3,2,1,0:T(8,128)S(1)}, f32[4,3,32,128]{3,2,1,0:T(8,128)S(1)}, u32[]{:S(2)}, u32[]{:S(2)}) collective-permute-start(f32[4,3,32,128]{3,2,1,0:T(8,128)S(1)} %slice.48), channel_id=1, source_target_pairs={{0,1},{8,9},{4,5},{12,13},{16,17},{24,25},{20,21},{28,29},{32,33},... | collective-permute-start | bytes 589832 | tf_op jit(solution)/shard_map/ppermute | solution.py:28
  78.8 14.4 %collective-permute-start.20 = (f32[256,512]{1,0:T(8,128)S(1)}, f32[256,512]{1,0:T(8,128)S(1)}, u32[]{:S(2)}, u32[]{:S(2)}) collective-permute-start(f32[256,512]{1,0:T(8,128)S(1)} %slice_bitcast_fusion), channel_id=1, source_target_pairs={{0,3},{8,11},{4,7},{12,15},{16,19},{24,27},{20,23},{28,31},{32,35}... | collective-permute-start | bytes 1572872 | tf_op jit(solution)/shard_map/ppermute | solution.py:28
  78.9 14.3 %collective-permute-start.19 = (f32[256,512]{1,0:T(8,128)S(1)}, f32[256,512]{1,0:T(8,128)S(1)}, u32[]{:S(2)}, u32[]{:S(2)}) collective-permute-start(f32[256,512]{1,0:T(8,128)S(1)} %slice_bitcast_fusion.1), channel_id=1, source_target_pairs={{0,1},{8,9},{4,5},{12,13},{16,17},{24,25},{20,21},{28,29},{32,33},... | collective-permute-start | bytes 1572872 | tf_op jit(solution)/shard_map/ppermute | solution.py:28
  104.3 62.7 %collective-permute-start.27 = (f32[4,2,256,512]{3,2,1,0:T(8,128)}, f32[4,2,256,512]{3,2,1,0:T(8,128)}, u32[]{:S(2)}, u32[]{:S(2)}) collective-permute-start(f32[4,2,256,512]{3,2,1,0:T(8,128)} %pad_maximum_fusion.refs_2_), channel_id=1, source_target_pairs={{0,8},{8,0},{4,12},{12,4},{16,24},{24,16},{20,28},{28,20},{32,40},... | collective-permute-start | bytes 12582920 | tf_op jit(solution)/shard_map/ppermute | solution.py:28
  104.4 62.6 %all-to-all-start.1 = ((f32[32,80,128]{2,1,0:T(8,128)}), f32[32,80,128]{2,1,0:T(8,128)S(1)}, u32[]{:S(2)}, u32[]{:S(2)}) async-start(f32[32,80,128]{2,1,0:T(8,128)} %param.3), calls=%async_computation.1 | async-start | bytes 2621440 | tf_op jit(solution)/shard_map/all_to_all | solution.py:89
  111.5 53.0 %collective-permute-start.22 = (f32[32,4,32,128]{3,2,1,0:T(8,128)}, f32[32,4,32,128]{3,2,1,0:T(8,128)S(1)}, u32[]{:S(2)}, u32[]{:S(2)}) collective-permute-start(f32[32,4,32,128]{3,2,1,0:T(8,128)} %copy-done.8), channel_id=1, source_target_pairs={{0,3},{8,11},{4,7},{12,15},{16,19},{24,27},{20,23},{28,31},{32,35}... | collective-permute-start | bytes 6291464 | tf_op jit(solution)/shard_map/ppermute | solution.py:28
  111.8 55.1 %collective-permute-start.21 = (f32[32,4,32,128]{3,2,1,0:T(8,128)}, f32[32,4,32,128]{3,2,1,0:T(8,128)}, u32[]{:S(2)}, u32[]{:S(2)}) collective-permute-start(f32[32,4,32,128]{3,2,1,0:T(8,128)} %copy-done.8), channel_id=1, source_target_pairs={{0,1},{8,9},{4,5},{12,13},{16,17},{24,25},{20,21},{28,29},{32,33},... | collective-permute-start | bytes 6291464 | tf_op jit(solution)/shard_map/ppermute | solution.py:28
  114.8 47.3 %collective-permute-start.24 = (f32[32,3,32,128]{3,2,1,0:T(8,128)}, f32[32,3,32,128]{3,2,1,0:T(8,128)S(1)}, u32[]{:S(2)}, u32[]{:S(2)}) collective-permute-start(f32[32,3,32,128]{3,2,1,0:T(8,128)} %copy-done.9), channel_id=1, source_target_pairs={{0,192},{8,200},{4,196},{12,204},{16,208},{24,216},{20,212},{28,22... | collective-permute-start | bytes 4718600 | tf_op jit(solution)/shard_map/ppermute | solution.py:28
  117.9 46.6 %collective-permute-start.23 = (f32[32,3,32,128]{3,2,1,0:T(8,128)}, f32[32,3,32,128]{3,2,1,0:T(8,128)S(1)}, u32[]{:S(2)}, u32[]{:S(2)}) collective-permute-start(f32[32,3,32,128]{3,2,1,0:T(8,128)} %copy-done.9), channel_id=1, source_target_pairs={{0,64},{8,72},{4,68},{12,76},{16,80},{24,88},{20,84},{28,92},{32,9... | collective-permute-start | bytes 4718600 | tf_op jit(solution)/shard_map/ppermute | solution.py:28
  168.7 18.5 %collective-permute-start.31 = (f32[16,3,32,128]{3,2,1,0:T(8,128)S(1)}, f32[16,3,32,128]{3,2,1,0:T(8,128)}, u32[]{:S(2)}, u32[]{:S(2)}) collective-permute-start(f32[16,3,32,128]{3,2,1,0:T(8,128)S(1)} %slice.55), channel_id=1, source_target_pairs={{0,192},{8,200},{4,196},{12,204},{16,208},{24,216},{20,212},{28,22... | collective-permute-start | bytes 2359304 | tf_op jit(solution)/shard_map/ppermute | solution.py:28
  171.7 19.8 %collective-permute-start.30 = (f32[16,3,32,128]{3,2,1,0:T(8,128)S(1)}, f32[16,3,32,128]{3,2,1,0:T(8,128)}, u32[]{:S(2)}, u32[]{:S(2)}) collective-permute-start(f32[16,3,32,128]{3,2,1,0:T(8,128)S(1)} %slice.54), channel_id=1, source_target_pairs={{0,64},{8,72},{4,68},{12,76},{16,80},{24,88},{20,84},{28,92},{32,9... | collective-permute-start | bytes 2359304 | tf_op jit(solution)/shard_map/ppermute | solution.py:28
  172.4 24.9 %collective-permute-start.29 = (f32[16,4,32,128]{3,2,1,0:T(8,128)S(1)}, f32[16,4,32,128]{3,2,1,0:T(8,128)S(1)}, u32[]{:S(2)}, u32[]{:S(2)}) collective-permute-start(f32[16,4,32,128]{3,2,1,0:T(8,128)S(1)} %slice.53), channel_id=1, source_target_pairs={{0,3},{8,11},{4,7},{12,15},{16,19},{24,27},{20,23},{28,31},{32,35}... | collective-permute-start | bytes 3145736 | tf_op jit(solution)/shard_map/ppermute | solution.py:28
  172.5 47.5 %collective-permute-start.32 = (f32[32,4,32,128]{3,2,1,0:T(8,128)}, f32[32,4,32,128]{3,2,1,0:T(8,128)S(1)}, u32[]{:S(2)}, u32[]{:S(2)}) collective-permute-start(f32[32,4,32,128]{3,2,1,0:T(8,128)} %collective-permute-done.21), channel_id=1, source_target_pairs={{0,8},{8,0},{4,12},{12,4},{16,24},{24,16},{20,28},{28,20},{32,40},... | collective-permute-start | bytes 6291464 | tf_op jit(solution)/shard_map/ppermute | solution.py:28
  172.6 47.5 %collective-permute-start.33 = (f32[32,4,32,128]{3,2,1,0:T(8,128)S(1)}, f32[32,4,32,128]{3,2,1,0:T(8,128)S(1)}, u32[]{:S(2)}, u32[]{:S(2)}) collective-permute-start(f32[32,4,32,128]{3,2,1,0:T(8,128)S(1)} %copy-done.3), channel_id=1, source_target_pairs={{0,8},{8,0},{4,12},{12,4},{16,24},{24,16},{20,28},{28,20},{32,40},... | collective-permute-start | bytes 6291464 | tf_op jit(solution)/shard_map/ppermute | solution.py:28
  187.2 32.8 %collective-permute-start.34 = (f32[32,3,32,128]{3,2,1,0:T(8,128)S(1)}, f32[32,3,32,128]{3,2,1,0:T(8,128)S(1)}, u32[]{:S(2)}, u32[]{:S(2)}) collective-permute-start(f32[32,3,32,128]{3,2,1,0:T(8,128)S(1)} %copy-done.7), channel_id=1, source_target_pairs={{0,8},{8,0},{4,12},{12,4},{16,24},{24,16},{20,28},{28,20},{32,40},... | collective-permute-start | bytes 4718600 | tf_op jit(solution)/shard_map/ppermute | solution.py:28
  191.6 28.5 %collective-permute-start.35 = (f32[32,3,32,128]{3,2,1,0:T(8,128)S(1)}, f32[32,3,32,128]{3,2,1,0:T(8,128)S(1)}, u32[]{:S(2)}, u32[]{:S(2)}) collective-permute-start(f32[32,3,32,128]{3,2,1,0:T(8,128)S(1)} %copy-done.5), channel_id=1, source_target_pairs={{0,8},{8,0},{4,12},{12,4},{16,24},{24,16},{20,28},{28,20},{32,40},... | collective-permute-start | bytes 4718600 | tf_op jit(solution)/shard_map/ppermute | solution.py:28
  197.3 22.7 %collective-permute-start.28 = (f32[16,4,32,128]{3,2,1,0:T(8,128)S(1)}, f32[16,4,32,128]{3,2,1,0:T(8,128)S(1)}, u32[]{:S(2)}, u32[]{:S(2)}) collective-permute-start(f32[16,4,32,128]{3,2,1,0:T(8,128)S(1)} %slice.52), channel_id=1, source_target_pairs={{0,1},{8,9},{4,5},{12,13},{16,17},{24,25},{20,21},{28,29},{32,33},... | collective-permute-start | bytes 3145736 | tf_op jit(solution)/shard_map/ppermute | solution.py:28
  (26 other events, 146.9 us)
where the time goes:
time: 284 us; the launch traced here: 281 us
  waiting for transfers between devices  151 us (53%)
  starting transfers between devices  58.2 us (20%)
  Pallas kernels  28.4 us (10%)
  blocking collectives  23.8 us (8%)
  local copies, waits for them, and re-layouts  14.4 us (5%)
  other arithmetic  4.74 us (2%)
    ppermute x39, waiting for transfers between devices, shift(): return lax.ppermute(value, ALL, pairs)  141 us
    ppermute x39, starting transfers between devices, shift(): return lax.ppermute(value, ALL, pairs)  38.7 us
    pallas_call x1, Pallas kernels, solve(): pl.pallas_call(kernel, out_shape=jax.ShapeDtypeStruct((PANELS, ROWS, PANE...  28.4 us
    all_to_all x1, blocking collectives, local(): result = lax.all_to_all(solved, 'aux', 0, 0, tiled=True)  23.8 us
    all_to_all x1, starting transfers between devices, spread(): lax.all_to_all(halves, ALL, 0, 0, axis_index_groups=groups, tiled=True)  12.3 us
    all_to_all x1, waiting for transfers between devices, spread(): lax.all_to_all(halves, ALL, 0, 0, axis_index_groups=groups, tiled=True)  9.89 us
    unnamed x52, local copies, waits for them, and re-layouts  9.77 us
    all_to_all x1, starting transfers between devices, gather(): rows = lax.all_to_all(integrals, 'pair', 0, 0, tiled=True)  7.11 us
  transfers between devices with their start and end apart: 42, of which 23 were waited for; matrix products, arithmetic and copies ran while one was open for 2% of the time, Pallas kernels for 0%

commit v1 on v0

--- a/solution.py
+++ b/solution.py
@@ -36,7 +36,7 @@
     near = [shift(piece, dz=d) for d in (1, -1, 2, -2)]
     one, minus_one, two, minus_two = lax.optimization_barrier(near)
     three, minus_three = shift(two, dz=1), shift(minus_two, dz=-1)
-    four = jnp.concatenate([shift(two[:EARLY], dz=2), shift(minus_two[EARLY:], dz=-2)])
+    four = shift(two, dz=2)
     return jnp.stack([piece, one, two, three, four, minus_three, minus_two, minus_one])
 
 
@@ -57,47 +57,38 @@
     return jnp.stack(held)
 
 
-def start(factor, diag_inverse, pair):
-    half = lax.dynamic_slice(diag_inverse[0], (256 * (pair % 2), 0), (256, PANEL))
-    neighbour = lax.ppermute(half, "aux", [(a, (a + 4) % 8) for a in range(8)])
-    both = spread(factor, pair)
-    both, neighbour = lax.optimization_barrier((both, neighbour))
-    own = jnp.stack([half, neighbour])
-    up, down = shift(own, dy=1), shift(own, dy=-1)
-    column = ring_of_eight(share(both, pair // 4))
-    column, up, down = lax.optimization_barrier((column, up, down))
-    return column, [own, up, down]
-
-
 def swap(values):
     return [shift(value, core=1) for value in values]
 
 
-def gather(column, diagonals, integrals):
+def gather(column, half, integrals):
     blocks = [column[:, :EARLY], column[:, EARLY:]]
-    first = [along("dx"), along("dy")]
-    second = [along("dy"), along("dx")]
+    first = [along("dy"), along("dx")]
+    second = [along("dx"), along("dy")]
     near = [(one(block, 1), one(block, -1)) for one, block in zip(first, blocks)]
-    near, diagonals = lax.optimization_barrier((near, diagonals))
+    neighbour = lax.ppermute(half, "aux", [(a, (a + 4) % 8) for a in range(8)])
+    near = lax.optimization_barrier(near)
     far = [(one(up[:4], 1), one(down[4:], -1)) for one, (up, down) in zip(first, near)]
-    ends = jnp.stack([shift(diagonals[1][0], dy=1), shift(diagonals[2][1], dy=-1)])
     whole = [jnp.concatenate([block, up, down, *ends]) for block, (up, down), ends in zip(blocks, near, far)]
-    whole, ends, integrals = lax.optimization_barrier((whole, ends, integrals))
+    inverses = jnp.stack([half, neighbour])
+    whole, inverses, integrals = lax.optimization_barrier((whole, inverses, integrals))
     near = [(two(block, 1), two(block, -1)) for two, block in zip(second, whole)]
-    swapped = swap(whole)
-    swapped, diagonals, ends = lax.optimization_barrier((swapped, diagonals, ends))
+    sides = shift(inverses, dy=1), shift(inverses, dy=-1)
+    swapped = swap([*whole, inverses])
     rows = lax.all_to_all(integrals, "pair", 0, 0, tiled=True)
-    diagonals = jnp.stack([*diagonals, ends])
-    swapped += swap([diagonals])
-    near, swapped, rows = lax.optimization_barrier((near, swapped, rows))
+    near, swapped, rows, sides = lax.optimization_barrier((near, swapped, rows, sides))
     far = [(two(up[:16], 1), two(down[16:], -1)) for two, (up, down) in zip(second, near)]
-    swapped_near = [swap(values) for values in near]
-    far, swapped_near = lax.optimization_barrier((far, swapped_near))
+    ends = shift(sides[0][0], dy=1), shift(sides[1][1], dy=-1)
+    sides = jnp.stack(sides)
+    swapped_near = [swap(values) for values in [*near, [sides]]]
+    far, swapped_near, ends = lax.optimization_barrier((far, swapped_near, ends))
+    ends = jnp.stack(ends)
     gathered = []
     for color in range(2):
         gathered += [whole[color], *near[color], *far[color]]
         gathered += [swapped[color], *swapped_near[color], *swap(far[color])]
-    return rows, (diagonals, swapped[2]), gathered
+    diagonals = [inverses, sides, ends, swapped[2], *swapped_near[2], *swap([ends])]
+    return rows, diagonals, gathered
 
 
 LAYOUT = ((0, 0, 4), (1, 0, 4), (2, 0, 4), (3, 0, 2), (3, 2, 2))
@@ -110,21 +101,24 @@
 
 def kernel(*refs):
     place_ref, x_ref = refs[:2]
-    diagonals, arrays = refs[2:4], refs[4:24]
-    out_ref, held, inverses, remain, parts, inverse_sem, early_sem, late_sem = refs[24:]
+    diagonals, arrays = refs[2:8], refs[8:28]
+    out_ref, held, inverses, remain, parts, inverse_sem, early_sem, late_sem = refs[28:]
     x, y, z, core = (place_ref[i] for i in range(4))
 
     for other in range(2):
-        pltpu.make_async_copy(diagonals[other], inverses.at[other], inverse_sem).start()
+        own, sides, ends = diagonals[3 * other : 3 * other + 3]
+        pltpu.make_async_copy(own, inverses.at[other, 0], inverse_sem).start()
+        pltpu.make_async_copy(sides, inverses.at[other, pl.ds(1, 2)], inverse_sem).start()
+        pltpu.make_async_copy(ends, inverses.at[other, 3], inverse_sem).start()
     for other in range(2):
         for number, (second, block, count) in enumerate(LAYOUT):
             ref = arrays[5 * other + number]
-            to = held.at[other, second, pl.ds(block, count), :, pl.ds(0, EARLY)]
+            to = held.at[other, pl.ds(block, count), second, :, pl.ds(0, EARLY)]
             pltpu.make_async_copy(ref, to, early_sem).start()
     for other in range(2):
         for number, (second, block, count) in enumerate(LAYOUT):
             ref = arrays[10 + 5 * other + number]
-            to = held.at[other, pl.ds(block, count), second, :, pl.ds(EARLY, LATE)]
+            to = held.at[other, second, pl.ds(block, count), :, pl.ds(EARLY, LATE)]
             pltpu.make_async_copy(ref, to, late_sem).start()
     y_positions = [position(sy - y) for sy in range(NY)]
 
@@ -224,8 +218,10 @@
     x, z, core = pair // 8, (pair // 2) % 4 * 2 + aux // NY, pair % 2
     place = jnp.stack([x, aux % NY, z, core]).astype(jnp.int32)
 
-    column, diagonals = start(factor, diag_inverse, pair)
-    rows, diagonals, gathered = gather(column, diagonals, integrals)
+    column = ring_of_eight(share(spread(factor, pair), pair // 4))
+    half = lax.dynamic_slice(diag_inverse[0], (256 * core, 0), (256, PANEL))
+    column, half = lax.optimization_barrier((column, half))
+    rows, diagonals, gathered = gather(column, half, integrals)
     solved = solve(place, rows, diagonals, gathered)
     result = lax.all_to_all(solved, "aux", 0, 0, tiled=True)
     return result.reshape(1, 8 * ROWS, PANEL)

time: 284 us -> 274 us (0.965)
  waiting for transfers between devices: 151 us -> 132 us
  blocking collectives: 23.8 us -> 31.1 us
  starting transfers between devices: 58.2 us -> 61.2 us
    ppermute x39 -> x40, waiting for transfers between devices: 141 us -> 122 us  [shift(): return lax.ppermute(value, ALL, pairs)]
    all_to_all x1, blocking collectives: 23.8 us -> 31.1 us  [local(): result = lax.all_to_all(solved, 'aux', 0, 0, tiled=True)]
    ppermute x39 -> x40, starting transfers between devices: 38.7 us -> 40.6 us  [shift(): return lax.ppermute(value, ALL, pairs)]
    unnamed x52 -> x37, local copies, waits for them, and re-layouts: 9.77 us -> 8.12 us
  transfers between devices with their start and end apart: 42 -> 43, of which waited for: 23 -> 22; matrix products, arithmetic and copies ran while one was open for 2% -> 4% of each run, Pallas kernels for 0% -> 0%
where the time goes in v1:
time: 274 us; the launch traced here: 272 us
  waiting for transfers between devices  132 us (48%)
  starting transfers between devices  61.2 us (22%)
  blocking collectives  31.1 us (11%)
  Pallas kernels  28.5 us (10%)
  local copies, waits for them, and re-layouts  15.2 us (6%)
  other arithmetic  3.48 us (1%)
    ppermute x40, waiting for transfers between devices, shift(): return lax.ppermute(value, ALL, pairs)  122 us
    ppermute x40, starting transfers between devices, shift(): return lax.ppermute(value, ALL, pairs)  40.6 us
    all_to_all x1, blocking collectives, local(): result = lax.all_to_all(solved, 'aux', 0, 0, tiled=True)  31.1 us
    pallas_call x1, Pallas kernels, solve(): pl.pallas_call(kernel, out_shape=jax.ShapeDtypeStruct((PANELS, ROWS, PANE...  28.5 us
    all_to_all x1, starting transfers between devices, spread(): lax.all_to_all(halves, ALL, 0, 0, axis_index_groups=groups, tiled=True)  11.6 us
    all_to_all x1, waiting for transfers between devices, spread(): lax.all_to_all(halves, ALL, 0, 0, axis_index_groups=groups, tiled=True)  10.2 us
    unnamed x37, local copies, waits for them, and re-layouts  8.12 us
    all_to_all x1, starting transfers between devices, gather(): rows = lax.all_to_all(integrals, 'pair', 0, 0, tiled=True)  7.06 us
  transfers between devices with their start and end apart: 43, of which 22 were waited for; matrix products, arithmetic and copies ran while one was open for 4% of the time, Pallas kernels for 0%

profile of v1, /device:TPU:56, one launch (start us, length us, event | category | flops | bytes accessed | tf_op | source)
XLA Modules:
  0.0 271.5 jit_solution(13799329634156562910)
XLA Ops:
  0.0 1.9 reverse_select_fusion
  1.9 11.6 %all-to-all-start = ((f32[16,32,128]{2,1,0:T(8,128)}), f32[16,32,128]{2,1,0:T(8,128)S(1)}, u32[]{:S(2)}, u32[]{:S(2)}) async-start(f32[16,32,128]{2,1,0:T(8,128)} %bitcast.5), calls=%async_computation | async-start | bytes 524288 | tf_op jit(solution)/shard_map/all_to_all | solution.py:47
  13.5 10.2 %all-to-all-done = f32[16,32,128]{2,1,0:T(8,128)S(1)} async-done(((f32[16,32,128]{2,1,0:T(8,128)}), f32[16,32,128]{2,1,0:T(8,128)S(1)}, u32[]{:S(2)}, u32[]{:S(2)}) %all-to-all-start) | async-done | bytes 262176 | tf_op jit(solution)/shard_map/all_to_all | solution.py:47
  24.1 2.7 %collective-permute-start.2 = (f32[7,32,128]{2,1,0:T(8,128)S(1)}, f32[7,32,128]{2,1,0:T(8,128)S(1)}, u32[]{:S(2)}, u32[]{:S(2)}) collective-permute-start(f32[7,32,128]{2,1,0:T(8,128)S(1)} %constant_dynamic-update-slice_fusion), channel_id=1, source_target_pairs={{0,16},{8,24},{4,20},{12,28},{16,32},{24,40},{20,36},{28,44},{32,4... | collective-permute-start | bytes 344072 | tf_op jit(solution)/shard_map/ppermute | solution.py:28
  26.8 2.0 collective-permute-start
  28.8 3.0 %collective-permute-done.3 = f32[7,32,128]{2,1,0:T(8,128)S(1)} collective-permute-done((f32[7,32,128]{2,1,0:T(8,128)S(1)}, f32[7,32,128]{2,1,0:T(8,128)S(1)}, u32[]{:S(2)}, u32[]{:S(2)}) %collective-permute-start.3) | collective-permute-done | bytes 114720 | tf_op jit(solution)/shard_map/ppermute | solution.py:28
  31.8 2.1 collective-permute-done.2
  35.2 2.7 collective-permute-start.5
  37.9 3.7 %collective-permute-start.4 = (f32[7,32,128]{2,1,0:T(8,128)S(1)}, f32[7,32,128]{2,1,0:T(8,128)S(1)}, u32[]{:S(2)}, u32[]{:S(2)}) collective-permute-start(f32[7,32,128]{2,1,0:T(8,128)S(1)} %collective-permute-done.2), channel_id=1, source_target_pairs={{0,4},{8,12},{4,16},{12,24},{16,20},{24,28},{20,32},{28,40},{32,36... | collective-permute-start | bytes 344072 | tf_op jit(solution)/shard_map/ppermute | solution.py:28
  41.6 4.9 %collective-permute-done.4 = f32[7,32,128]{2,1,0:T(8,128)S(1)} collective-permute-done((f32[7,32,128]{2,1,0:T(8,128)S(1)}, f32[7,32,128]{2,1,0:T(8,128)S(1)}, u32[]{:S(2)}, u32[]{:S(2)}) %collective-permute-start.4) | collective-permute-done | bytes 114720 | tf_op jit(solution)/shard_map/ppermute | solution.py:28
  47.9 2.3 collective-permute-start.7
  51.2 1.9 collective-permute-start.9
  53.1 1.9 collective-permute-start.15
  55.0 5.6 %collective-permute-done.10 = f32[8,3,32,128]{3,2,1,0:T(8,128)S(1)} collective-permute-done((f32[8,3,32,128]{3,2,1,0:T(8,128)S(1)}, f32[8,3,32,128]{3,2,1,0:T(8,128)S(1)}, u32[]{:S(2)}, u32[]{:S(2)}) %collective-permute-start.10) | collective-permute-done | bytes 393248 | tf_op jit(solution)/shard_map/ppermute | solution.py:28
  62.5 1.7 collective-permute-start.13
  64.3 3.1 %collective-permute-start.11 = (f32[4,4,32,128]{3,2,1,0:T(8,128)S(1)}, f32[4,4,32,128]{3,2,1,0:T(8,128)S(1)}, u32[]{:S(2)}, u32[]{:S(2)}) collective-permute-start(f32[4,4,32,128]{3,2,1,0:T(8,128)S(1)} %slice.38), channel_id=1, source_target_pairs={{0,1},{8,9},{4,5},{12,13},{16,17},{24,25},{20,21},{28,29},{32,33},... | collective-permute-start | bytes 786440 | tf_op jit(solution)/shard_map/ppermute | solution.py:28
  73.1 3.3 %collective-permute-start.23 = (f32[2,256,512]{2,1,0:T(8,128)S(1)}, f32[2,256,512]{2,1,0:T(8,128)}, u32[]{:S(2)}, u32[]{:S(2)}) collective-permute-start(f32[2,256,512]{2,1,0:T(8,128)S(1)} %pad_maximum_fusion.1.refs_2_), channel_id=1, source_target_pairs={{0,1},{8,9},{4,5},{12,13},{16,17},{24,25},{20,21},{28,29},{32,33},... | collective-permute-start | bytes 3145736 | tf_op jit(solution)/shard_map/ppermute | solution.py:28
  76.4 7.1 %all-to-all-start.1 = ((f32[32,80,128]{2,1,0:T(8,128)}), f32[32,80,128]{2,1,0:T(8,128)}, u32[]{:S(2)}, u32[]{:S(2)}) async-start(f32[32,80,128]{2,1,0:T(8,128)} %param.3), calls=%async_computation.1 | async-start | bytes 2621440 | tf_op jit(solution)/shard_map/all_to_all | solution.py:78
  83.8 15.2 %collective-permute-done.24 = f32[2,256,512]{2,1,0:T(8,128)S(1)} collective-permute-done((f32[2,256,512]{2,1,0:T(8,128)S(1)}, f32[2,256,512]{2,1,0:T(8,128)S(1)}, u32[]{:S(2)}, u32[]{:S(2)}) %collective-permute-start.24) | collective-permute-done | bytes 1048608 | tf_op jit(solution)/shard_map/ppermute | solution.py:28
  101.1 3.2 %collective-permute-start.18 = (f32[32,3,32,128]{3,2,1,0:T(8,128)}, f32[32,3,32,128]{3,2,1,0:T(8,128)}, u32[]{:S(2)}, u32[]{:S(2)}) collective-permute-start(f32[32,3,32,128]{3,2,1,0:T(8,128)} %constant_dynamic-update-slice_fusion.12), channel_id=1, source_target_pairs={{0,1},{8,9},{4,5},{12,13},{16,17},{24,25},{20,21},{28,29},{32,33},... | collective-permute-start | bytes 4718600 | tf_op jit(solution)/shard_map/ppermute | solution.py:28
  104.3 34.0 %collective-permute-done.19 = f32[32,3,32,128]{3,2,1,0:T(8,128)} collective-permute-done((f32[32,3,32,128]{3,2,1,0:T(8,128)}, f32[32,3,32,128]{3,2,1,0:T(8,128)}, u32[]{:S(2)}, u32[]{:S(2)}) %collective-permute-start.19) | collective-permute-done | bytes 1572896 | tf_op jit(solution)/shard_map/ppermute | solution.py:28
  138.3 12.1 %collective-permute-done.17 = f32[32,4,32,128]{3,2,1,0:T(8,128)} collective-permute-done((f32[32,4,32,128]{3,2,1,0:T(8,128)}, f32[32,4,32,128]{3,2,1,0:T(8,128)}, u32[]{:S(2)}, u32[]{:S(2)}) %collective-permute-start.17) | collective-permute-done | bytes 2097184 | tf_op jit(solution)/shard_map/ppermute | solution.py:28
  154.7 2.6 collective-permute-start.27
  158.4 2.1 collective-permute-start.34
  164.4 3.1 %collective-permute-done.35 = f32[256,512]{1,0:T(8,128)S(1)} collective-permute-done((f32[256,512]{1,0:T(8,128)S(1)}, f32[256,512]{1,0:T(8,128)S(1)}, u32[]{:S(2)}, u32[]{:S(2)}) %collective-permute-start.35) | collective-permute-done | bytes 524320 | tf_op jit(solution)/shard_map/ppermute | solution.py:28
  169.0 15.6 %collective-permute-done.34 = f32[256,512]{1,0:T(8,128)S(1)} collective-permute-done((f32[256,512]{1,0:T(8,128)S(1)}, f32[256,512]{1,0:T(8,128)S(1)}, u32[]{:S(2)}, u32[]{:S(2)}) %collective-permute-start.34) | collective-permute-done | bytes 524320 | tf_op jit(solution)/shard_map/ppermute | solution.py:28
  186.6 4.2 %collective-permute-done.25 = f32[16,4,32,128]{3,2,1,0:T(8,128)} collective-permute-done((f32[16,4,32,128]{3,2,1,0:T(8,128)S(1)}, f32[16,4,32,128]{3,2,1,0:T(8,128)}, u32[]{:S(2)}, u32[]{:S(2)}) %collective-permute-start.25) | collective-permute-done | bytes 1048608 | tf_op jit(solution)/shard_map/ppermute | solution.py:28
  190.9 6.3 %collective-permute-done.31 = f32[32,3,32,128]{3,2,1,0:T(8,128)S(1)} collective-permute-done((f32[32,3,32,128]{3,2,1,0:T(8,128)}, f32[32,3,32,128]{3,2,1,0:T(8,128)S(1)}, u32[]{:S(2)}, u32[]{:S(2)}) %collective-permute-start.31) | collective-permute-done | bytes 1572896 | tf_op jit(solution)/shard_map/ppermute | solution.py:28
  197.2 2.2 collective-permute-done.32
  204.0 5.7 %collective-permute-done.39 = f32[16,3,32,128]{3,2,1,0:T(8,128)} collective-permute-done((f32[16,3,32,128]{3,2,1,0:T(8,128)}, f32[16,3,32,128]{3,2,1,0:T(8,128)}, u32[]{:S(2)}, u32[]{:S(2)}) %collective-permute-start.39) | collective-permute-done | bytes 786464 | tf_op jit(solution)/shard_map/ppermute | solution.py:28
  210.9 28.5 %shard_map.37 = f32[8,80,512]{2,1,0:T(8,128)} custom-call(s32[4]{0:T(128)S(1)} %pad_add_fusion.refs_0_, f32[32,80,128]{2,1,0:T(8,128)} %all-to-all-done.1.refs_1_, f32[2,256,512]{2,1,0:T(8,128)S(1)} %pad_maximum_fusion.1.refs_2_, f32[2,2,256,512]{3,2,1,0:T(8,128)} %copy-done.1, f32[2,256,512]{2,1,0:T(8,128)S(1)} %pad_maximum_fusion.2.refs_4_, ...), custom_call_target="tpu_custom_call" | custom-call | flops 16000000000 | bytes 40000000 | tf_op jit(solution)/shard_map/pallas_call | solution.py:196
  239.4 31.1 %all_to_all.15 = f32[8,80,512]{2,1,0:T(8,128)S(1)} all-to-all(f32[8,80,512]{2,1,0:T(8,128)} %shard_map.37), channel_id=1, replica_groups=mesh['pair'=32,'aux'=8] {'aux'}, dimensions={0} | all-to-all | bytes 2621440 | tf_op jit(solution)/shard_map/all_to_all | solution.py:226
  (114 shorter events, 33.4 us)
Async XLA Ops:
  1.9 21.8 %all-to-all-start = ((f32[16,32,128]{2,1,0:T(8,128)}), f32[16,32,128]{2,1,0:T(8,128)S(1)}, u32[]{:S(2)}, u32[]{:S(2)}) async-start(f32[16,32,128]{2,1,0:T(8,128)} %bitcast.5), calls=%async_computation | async-start | bytes 524288 | tf_op jit(solution)/shard_map/all_to_all | solution.py:47
  24.1 9.9 %collective-permute-start.2 = (f32[7,32,128]{2,1,0:T(8,128)S(1)}, f32[7,32,128]{2,1,0:T(8,128)S(1)}, u32[]{:S(2)}, u32[]{:S(2)}) collective-permute-start(f32[7,32,128]{2,1,0:T(8,128)S(1)} %constant_dynamic-update-slice_fusion), channel_id=1, source_target_pairs={{0,16},{8,24},{4,20},{12,28},{16,32},{24,40},{20,36},{28,44},{32,4... | collective-permute-start | bytes 344072 | tf_op jit(solution)/shard_map/ppermute | solution.py:28
  26.8 8.4 %collective-permute-start = (f32[7,32,128]{2,1,0:T(8,128)S(1)}, f32[7,32,128]{2,1,0:T(8,128)S(1)}, u32[]{:S(2)}, u32[]{:S(2)}) collective-permute-start(f32[7,32,128]{2,1,0:T(8,128)S(1)} %constant_dynamic-update-slice_fusion), channel_id=1, source_target_pairs={{0,4},{8,12},{4,16},{12,24},{16,20},{24,28},{20,32},{28,40},{32,36... | collective-permute-start | bytes 344072 | tf_op jit(solution)/shard_map/ppermute | solution.py:28
  35.2 11.3 %collective-permute-start.5 = (f32[7,32,128]{2,1,0:T(8,128)S(1)}, f32[7,32,128]{2,1,0:T(8,128)S(1)}, u32[]{:S(2)}, u32[]{:S(2)}) collective-permute-start(f32[7,32,128]{2,1,0:T(8,128)S(1)} %collective-permute-done.2), channel_id=1, source_target_pairs={{0,16},{8,24},{4,20},{12,28},{16,32},{24,40},{20,36},{28,44},{32,4... | collective-permute-start | bytes 344072 | tf_op jit(solution)/shard_map/ppermute | solution.py:28
  37.9 8.6 %collective-permute-start.4 = (f32[7,32,128]{2,1,0:T(8,128)S(1)}, f32[7,32,128]{2,1,0:T(8,128)S(1)}, u32[]{:S(2)}, u32[]{:S(2)}) collective-permute-start(f32[7,32,128]{2,1,0:T(8,128)S(1)} %collective-permute-done.2), channel_id=1, source_target_pairs={{0,4},{8,12},{4,16},{12,24},{16,20},{24,28},{20,32},{28,40},{32,36... | collective-permute-start | bytes 344072 | tf_op jit(solution)/shard_map/ppermute | solution.py:28
  46.8 15.2 %collective-permute-start.8 = (f32[8,4,32,128]{3,2,1,0:T(8,128)S(1)}, f32[8,4,32,128]{3,2,1,0:T(8,128)S(1)}, u32[]{:S(2)}, u32[]{:S(2)}) collective-permute-start(f32[8,4,32,128]{3,2,1,0:T(8,128)S(1)} %get-tuple-element.77), channel_id=1, source_target_pairs={{0,3},{8,11},{4,7},{12,15},{16,19},{24,27},{20,23},{28,31},{32,35}... | collective-permute-start | bytes 1572872 | tf_op jit(solution)/shard_map/ppermute | solution.py:28
  47.9 14.1 %collective-permute-start.7 = (f32[8,4,32,128]{3,2,1,0:T(8,128)S(1)}, f32[8,4,32,128]{3,2,1,0:T(8,128)S(1)}, u32[]{:S(2)}, u32[]{:S(2)}) collective-permute-start(f32[8,4,32,128]{3,2,1,0:T(8,128)S(1)} %get-tuple-element.77), channel_id=1, source_target_pairs={{0,1},{8,9},{4,5},{12,13},{16,17},{24,25},{20,21},{28,29},{32,33},... | collective-permute-start | bytes 1572872 | tf_op jit(solution)/shard_map/ppermute | solution.py:28
  51.1 9.5 %collective-permute-start.10 = (f32[8,3,32,128]{3,2,1,0:T(8,128)S(1)}, f32[8,3,32,128]{3,2,1,0:T(8,128)S(1)}, u32[]{:S(2)}, u32[]{:S(2)}) collective-permute-start(f32[8,3,32,128]{3,2,1,0:T(8,128)S(1)} %get-tuple-element.76), channel_id=1, source_target_pairs={{0,192},{8,200},{4,196},{12,204},{16,208},{24,216},{20,212},{28,22... | collective-permute-start | bytes 1179656 | tf_op jit(solution)/shard_map/ppermute | solution.py:28
  51.2 10.7 %collective-permute-start.9 = (f32[8,3,32,128]{3,2,1,0:T(8,128)S(1)}, f32[8,3,32,128]{3,2,1,0:T(8,128)S(1)}, u32[]{:S(2)}, u32[]{:S(2)}) collective-permute-start(f32[8,3,32,128]{3,2,1,0:T(8,128)S(1)} %get-tuple-element.76), channel_id=1, source_target_pairs={{0,64},{8,72},{4,68},{12,76},{16,80},{24,88},{20,84},{28,92},{32,9... | collective-permute-start | bytes 1179656 | tf_op jit(solution)/shard_map/ppermute | solution.py:28
  53.1 14.4 %collective-permute-start.15 = (f32[256,512]{1,0:T(8,128)S(1)}, f32[256,512]{1,0:T(8,128)S(1)}, u32[]{:S(2)}, u32[]{:S(2)}) collective-permute-start(f32[256,512]{1,0:T(8,128)S(1)} %dynamic-slice_bitcast_fusion), channel_id=1, source_target_pairs={{0,4},{1,5},{2,6},{3,7},{4,0},{5,1},{6,2},{7,3},{8,12},{9,13},{10,... | collective-permute-start | bytes 1572872 | tf_op jit(solution)/shard_map/ppermute | solution.py:69
  71.8 29.2 %collective-permute-start.21 = (f32[32,3,32,128]{3,2,1,0:T(8,128)}, f32[32,3,32,128]{3,2,1,0:T(8,128)}, u32[]{:S(2)}, u32[]{:S(2)}) collective-permute-start(f32[32,3,32,128]{3,2,1,0:T(8,128)} %constant_dynamic-update-slice_fusion.12), channel_id=1, source_target_pairs={{0,8},{8,0},{4,12},{12,4},{16,24},{24,16},{20,28},{28,20},{32,40},... | collective-permute-start | bytes 4718600 | tf_op jit(solution)/shard_map/ppermute | solution.py:28
  71.9 27.1 %collective-permute-start.24 = (f32[2,256,512]{2,1,0:T(8,128)S(1)}, f32[2,256,512]{2,1,0:T(8,128)S(1)}, u32[]{:S(2)}, u32[]{:S(2)}) collective-permute-start(f32[2,256,512]{2,1,0:T(8,128)S(1)} %pad_maximum_fusion.1.refs_2_), channel_id=1, source_target_pairs={{0,3},{8,11},{4,7},{12,15},{16,19},{24,27},{20,23},{28,31},{32,35}... | collective-permute-start | bytes 3145736 | tf_op jit(solution)/shard_map/ppermute | solution.py:28
  73.1 27.4 %collective-permute-start.23 = (f32[2,256,512]{2,1,0:T(8,128)S(1)}, f32[2,256,512]{2,1,0:T(8,128)}, u32[]{:S(2)}, u32[]{:S(2)}) collective-permute-start(f32[2,256,512]{2,1,0:T(8,128)S(1)} %pad_maximum_fusion.1.refs_2_), channel_id=1, source_target_pairs={{0,1},{8,9},{4,5},{12,13},{16,17},{24,25},{20,21},{28,29},{32,33},... | collective-permute-start | bytes 3145736 | tf_op jit(solution)/shard_map/ppermute | solution.py:28
  76.4 24.6 %collective-permute-start.22 = (f32[2,256,512]{2,1,0:T(8,128)S(1)}, f32[2,256,512]{2,1,0:T(8,128)}, u32[]{:S(2)}, u32[]{:S(2)}) collective-permute-start(f32[2,256,512]{2,1,0:T(8,128)S(1)} %pad_maximum_fusion.1.refs_2_), channel_id=1, source_target_pairs={{0,8},{8,0},{4,12},{12,4},{16,24},{24,16},{20,28},{28,20},{32,40},... | collective-permute-start | bytes 3145736 | tf_op jit(solution)/shard_map/ppermute | solution.py:28
  76.4 75.0 %all-to-all-start.1 = ((f32[32,80,128]{2,1,0:T(8,128)}), f32[32,80,128]{2,1,0:T(8,128)}, u32[]{:S(2)}, u32[]{:S(2)}) async-start(f32[32,80,128]{2,1,0:T(8,128)} %param.3), calls=%async_computation.1 | async-start | bytes 2621440 | tf_op jit(solution)/shard_map/all_to_all | solution.py:78
  83.5 54.8 %collective-permute-start.20 = (f32[32,4,32,128]{3,2,1,0:T(8,128)}, f32[32,4,32,128]{3,2,1,0:T(8,128)}, u32[]{:S(2)}, u32[]{:S(2)}) collective-permute-start(f32[32,4,32,128]{3,2,1,0:T(8,128)} %copy-done.2), channel_id=1, source_target_pairs={{0,8},{8,0},{4,12},{12,4},{16,24},{24,16},{20,28},{28,20},{32,40},... | collective-permute-start | bytes 6291464 | tf_op jit(solution)/shard_map/ppermute | solution.py:28
  99.0 51.4 %collective-permute-start.17 = (f32[32,4,32,128]{3,2,1,0:T(8,128)}, f32[32,4,32,128]{3,2,1,0:T(8,128)}, u32[]{:S(2)}, u32[]{:S(2)}) collective-permute-start(f32[32,4,32,128]{3,2,1,0:T(8,128)} %copy-done.2), channel_id=1, source_target_pairs={{0,192},{8,200},{4,196},{12,204},{16,208},{24,216},{20,212},{28,22... | collective-permute-start | bytes 6291464 | tf_op jit(solution)/shard_map/ppermute | solution.py:28
  100.5 50.9 %collective-permute-start.16 = (f32[32,4,32,128]{3,2,1,0:T(8,128)}, f32[32,4,32,128]{3,2,1,0:T(8,128)}, u32[]{:S(2)}, u32[]{:S(2)}) collective-permute-start(f32[32,4,32,128]{3,2,1,0:T(8,128)} %copy-done.2), channel_id=1, source_target_pairs={{0,64},{8,72},{4,68},{12,76},{16,80},{24,88},{20,84},{28,92},{32,9... | collective-permute-start | bytes 6291464 | tf_op jit(solution)/shard_map/ppermute | solution.py:28
  101.0 37.2 %collective-permute-start.19 = (f32[32,3,32,128]{3,2,1,0:T(8,128)}, f32[32,3,32,128]{3,2,1,0:T(8,128)}, u32[]{:S(2)}, u32[]{:S(2)}) collective-permute-start(f32[32,3,32,128]{3,2,1,0:T(8,128)} %constant_dynamic-update-slice_fusion.12), channel_id=1, source_target_pairs={{0,3},{8,11},{4,7},{12,15},{16,19},{24,27},{20,23},{28,31},{32,35}... | collective-permute-start | bytes 4718600 | tf_op jit(solution)/shard_map/ppermute | solution.py:28
  101.1 37.2 %collective-permute-start.18 = (f32[32,3,32,128]{3,2,1,0:T(8,128)}, f32[32,3,32,128]{3,2,1,0:T(8,128)}, u32[]{:S(2)}, u32[]{:S(2)}) collective-permute-start(f32[32,3,32,128]{3,2,1,0:T(8,128)} %constant_dynamic-update-slice_fusion.12), channel_id=1, source_target_pairs={{0,1},{8,9},{4,5},{12,13},{16,17},{24,25},{20,21},{28,29},{32,33},... | collective-permute-start | bytes 4718600 | tf_op jit(solution)/shard_map/ppermute | solution.py:28
  151.4 16.1 %collective-permute-start.35 = (f32[256,512]{1,0:T(8,128)S(1)}, f32[256,512]{1,0:T(8,128)S(1)}, u32[]{:S(2)}, u32[]{:S(2)}) collective-permute-start(f32[256,512]{1,0:T(8,128)S(1)} %slice_bitcast_fusion), channel_id=1, source_target_pairs={{0,3},{8,11},{4,7},{12,15},{16,19},{24,27},{20,23},{28,31},{32,35}... | collective-permute-start | bytes 1572872 | tf_op jit(solution)/shard_map/ppermute | solution.py:28
  152.7 31.9 %collective-permute-start.28 = (f32[16,3,32,128]{3,2,1,0:T(8,128)S(1)}, f32[16,3,32,128]{3,2,1,0:T(8,128)}, u32[]{:S(2)}, u32[]{:S(2)}) collective-permute-start(f32[16,3,32,128]{3,2,1,0:T(8,128)S(1)} %slice.45), channel_id=1, source_target_pairs={{0,3},{8,11},{4,7},{12,15},{16,19},{24,27},{20,23},{28,31},{32,35}... | collective-permute-start | bytes 2359304 | tf_op jit(solution)/shard_map/ppermute | solution.py:28
  154.7 30.4 %collective-permute-start.27 = (f32[16,3,32,128]{3,2,1,0:T(8,128)S(1)}, f32[16,3,32,128]{3,2,1,0:T(8,128)}, u32[]{:S(2)}, u32[]{:S(2)}) collective-permute-start(f32[16,3,32,128]{3,2,1,0:T(8,128)S(1)} %slice.44), channel_id=1, source_target_pairs={{0,1},{8,9},{4,5},{12,13},{16,17},{24,25},{20,21},{28,29},{32,33},... | collective-permute-start | bytes 2359304 | tf_op jit(solution)/shard_map/ppermute | solution.py:28
  158.4 26.2 %collective-permute-start.34 = (f32[256,512]{1,0:T(8,128)S(1)}, f32[256,512]{1,0:T(8,128)S(1)}, u32[]{:S(2)}, u32[]{:S(2)}) collective-permute-start(f32[256,512]{1,0:T(8,128)S(1)} %slice_bitcast_fusion.1), channel_id=1, source_target_pairs={{0,1},{8,9},{4,5},{12,13},{16,17},{24,25},{20,21},{28,29},{32,33},... | collective-permute-start | bytes 1572872 | tf_op jit(solution)/shard_map/ppermute | solution.py:28
  163.1 23.5 %collective-permute-start.26 = (f32[16,4,32,128]{3,2,1,0:T(8,128)S(1)}, f32[16,4,32,128]{3,2,1,0:T(8,128)}, u32[]{:S(2)}, u32[]{:S(2)}) collective-permute-start(f32[16,4,32,128]{3,2,1,0:T(8,128)S(1)} %slice.43), channel_id=1, source_target_pairs={{0,192},{8,200},{4,196},{12,204},{16,208},{24,216},{20,212},{28,22... | collective-permute-start | bytes 3145736 | tf_op jit(solution)/shard_map/ppermute | solution.py:28
  167.5 23.4 %collective-permute-start.25 = (f32[16,4,32,128]{3,2,1,0:T(8,128)S(1)}, f32[16,4,32,128]{3,2,1,0:T(8,128)}, u32[]{:S(2)}, u32[]{:S(2)}) collective-permute-start(f32[16,4,32,128]{3,2,1,0:T(8,128)S(1)} %slice.42), channel_id=1, source_target_pairs={{0,64},{8,72},{4,68},{12,76},{16,80},{24,88},{20,84},{28,92},{32,9... | collective-permute-start | bytes 3145736 | tf_op jit(solution)/shard_map/ppermute | solution.py:28
  184.6 14.9 %collective-permute-start.29 = (f32[32,4,32,128]{3,2,1,0:T(8,128)}, f32[32,4,32,128]{3,2,1,0:T(8,128)S(1)}, u32[]{:S(2)}, u32[]{:S(2)}) collective-permute-start(f32[32,4,32,128]{3,2,1,0:T(8,128)} %collective-permute-done.16), channel_id=1, source_target_pairs={{0,8},{8,0},{4,12},{12,4},{16,24},{24,16},{20,28},{28,20},{32,40},... | collective-permute-start | bytes 6291464 | tf_op jit(solution)/shard_map/ppermute | solution.py:28
  184.6 14.9 %collective-permute-start.33 = (f32[2,2,256,512]{3,2,1,0:T(8,128)S(1)}, f32[2,2,256,512]{3,2,1,0:T(8,128)S(1)}, u32[]{:S(2)}, u32[]{:S(2)}) collective-permute-start(f32[2,2,256,512]{3,2,1,0:T(8,128)S(1)} %pad_maximum_fusion.refs_3_), channel_id=1, source_target_pairs={{0,8},{8,0},{4,12},{12,4},{16,24},{24,16},{20,28},{28,20},{32,40},... | collective-permute-start | bytes 6291464 | tf_op jit(solution)/shard_map/ppermute | solution.py:28
  185.1 14.4 %collective-permute-start.30 = (f32[32,4,32,128]{3,2,1,0:T(8,128)}, f32[32,4,32,128]{3,2,1,0:T(8,128)S(1)}, u32[]{:S(2)}, u32[]{:S(2)}) collective-permute-start(f32[32,4,32,128]{3,2,1,0:T(8,128)} %collective-permute-done.17), channel_id=1, source_target_pairs={{0,8},{8,0},{4,12},{12,4},{16,24},{24,16},{20,28},{28,20},{32,40},... | collective-permute-start | bytes 6291464 | tf_op jit(solution)/shard_map/ppermute | solution.py:28
  186.6 10.6 %collective-permute-start.31 = (f32[32,3,32,128]{3,2,1,0:T(8,128)}, f32[32,3,32,128]{3,2,1,0:T(8,128)S(1)}, u32[]{:S(2)}, u32[]{:S(2)}) collective-permute-start(f32[32,3,32,128]{3,2,1,0:T(8,128)} %collective-permute-done.18), channel_id=1, source_target_pairs={{0,8},{8,0},{4,12},{12,4},{16,24},{24,16},{20,28},{28,20},{32,40},... | collective-permute-start | bytes 4718600 | tf_op jit(solution)/shard_map/ppermute | solution.py:28
  190.9 8.6 %collective-permute-start.32 = (f32[32,3,32,128]{3,2,1,0:T(8,128)}, f32[32,3,32,128]{3,2,1,0:T(8,128)S(1)}, u32[]{:S(2)}, u32[]{:S(2)}) collective-permute-start(f32[32,3,32,128]{3,2,1,0:T(8,128)} %collective-permute-done.19), channel_id=1, source_target_pairs={{0,8},{8,0},{4,12},{12,4},{16,24},{24,16},{20,28},{28,20},{32,40},... | collective-permute-start | bytes 4718600 | tf_op jit(solution)/shard_map/ppermute | solution.py:28
  202.7 8.1 %collective-permute-start.36 = (f32[2,256,512]{2,1,0:T(8,128)S(1)}, f32[2,256,512]{2,1,0:T(8,128)}, u32[]{:S(2)}, u32[]{:S(2)}) collective-permute-start(f32[2,256,512]{2,1,0:T(8,128)S(1)} %pad_maximum_fusion.2.refs_4_), channel_id=1, source_target_pairs={{0,8},{8,0},{4,12},{12,4},{16,24},{24,16},{20,28},{28,20},{32,40},... | collective-permute-start | bytes 3145736 | tf_op jit(solution)/shard_map/ppermute | solution.py:28
  (19 other events, 137.9 us)

commit v2 on v1

v2 whole, which is shorter than its diff:
```python
import jax
import jax.numpy as jnp
from jax import lax
from jax.experimental import pallas as pl
from jax.experimental.pallas import tpu as pltpu
from jax.sharding import PartitionSpec as P


NX, NY, NZ = 4, 4, 8
ALL = ("pair", "aux")
EARLY, LATE = 4, 3
SLOTS = EARLY + LATE
PANELS, PANEL, LANES, ROWS = 8, 512, 128, 80


def device_id(x, y, z, core):
    return ((x * NZ // 2 + z // 2) * 2 + core) * 8 + (z % 2) * NY + y


def shift(value, dx=0, dy=0, dz=0, core=0):
    pairs = [
        (device_id(x, y, z, c), device_id((x + dx) % NX, (y + dy) % NY, (z + dz) % NZ, (c + core) % 2))
        for x in range(NX)
        for y in range(NY)
        for z in range(NZ)
        for c in range(2)
    ]
    return lax.ppermute(value, ALL, pairs)


def ring_of_eight(piece):
    near = [shift(piece, dz=d) for d in (1, -1, 2, -2)]
    one, minus_one, two, minus_two = lax.optimization_barrier(near)
    three, minus_three = shift(two, dz=1), shift(minus_two, dz=-1)
    four = shift(two, dz=2)
    return jnp.stack([piece, one, two, three, four, minus_three, minus_two, minus_one])


def spread(factor, pair):
    halves = factor.reshape(2, 8, 32, LANES)
    halves = jnp.where(pair < 16, halves, halves[::-1]).reshape(16, 32, LANES)
    groups = [[8 * p + a for p in (low, 31 - low) for a in range(8)] for low in range(16)]
    return lax.all_to_all(halves, ALL, 0, 0, axis_index_groups=groups, tiled=True)


def share(both, column):
    least = jnp.minimum(column, 7 - column)
    held = []
    for slot in range(SLOTS):
        paired = (slot + 9) // 2 if slot % 2 else 8 + (slot + 8) // 2
        index = jnp.where(slot < 7 - 2 * least, slot + least + 1, paired)
        held.append(lax.dynamic_index_in_dim(both, index, 0, keepdims=False))
    return jnp.stack(held)


def swap(values):
    return [shift(value, core=1) for value in values]


def gather(column, quarter, integrals):
    early, late = column[:, :EARLY], column[:, EARLY:]
    near = [shift(early, dy=1), shift(early, dy=-1), shift(late, dx=1), shift(late, dx=-1)]
    rows = lax.all_to_all(integrals, "pair", 0, 0, tiled=True)
    neighbour = lax.ppermute(quarter, "aux", [(a, (a + 4) % 8) for a in range(8)])
    up, down, late_up, late_down = lax.optimization_barrier(near)
    ends = [shift(up[:4], dy=1), shift(down[4:], dy=-1)]
    late_ends = [shift(late_up[:4], dx=1), shift(late_down[4:], dx=-1)]
    head = jnp.concatenate([early, up])
    head_up, head_down = shift(head, dx=1), shift(head, dx=-1)
    swapped_head = shift(head, core=1)
    ends, late_ends, swapped_head = lax.optimization_barrier((ends, late_ends, swapped_head))
    tail = jnp.concatenate([down, *ends])
    whole = jnp.concatenate([late, late_up, late_down, *late_ends])
    tail_up, tail_down = shift(tail, dx=1), shift(tail, dx=-1)
    late_up, late_down = shift(whole, dy=1), shift(whole, dy=-1)
    swapped = [swapped_head, *swap([tail, whole, quarter])]
    head_up, swapped = lax.optimization_barrier((head_up, swapped))
    far_up = shift(head_up, dx=1)
    tail_down, late_up, late_down, rows, neighbour = lax.optimization_barrier(
        (tail_down, late_up, late_down, rows, neighbour)
    )
    far_down = shift(tail_down, dx=-1)
    late_far = [shift(late_up[:16], dy=1), shift(late_down[16:], dy=-1)]
    sides = [head_up, tail_up, head_down, tail_down, late_up, late_down, neighbour]
    swapped_sides = swap(sides)
    far, swapped_sides = lax.optimization_barrier(([far_up, far_down, *late_far], swapped_sides))
    swapped_far = swap(far)
    diagonals = [quarter, neighbour, swapped[3], swapped_sides[6]]
    arrays = [head, tail, *sides[:4], *far[:2], *swapped[:2], *swapped_sides[:4], *swapped_far[:2]]
    late_arrays = [whole, *sides[4:6], *far[2:], swapped[2], *swapped_sides[4:6], *swapped_far[2:]]
    return rows, diagonals + arrays + late_arrays


EARLY_LAYOUT = ((0, 0, 2), (0, 2, 2), (1, 0, 2), (1, 2, 2), (2, 0, 2), (2, 2, 2), (3, 0, 2), (3, 2, 2))
LATE_LAYOUT = ((0, 0, 4), (1, 0, 4), (2, 0, 4), (3, 0, 2), (3, 2, 2))


def position(delta):
    delta = lax.rem(delta + 4, 4)
    return jnp.where(delta == 3, 1, jnp.where(delta == 0, 0, delta + 1))


def kernel(*refs):
    place_ref, x_ref = refs[:2]
    diagonals, arrays, late_arrays = refs[2:6], refs[6:22], refs[22:32]
    out_ref, held, inverses, remain, parts, inverse_sem, first_sem, second_sem, late_sem = refs[32:]
    x, y, z, core = (place_ref[i] for i in range(4))

    for other in range(2):
        for z_lo in range(2):
            ref = diagonals[2 * other + z_lo]
            pltpu.make_async_copy(ref, inverses.at[other, z_lo], inverse_sem).start()
    for slots, sem in ((pl.ds(0, 2), first_sem), (pl.ds(2, 2), second_sem)):
        for other in range(2):
            for number, (second, block, count) in enumerate(EARLY_LAYOUT):
                ref = arrays[8 * other + number]
                to = held.at[other, pl.ds(block, count), second, :, slots]
                pltpu.make_async_copy(ref.at[:, :, slots], to, sem).start()
    for other in range(2):
        for number, (second, block, count) in enumerate(LATE_LAYOUT):
            to = held.at[other, second, pl.ds(block, count), :, pl.ds(EARLY, LATE)]
            pltpu.make_async_copy(late_arrays[5 * other + number], to, late_sem).start()
    parts[...] = jnp.zeros_like(parts)
    y_positions = [position(sy - y) for sy in range(NY)]

    def slab(p, slot):
        x_position = position(lax.div(p, 8) - x)
        other = lax.rem(p + core, 2)
        sz = 2 * lax.rem(lax.div(p, 2), 4)
        rows = []
        for z_lo in range(2):
            d = lax.rem(z - sz - z_lo + NZ, NZ)
            rows += [held[other, y_positions[sy], x_position, d, slot] for sy in range(NY)]
        return jnp.concatenate(rows)

    def product(left, loads):
        dims = (((1,), (1,)), ((), ()))
        halves = []
        for half in range(2):
            weight = jnp.concatenate([load(half, side) for load in loads for side in range(2)], axis=1)
            high = weight.astype(jnp.bfloat16)
            low = (weight - high.astype(jnp.float32)).astype(jnp.bfloat16)
            twice = lax.dot_general(left, high, dims, preferred_element_type=jnp.float32)
            once = lax.dot_general(left[:ROWS], low, dims, preferred_element_type=jnp.float32)
            halves.append(twice[:ROWS] + (twice[ROWS:] + once))
        return jnp.concatenate(halves, axis=1)

    def split(value):
        high = value.astype(jnp.bfloat16)
        low = (value - high.astype(jnp.float32)).astype(jnp.bfloat16)
        return jnp.concatenate([high, low], axis=0)

    def block(j, k):
        low_slot = jnp.where(j < 8 - k, jnp.maximum(j - k - 1, 0), 2 * j - 9)
        slot = jnp.where(k < 4, low_slot, 2 * j - 8)

        def load(half, side):
            columns = [4 * k + 2 * side + s for s in range(2)]
            return jnp.concatenate([slab(31 - p if half else p, slot) for p in columns], axis=1)

        return load

    def panel(j, carry):
        for first, slots, sem in ((1, pl.ds(0, 2), first_sem), (3, pl.ds(2, 2), second_sem), (5, pl.ds(EARLY, LATE), late_sem)):

            @pl.when(j == first)
            def _():
                arrived = held.at[:, :, :, :, slots]
                pltpu.make_async_copy(arrived, arrived, sem).wait()

        remain[...] = jnp.concatenate([x_ref[4 * j + s] for s in range(4)], axis=1)

        def update(pair, carry):
            k = 2 * pair
            left = jnp.concatenate([parts[k], parts[k + 1]], axis=1)
            remain[...] -= product(left, [block(j, k), block(j, k + 1)])
            return carry

        lax.fori_loop(0, lax.div(j + 1, 2), update, 0)

        def load(half, side):
            other, z_lo = lax.rem(core + half, 2), lax.rem(z + lax.div(j, 4), 2)
            at = position(lax.rem(j, 4) - y)
            return inverses[other, z_lo, at, :, 256 * side : 256 * (side + 1)]

        solved = product(split(remain[...]), [load])
        out_ref[j] = solved
        parts[j] = split(solved)
        return carry

    pltpu.make_async_copy(inverses, inverses, inverse_sem).wait()
    lax.fori_loop(0, PANELS, panel, 0)


def solve(place, rows, arrays):
    arrays = arrays[:4] + [v.reshape(-1, NZ, *v.shape[1:]) for v in arrays[4:]]
    return pl.pallas_call(
        kernel,
        out_shape=jax.ShapeDtypeStruct((PANELS, ROWS, PANEL), jnp.float32),
        in_specs=[pl.BlockSpec(memory_space=pltpu.SMEM), pl.BlockSpec(memory_space=pltpu.VMEM)]
        + [pl.BlockSpec(memory_space=pl.ANY)] * len(arrays),
        out_specs=pl.BlockSpec(memory_space=pltpu.VMEM),
        scratch_shapes=[
            pltpu.VMEM((2, 4, 4, NZ, SLOTS, 32, LANES), jnp.float32),
            pltpu.VMEM((2, 2, 4, 256, PANEL), jnp.float32),
            pltpu.VMEM((ROWS, PANEL), jnp.float32),
            pltpu.VMEM((PANELS, 2 * ROWS, PANEL), jnp.bfloat16),
        ]
        + [pltpu.SemaphoreType.DMA] * 4,
        compiler_params=pltpu.CompilerParams(vmem_limit_bytes=48 * 2**20),
        cost_estimate=pl.CostEstimate(flops=16 * 10**9, bytes_accessed=40 * 10**6, transcendentals=0),
    )(place, rows, *arrays)


def local(integrals, factor, diag_inverse):
    pair, aux = lax.axis_index("pair"), lax.axis_index("aux")
    x, z, core = pair // 8, (pair // 2) % 4 * 2 + aux // NY, pair % 2
    place = jnp.stack([x, aux % NY, z, core]).astype(jnp.int32)

    half = lax.dynamic_slice(diag_inverse[0], (256 * core, 0), (256, PANEL))
    up, down = shift(half, dy=1), shift(half, dy=-1)
    both, up, down = lax.optimization_barrier((spread(factor, pair), up, down))
    ends = jnp.concatenate([shift(up[:128], dy=1), shift(down[128:], dy=-1)])
    column, ends = lax.optimization_barrier((ring_of_eight(share(both, pair // 4)), ends))
    quarter = jnp.stack([half, up, down, ends])
    rows, arrays = gather(column, quarter, integrals)
    solved = solve(place, rows, arrays)
    result = lax.all_to_all(solved, "aux", 0, 0, tiled=True)
    return result.reshape(1, 8 * ROWS, PANEL)


def solution(mesh):
    in_specs = (P(None, "aux", "pair"), P("aux", "pair"), P("aux", None, None))
    out_specs = P("pair", None, "aux")
    return jax.shard_map(local, mesh=mesh, in_specs=in_specs, out_specs=out_specs, check_vma=False)
```

time: 274 us -> 267 us (0.974)
  blocking collectives: 31.1 us -> 22.4 us
  waiting for transfers between devices: 132 us -> 140 us
  starting transfers between devices: 61.2 us -> 57.5 us
    all_to_all x1, blocking collectives: 31.1 us -> 22.4 us  [local(): result = lax.all_to_all(solved, 'aux', 0, 0, tiled=True)]
    ppermute x40 -> x44, waiting for transfers between devices: 122 us -> 130 us  [shift(): return lax.ppermute(value, ALL, pairs)]
    ppermute x40 -> x44, starting transfers between devices: 40.6 us -> 38.9 us  [shift(): return lax.ppermute(value, ALL, pairs)]
    unnamed x37 -> x38, local copies, waits for them, and re-layouts: 8.12 us -> 8.42 us
  transfers between devices with their start and end apart: 43 -> 47, of which waited for: 22 -> 19; matrix products, arithmetic and copies ran while one was open for 4% -> 5% of each run, Pallas kernels for 0% -> 0%
where the time goes in v2:
time: 267 us; the launch traced here: 264 us
  waiting for transfers between devices  140 us (52%)
  starting transfers between devices  57.5 us (22%)
  Pallas kernels  26.2 us (10%)
  blocking collectives  22.4 us (8%)
  local copies, waits for them, and re-layouts  14.2 us (5%)
  other arithmetic  3.54 us (1%)
    ppermute x44, waiting for transfers between devices, shift(): return lax.ppermute(value, ALL, pairs)  130 us
    ppermute x44, starting transfers between devices, shift(): return lax.ppermute(value, ALL, pairs)  38.9 us
    pallas_call x1, Pallas kernels, solve(): pl.pallas_call(kernel, out_shape=jax.ShapeDtypeStruct((PANELS, ROWS, PANE...  26.2 us
    all_to_all x1, blocking collectives, local(): result = lax.all_to_all(solved, 'aux', 0, 0, tiled=True)  22.4 us
    all_to_all x1, starting transfers between devices, spread(): lax.all_to_all(halves, ALL, 0, 0, axis_index_groups=groups, tiled=True)  10.9 us
    all_to_all x1, waiting for transfers between devices, spread(): lax.all_to_all(halves, ALL, 0, 0, axis_index_groups=groups, tiled=True)  9.65 us
    unnamed x38, local copies, waits for them, and re-layouts  8.42 us
    all_to_all x1, starting transfers between devices, gather(): rows = lax.all_to_all(integrals, 'pair', 0, 0, tiled=True)  6.59 us
  transfers between devices with their start and end apart: 47, of which 19 were waited for; matrix products, arithmetic and copies ran while one was open for 5% of the time, Pallas kernels for 0%

profile of v2, /device:TPU:56, one launch (start us, length us, event | category | flops | bytes accessed | tf_op | source)
XLA Modules:
  0.0 263.9 jit_solution(17190711809626261922)
XLA Ops:
  2.1 2.5 collective-permute-start
  4.6 1.8 reverse_select_fusion
  6.4 10.9 %all-to-all-start = ((f32[16,32,128]{2,1,0:T(8,128)}), f32[16,32,128]{2,1,0:T(8,128)S(1)}, u32[]{:S(2)}, u32[]{:S(2)}) async-start(f32[16,32,128]{2,1,0:T(8,128)} %bitcast.5), calls=%async_computation | async-start | bytes 524288 | tf_op jit(solution)/shard_map/all_to_all | solution.py:43
  17.3 9.6 %all-to-all-done = f32[16,32,128]{2,1,0:T(8,128)S(1)} async-done(((f32[16,32,128]{2,1,0:T(8,128)}), f32[16,32,128]{2,1,0:T(8,128)S(1)}, u32[]{:S(2)}, u32[]{:S(2)}) %all-to-all-start) | async-done | bytes 262176 | tf_op jit(solution)/shard_map/all_to_all | solution.py:43
  28.4 1.6 collective-permute-start.4
  30.0 2.0 collective-permute-start.2
  34.5 1.9 collective-permute-start.9
  36.4 1.8 collective-permute-done.4
  39.2 2.2 collective-permute-start.7
  41.4 3.7 %collective-permute-start.6 = (f32[7,32,128]{2,1,0:T(8,128)S(1)}, f32[7,32,128]{2,1,0:T(8,128)S(1)}, u32[]{:S(2)}, u32[]{:S(2)}) collective-permute-start(f32[7,32,128]{2,1,0:T(8,128)S(1)} %collective-permute-done.4), channel_id=1, source_target_pairs={{0,4},{8,12},{4,16},{12,24},{16,20},{24,28},{20,32},{28,40},{32,36... | collective-permute-start | bytes 344072 | tf_op jit(solution)/shard_map/ppermute | solution.py:28
  45.1 6.0 %collective-permute-done.6 = f32[7,32,128]{2,1,0:T(8,128)S(1)} collective-permute-done((f32[7,32,128]{2,1,0:T(8,128)S(1)}, f32[7,32,128]{2,1,0:T(8,128)S(1)}, u32[]{:S(2)}, u32[]{:S(2)}) %collective-permute-start.6) | collective-permute-done | bytes 114720 | tf_op jit(solution)/shard_map/ppermute | solution.py:28
  51.4 3.2 %collective-permute-start.11 = (f32[8,4,32,128]{3,2,1,0:T(8,128)S(1)}, f32[8,4,32,128]{3,2,1,0:T(8,128)S(1)}, u32[]{:S(2)}, u32[]{:S(2)}) collective-permute-start(f32[8,4,32,128]{3,2,1,0:T(8,128)S(1)} %slice.32), channel_id=1, source_target_pairs={{0,1},{8,9},{4,5},{12,13},{16,17},{24,25},{20,21},{28,29},{32,33},... | collective-permute-start | bytes 1572872 | tf_op jit(solution)/shard_map/ppermute | solution.py:28
  55.4 2.0 collective-permute-start.13
  60.1 5.8 %collective-permute-done.14 = f32[8,3,32,128]{3,2,1,0:T(8,128)S(1)} collective-permute-done((f32[8,3,32,128]{3,2,1,0:T(8,128)S(1)}, f32[8,3,32,128]{3,2,1,0:T(8,128)S(1)}, u32[]{:S(2)}, u32[]{:S(2)}) %collective-permute-start.14) | collective-permute-done | bytes 393248 | tf_op jit(solution)/shard_map/ppermute | solution.py:28
  68.4 2.0 collective-permute-start.15
  71.1 4.1 %collective-permute-done.18 = f32[4,3,32,128]{3,2,1,0:T(8,128)} collective-permute-done((f32[4,3,32,128]{3,2,1,0:T(8,128)S(1)}, f32[4,3,32,128]{3,2,1,0:T(8,128)}, u32[]{:S(2)}, u32[]{:S(2)}) %collective-permute-start.18) | collective-permute-done | bytes 196640 | tf_op jit(solution)/shard_map/ppermute | solution.py:28
  75.6 6.6 %all-to-all-start.1 = ((f32[32,80,128]{2,1,0:T(8,128)}), f32[32,80,128]{2,1,0:T(8,128)}, u32[]{:S(2)}, u32[]{:S(2)}) async-start(f32[32,80,128]{2,1,0:T(8,128)} %param.3), calls=%async_computation.1 | async-start | bytes 2621440 | tf_op jit(solution)/shard_map/all_to_all | solution.py:63
  86.0 7.3 %collective-permute-done.16 = f32[4,4,32,128]{3,2,1,0:T(8,128)S(1)} collective-permute-done((f32[4,4,32,128]{3,2,1,0:T(8,128)S(1)}, f32[4,4,32,128]{3,2,1,0:T(8,128)S(1)}, u32[]{:S(2)}, u32[]{:S(2)}) %collective-permute-start.16) | collective-permute-done | bytes 262176 | tf_op jit(solution)/shard_map/ppermute | solution.py:28
  95.9 1.6 constant_dynamic-update-slice_fusion.11
  97.5 1.6 constant_dynamic-update-slice_fusion.10
  99.1 2.1 collective-permute-done.35
  101.3 2.3 collective-permute-start.21
  103.5 14.8 %collective-permute-done.24 = f32[16,4,32,128]{3,2,1,0:T(8,128)S(1)} collective-permute-done((f32[16,4,32,128]{3,2,1,0:T(8,128)S(1)}, f32[16,4,32,128]{3,2,1,0:T(8,128)S(1)}, u32[]{:S(2)}, u32[]{:S(2)}) %collective-permute-start.24) | collective-permute-done | bytes 1048608 | tf_op jit(solution)/shard_map/ppermute | solution.py:28
  119.4 25.9 %collective-permute-done.33 = f32[16,4,32,128]{3,2,1,0:T(8,128)} collective-permute-done((f32[16,4,32,128]{3,2,1,0:T(8,128)S(1)}, f32[16,4,32,128]{3,2,1,0:T(8,128)}, u32[]{:S(2)}, u32[]{:S(2)}) %collective-permute-start.33) | collective-permute-done | bytes 1048608 | tf_op jit(solution)/shard_map/ppermute | solution.py:28
  145.3 3.1 %collective-permute-done.20 = f32[16,4,32,128]{3,2,1,0:T(8,128)S(1)} collective-permute-done((f32[16,4,32,128]{3,2,1,0:T(8,128)S(1)}, f32[16,4,32,128]{3,2,1,0:T(8,128)S(1)}, u32[]{:S(2)}, u32[]{:S(2)}) %collective-permute-start.20) | collective-permute-done | bytes 1048608 | tf_op jit(solution)/shard_map/ppermute | solution.py:28
  152.9 2.8 %collective-permute-start.30 = (f32[16,3,32,128]{3,2,1,0:T(8,128)S(1)}, f32[16,3,32,128]{3,2,1,0:T(8,128)}, u32[]{:S(2)}, u32[]{:S(2)}) collective-permute-start(f32[16,3,32,128]{3,2,1,0:T(8,128)S(1)} %slice.38), channel_id=1, source_target_pairs={{0,1},{8,9},{4,5},{12,13},{16,17},{24,25},{20,21},{28,29},{32,33},... | collective-permute-start | bytes 2359304 | tf_op jit(solution)/shard_map/ppermute | solution.py:28
  156.4 17.2 %collective-permute-done.31 = f32[16,3,32,128]{3,2,1,0:T(8,128)} collective-permute-done((f32[16,3,32,128]{3,2,1,0:T(8,128)S(1)}, f32[16,3,32,128]{3,2,1,0:T(8,128)}, u32[]{:S(2)}, u32[]{:S(2)}) %collective-permute-start.31) | collective-permute-done | bytes 786464 | tf_op jit(solution)/shard_map/ppermute | solution.py:28
  174.2 8.4 %collective-permute-done.28 = f32[16,4,32,128]{3,2,1,0:T(8,128)} collective-permute-done((f32[16,4,32,128]{3,2,1,0:T(8,128)S(1)}, f32[16,4,32,128]{3,2,1,0:T(8,128)}, u32[]{:S(2)}, u32[]{:S(2)}) %collective-permute-start.28) | collective-permute-done | bytes 1048608 | tf_op jit(solution)/shard_map/ppermute | solution.py:28
  183.5 23.8 %collective-permute-done.29 = f32[16,4,32,128]{3,2,1,0:T(8,128)} collective-permute-done((f32[16,4,32,128]{3,2,1,0:T(8,128)S(1)}, f32[16,4,32,128]{3,2,1,0:T(8,128)}, u32[]{:S(2)}, u32[]{:S(2)}) %collective-permute-start.29) | collective-permute-done | bytes 1048608 | tf_op jit(solution)/shard_map/ppermute | solution.py:28
  208.6 4.5 %collective-permute-done.43 = f32[16,3,32,128]{3,2,1,0:T(8,128)} collective-permute-done((f32[16,3,32,128]{3,2,1,0:T(8,128)}, f32[16,3,32,128]{3,2,1,0:T(8,128)}, u32[]{:S(2)}, u32[]{:S(2)}) %collective-permute-start.43) | collective-permute-done | bytes 786464 | tf_op jit(solution)/shard_map/ppermute | solution.py:28
  214.3 26.2 %shard_map.37 = f32[8,80,512]{2,1,0:T(8,128)} custom-call(s32[4]{0:T(128)S(1)} %pad_add_fusion.refs_0_, f32[32,80,128]{2,1,0:T(8,128)} %all-to-all-done.1.refs_1_, f32[4,256,512]{2,1,0:T(8,128)} %pad_maximum_fusion.refs_2_, f32[4,256,512]{2,1,0:T(8,128)} %collective-permute-done.23.refs_3_, f32[4,256,512]{2,1,0:T(8,128)} %collective-permute-done.27.refs_4_, ...), custom_call_target="tpu_custom_call" | custom-call | flops 16000000000 | bytes 40000000 | tf_op jit(solution)/shard_map/pallas_call | solution.py:197
  240.4 22.4 %all_to_all.15 = f32[8,80,512]{2,1,0:T(8,128)S(1)} all-to-all(f32[8,80,512]{2,1,0:T(8,128)} %shard_map.37), channel_id=1, replica_groups=mesh['pair'=32,'aux'=8] {'aux'}, dimensions={0} | all-to-all | bytes 2621440 | tf_op jit(solution)/shard_map/all_to_all | solution.py:228
  (122 shorter events, 31.6 us)
Async XLA Ops:
  1.3 25.7 %collective-permute-start.1 = (f32[256,512]{1,0:T(8,128)S(1)}, f32[256,512]{1,0:T(8,128)S(1)}, u32[]{:S(2)}, u32[]{:S(2)}) collective-permute-start(f32[256,512]{1,0:T(8,128)S(1)} %fusion), channel_id=1, source_target_pairs={{0,3},{8,11},{4,7},{12,15},{16,19},{24,27},{20,23},{28,31},{32,35}... | collective-permute-start | bytes 1572872 | tf_op jit(solution)/shard_map/ppermute | solution.py:28
  2.1 24.8 %collective-permute-start = (f32[256,512]{1,0:T(8,128)S(1)}, f32[256,512]{1,0:T(8,128)S(1)}, u32[]{:S(2)}, u32[]{:S(2)}) collective-permute-start(f32[256,512]{1,0:T(8,128)S(1)} %fusion), channel_id=1, source_target_pairs={{0,1},{8,9},{4,5},{12,13},{16,17},{24,25},{20,21},{28,29},{32,33},... | collective-permute-start | bytes 1572872 | tf_op jit(solution)/shard_map/ppermute | solution.py:28
  6.4 20.5 %all-to-all-start = ((f32[16,32,128]{2,1,0:T(8,128)}), f32[16,32,128]{2,1,0:T(8,128)S(1)}, u32[]{:S(2)}, u32[]{:S(2)}) async-start(f32[16,32,128]{2,1,0:T(8,128)} %bitcast.5), calls=%async_computation | async-start | bytes 524288 | tf_op jit(solution)/shard_map/all_to_all | solution.py:43
  28.4 9.8 %collective-permute-start.4 = (f32[7,32,128]{2,1,0:T(8,128)S(1)}, f32[7,32,128]{2,1,0:T(8,128)S(1)}, u32[]{:S(2)}, u32[]{:S(2)}) collective-permute-start(f32[7,32,128]{2,1,0:T(8,128)S(1)} %constant_dynamic-update-slice_fusion), channel_id=1, source_target_pairs={{0,16},{8,24},{4,20},{12,28},{16,32},{24,40},{20,36},{28,44},{32,4... | collective-permute-start | bytes 344072 | tf_op jit(solution)/shard_map/ppermute | solution.py:28
  32.1 19.0 %collective-permute-start.10 = (f32[128,512]{1,0:T(8,128)S(1)}, f32[128,512]{1,0:T(8,128)S(1)}, u32[]{:S(2)}, u32[]{:S(2)}) collective-permute-start(f32[128,512]{1,0:T(8,128)S(1)} %slice.31), channel_id=1, source_target_pairs={{0,3},{8,11},{4,7},{12,15},{16,19},{24,27},{20,23},{28,31},{32,35}... | collective-permute-start | bytes 786440 | tf_op jit(solution)/shard_map/ppermute | solution.py:28
  34.5 16.7 %collective-permute-start.9 = (f32[128,512]{1,0:T(8,128)S(1)}, f32[128,512]{1,0:T(8,128)S(1)}, u32[]{:S(2)}, u32[]{:S(2)}) collective-permute-start(f32[128,512]{1,0:T(8,128)S(1)} %slice.30), channel_id=1, source_target_pairs={{0,1},{8,9},{4,5},{12,13},{16,17},{24,25},{20,21},{28,29},{32,33},... | collective-permute-start | bytes 786440 | tf_op jit(solution)/shard_map/ppermute | solution.py:28
  39.2 11.9 %collective-permute-start.7 = (f32[7,32,128]{2,1,0:T(8,128)S(1)}, f32[7,32,128]{2,1,0:T(8,128)S(1)}, u32[]{:S(2)}, u32[]{:S(2)}) collective-permute-start(f32[7,32,128]{2,1,0:T(8,128)S(1)} %collective-permute-done.4), channel_id=1, source_target_pairs={{0,16},{8,24},{4,20},{12,28},{16,32},{24,40},{20,36},{28,44},{32,4... | collective-permute-start | bytes 344072 | tf_op jit(solution)/shard_map/ppermute | solution.py:28
  41.4 9.7 %collective-permute-start.6 = (f32[7,32,128]{2,1,0:T(8,128)S(1)}, f32[7,32,128]{2,1,0:T(8,128)S(1)}, u32[]{:S(2)}, u32[]{:S(2)}) collective-permute-start(f32[7,32,128]{2,1,0:T(8,128)S(1)} %collective-permute-done.4), channel_id=1, source_target_pairs={{0,4},{8,12},{4,16},{12,24},{16,20},{24,28},{20,32},{28,40},{32,36... | collective-permute-start | bytes 344072 | tf_op jit(solution)/shard_map/ppermute | solution.py:28
  51.3 15.8 %collective-permute-start.12 = (f32[8,4,32,128]{3,2,1,0:T(8,128)S(1)}, f32[8,4,32,128]{3,2,1,0:T(8,128)S(1)}, u32[]{:S(2)}, u32[]{:S(2)}) collective-permute-start(f32[8,4,32,128]{3,2,1,0:T(8,128)S(1)} %slice.32), channel_id=1, source_target_pairs={{0,3},{8,11},{4,7},{12,15},{16,19},{24,27},{20,23},{28,31},{32,35}... | collective-permute-start | bytes 1572872 | tf_op jit(solution)/shard_map/ppermute | solution.py:28
  51.4 15.7 %collective-permute-start.11 = (f32[8,4,32,128]{3,2,1,0:T(8,128)S(1)}, f32[8,4,32,128]{3,2,1,0:T(8,128)S(1)}, u32[]{:S(2)}, u32[]{:S(2)}) collective-permute-start(f32[8,4,32,128]{3,2,1,0:T(8,128)S(1)} %slice.32), channel_id=1, source_target_pairs={{0,1},{8,9},{4,5},{12,13},{16,17},{24,25},{20,21},{28,29},{32,33},... | collective-permute-start | bytes 1572872 | tf_op jit(solution)/shard_map/ppermute | solution.py:28
  55.4 10.5 %collective-permute-start.14 = (f32[8,3,32,128]{3,2,1,0:T(8,128)S(1)}, f32[8,3,32,128]{3,2,1,0:T(8,128)S(1)}, u32[]{:S(2)}, u32[]{:S(2)}) collective-permute-start(f32[8,3,32,128]{3,2,1,0:T(8,128)S(1)} %get-tuple-element.84), channel_id=1, source_target_pairs={{0,192},{8,200},{4,196},{12,204},{16,208},{24,216},{20,212},{28,22... | collective-permute-start | bytes 1179656 | tf_op jit(solution)/shard_map/ppermute | solution.py:28
  55.4 11.7 %collective-permute-start.13 = (f32[8,3,32,128]{3,2,1,0:T(8,128)S(1)}, f32[8,3,32,128]{3,2,1,0:T(8,128)S(1)}, u32[]{:S(2)}, u32[]{:S(2)}) collective-permute-start(f32[8,3,32,128]{3,2,1,0:T(8,128)S(1)} %get-tuple-element.84), channel_id=1, source_target_pairs={{0,64},{8,72},{4,68},{12,76},{16,80},{24,88},{20,84},{28,92},{32,9... | collective-permute-start | bytes 1179656 | tf_op jit(solution)/shard_map/ppermute | solution.py:28
  59.0 59.4 %collective-permute-start.23 = (f32[4,256,512]{2,1,0:T(8,128)}, f32[4,256,512]{2,1,0:T(8,128)}, u32[]{:S(2)}, u32[]{:S(2)}) collective-permute-start(f32[4,256,512]{2,1,0:T(8,128)} %pad_maximum_fusion.refs_2_), channel_id=1, source_target_pairs={{0,4},{1,5},{2,6},{3,7},{4,0},{5,1},{6,2},{7,3},{8,12},{9,13},{10,... | collective-permute-start | bytes 6291464 | tf_op jit(solution)/shard_map/ppermute | solution.py:64
  67.2 26.1 %collective-permute-start.19 = (f32[16,4,32,128]{3,2,1,0:T(8,128)S(1)}, f32[16,4,32,128]{3,2,1,0:T(8,128)}, u32[]{:S(2)}, u32[]{:S(2)}) collective-permute-start(f32[16,4,32,128]{3,2,1,0:T(8,128)S(1)} %pad_maximum_fusion.1), channel_id=1, source_target_pairs={{0,8},{8,0},{4,12},{12,4},{16,24},{24,16},{20,28},{28,20},{32,40},... | collective-permute-start | bytes 3145736 | tf_op jit(solution)/shard_map/ppermute | solution.py:28
  68.4 15.6 %collective-permute-start.15 = (f32[4,4,32,128]{3,2,1,0:T(8,128)}, f32[4,4,32,128]{3,2,1,0:T(8,128)}, u32[]{:S(2)}, u32[]{:S(2)}) collective-permute-start(f32[4,4,32,128]{3,2,1,0:T(8,128)} %slice.34), channel_id=1, source_target_pairs={{0,1},{8,9},{4,5},{12,13},{16,17},{24,25},{20,21},{28,29},{32,33},... | collective-permute-start | bytes 786440 | tf_op jit(solution)/shard_map/ppermute | solution.py:28
  70.4 30.8 %collective-permute-start.35 = (f32[16,4,32,128]{3,2,1,0:T(8,128)S(1)}, f32[16,4,32,128]{3,2,1,0:T(8,128)}, u32[]{:S(2)}, u32[]{:S(2)}) collective-permute-start(f32[16,4,32,128]{3,2,1,0:T(8,128)S(1)} %pad_maximum_fusion.1), channel_id=1, source_target_pairs={{0,192},{8,200},{4,196},{12,204},{16,208},{24,216},{20,212},{28,22... | collective-permute-start | bytes 3145736 | tf_op jit(solution)/shard_map/ppermute | solution.py:28
  75.6 74.3 %all-to-all-start.1 = ((f32[32,80,128]{2,1,0:T(8,128)}), f32[32,80,128]{2,1,0:T(8,128)}, u32[]{:S(2)}, u32[]{:S(2)}) async-start(f32[32,80,128]{2,1,0:T(8,128)} %param.3), calls=%async_computation.1 | async-start | bytes 2621440 | tf_op jit(solution)/shard_map/all_to_all | solution.py:63
  82.8 35.6 %collective-permute-start.24 = (f32[16,4,32,128]{3,2,1,0:T(8,128)S(1)}, f32[16,4,32,128]{3,2,1,0:T(8,128)S(1)}, u32[]{:S(2)}, u32[]{:S(2)}) collective-permute-start(f32[16,4,32,128]{3,2,1,0:T(8,128)S(1)} %pad_maximum_fusion.1), channel_id=1, source_target_pairs={{0,64},{8,72},{4,68},{12,76},{16,80},{24,88},{20,84},{28,92},{32,9... | collective-permute-start | bytes 3145736 | tf_op jit(solution)/shard_map/ppermute | solution.py:28
  94.3 51.0 %collective-permute-start.33 = (f32[16,4,32,128]{3,2,1,0:T(8,128)S(1)}, f32[16,4,32,128]{3,2,1,0:T(8,128)}, u32[]{:S(2)}, u32[]{:S(2)}) collective-permute-start(f32[16,4,32,128]{3,2,1,0:T(8,128)S(1)} %constant_dynamic-update-slice_fusion.7), channel_id=1, source_target_pairs={{0,64},{8,72},{4,68},{12,76},{16,80},{24,88},{20,84},{28,92},{32,9... | collective-permute-start | bytes 3145736 | tf_op jit(solution)/shard_map/ppermute | solution.py:28
  99.1 50.3 %collective-permute-start.22 = (f32[32,3,32,128]{3,2,1,0:T(8,128)}, f32[32,3,32,128]{3,2,1,0:T(8,128)}, u32[]{:S(2)}, u32[]{:S(2)}) collective-permute-start(f32[32,3,32,128]{3,2,1,0:T(8,128)} %constant_dynamic-update-slice_fusion.10), channel_id=1, source_target_pairs={{0,3},{8,11},{4,7},{12,15},{16,19},{24,27},{20,23},{28,31},{32,35}... | collective-permute-start | bytes 4718600 | tf_op jit(solution)/shard_map/ppermute | solution.py:28
  101.3 48.1 %collective-permute-start.21 = (f32[32,3,32,128]{3,2,1,0:T(8,128)}, f32[32,3,32,128]{3,2,1,0:T(8,128)}, u32[]{:S(2)}, u32[]{:S(2)}) collective-permute-start(f32[32,3,32,128]{3,2,1,0:T(8,128)} %constant_dynamic-update-slice_fusion.10), channel_id=1, source_target_pairs={{0,1},{8,9},{4,5},{12,13},{16,17},{24,25},{20,21},{28,29},{32,33},... | collective-permute-start | bytes 4718600 | tf_op jit(solution)/shard_map/ppermute | solution.py:28
  118.4 34.0 %collective-permute-start.27 = (f32[4,256,512]{2,1,0:T(8,128)}, f32[4,256,512]{2,1,0:T(8,128)}, u32[]{:S(2)}, u32[]{:S(2)}) collective-permute-start(f32[4,256,512]{2,1,0:T(8,128)} %pad_maximum_fusion.refs_2_), channel_id=1, source_target_pairs={{0,8},{8,0},{4,12},{12,4},{16,24},{24,16},{20,28},{28,20},{32,40},... | collective-permute-start | bytes 6291464 | tf_op jit(solution)/shard_map/ppermute | solution.py:28
  118.4 30.0 %collective-permute-start.20 = (f32[16,4,32,128]{3,2,1,0:T(8,128)S(1)}, f32[16,4,32,128]{3,2,1,0:T(8,128)S(1)}, u32[]{:S(2)}, u32[]{:S(2)}) collective-permute-start(f32[16,4,32,128]{3,2,1,0:T(8,128)S(1)} %constant_dynamic-update-slice_fusion.7), channel_id=1, source_target_pairs={{0,192},{8,200},{4,196},{12,204},{16,208},{24,216},{20,212},{28,22... | collective-permute-start | bytes 3145736 | tf_op jit(solution)/shard_map/ppermute | solution.py:28
  145.3 10.5 %collective-permute-start.26 = (f32[32,3,32,128]{3,2,1,0:T(8,128)}, f32[32,3,32,128]{3,2,1,0:T(8,128)}, u32[]{:S(2)}, u32[]{:S(2)}) collective-permute-start(f32[32,3,32,128]{3,2,1,0:T(8,128)} %constant_dynamic-update-slice_fusion.10), channel_id=1, source_target_pairs={{0,8},{8,0},{4,12},{12,4},{16,24},{24,16},{20,28},{28,20},{32,40},... | collective-permute-start | bytes 4718600 | tf_op jit(solution)/shard_map/ppermute | solution.py:28
  152.4 21.1 %collective-permute-start.31 = (f32[16,3,32,128]{3,2,1,0:T(8,128)S(1)}, f32[16,3,32,128]{3,2,1,0:T(8,128)}, u32[]{:S(2)}, u32[]{:S(2)}) collective-permute-start(f32[16,3,32,128]{3,2,1,0:T(8,128)S(1)} %slice.39), channel_id=1, source_target_pairs={{0,3},{8,11},{4,7},{12,15},{16,19},{24,27},{20,23},{28,31},{32,35}... | collective-permute-start | bytes 2359304 | tf_op jit(solution)/shard_map/ppermute | solution.py:28
  152.9 20.6 %collective-permute-start.30 = (f32[16,3,32,128]{3,2,1,0:T(8,128)S(1)}, f32[16,3,32,128]{3,2,1,0:T(8,128)}, u32[]{:S(2)}, u32[]{:S(2)}) collective-permute-start(f32[16,3,32,128]{3,2,1,0:T(8,128)S(1)} %slice.38), channel_id=1, source_target_pairs={{0,1},{8,9},{4,5},{12,13},{16,17},{24,25},{20,21},{28,29},{32,33},... | collective-permute-start | bytes 2359304 | tf_op jit(solution)/shard_map/ppermute | solution.py:28
  155.8 18.3 %collective-permute-start.32 = (f32[16,4,32,128]{3,2,1,0:T(8,128)S(1)}, f32[16,4,32,128]{3,2,1,0:T(8,128)S(1)}, u32[]{:S(2)}, u32[]{:S(2)}) collective-permute-start(f32[16,4,32,128]{3,2,1,0:T(8,128)S(1)} %copy-done.4), channel_id=1, source_target_pairs={{0,8},{8,0},{4,12},{12,4},{16,24},{24,16},{20,28},{28,20},{32,40},... | collective-permute-start | bytes 3145736 | tf_op jit(solution)/shard_map/ppermute | solution.py:28
  155.8 26.9 %collective-permute-start.28 = (f32[16,4,32,128]{3,2,1,0:T(8,128)S(1)}, f32[16,4,32,128]{3,2,1,0:T(8,128)}, u32[]{:S(2)}, u32[]{:S(2)}) collective-permute-start(f32[16,4,32,128]{3,2,1,0:T(8,128)S(1)} %copy-done.4), channel_id=1, source_target_pairs={{0,64},{8,72},{4,68},{12,76},{16,80},{24,88},{20,84},{28,92},{32,9... | collective-permute-start | bytes 3145736 | tf_op jit(solution)/shard_map/ppermute | solution.py:28
  155.9 51.5 %collective-permute-start.40 = (f32[4,256,512]{2,1,0:T(8,128)}, f32[4,256,512]{2,1,0:T(8,128)}, u32[]{:S(2)}, u32[]{:S(2)}) collective-permute-start(f32[4,256,512]{2,1,0:T(8,128)} %collective-permute-done.23.refs_3_), channel_id=1, source_target_pairs={{0,8},{8,0},{4,12},{12,4},{16,24},{24,16},{20,28},{28,20},{32,40},... | collective-permute-start | bytes 6291464 | tf_op jit(solution)/shard_map/ppermute | solution.py:28
  173.6 33.8 %collective-permute-start.38 = (f32[32,3,32,128]{3,2,1,0:T(8,128)}, f32[32,3,32,128]{3,2,1,0:T(8,128)}, u32[]{:S(2)}, u32[]{:S(2)}) collective-permute-start(f32[32,3,32,128]{3,2,1,0:T(8,128)} %collective-permute-done.21), channel_id=1, source_target_pairs={{0,8},{8,0},{4,12},{12,4},{16,24},{24,16},{20,28},{28,20},{32,40},... | collective-permute-start | bytes 4718600 | tf_op jit(solution)/shard_map/ppermute | solution.py:28
  173.6 33.8 %collective-permute-start.39 = (f32[32,3,32,128]{3,2,1,0:T(8,128)}, f32[32,3,32,128]{3,2,1,0:T(8,128)}, u32[]{:S(2)}, u32[]{:S(2)}) collective-permute-start(f32[32,3,32,128]{3,2,1,0:T(8,128)} %collective-permute-done.22), channel_id=1, source_target_pairs={{0,8},{8,0},{4,12},{12,4},{16,24},{24,16},{20,28},{28,20},{32,40},... | collective-permute-start | bytes 4718600 | tf_op jit(solution)/shard_map/ppermute | solution.py:28
  182.7 24.7 %collective-permute-start.29 = (f32[16,4,32,128]{3,2,1,0:T(8,128)S(1)}, f32[16,4,32,128]{3,2,1,0:T(8,128)}, u32[]{:S(2)}, u32[]{:S(2)}) collective-permute-start(f32[16,4,32,128]{3,2,1,0:T(8,128)S(1)} %copy-done.6), channel_id=1, source_target_pairs={{0,192},{8,200},{4,196},{12,204},{16,208},{24,216},{20,212},{28,22... | collective-permute-start | bytes 3145736 | tf_op jit(solution)/shard_map/ppermute | solution.py:28
  (24 other events, 245.5 us)

commit v3 on v2

--- a/solution.py
+++ b/solution.py
@@ -76,18 +76,16 @@
     swapped = [swapped_head, *swap([tail, whole, quarter])]
     head_up, swapped = lax.optimization_barrier((head_up, swapped))
     far_up = shift(head_up, dx=1)
-    tail_down, late_up, late_down, rows, neighbour = lax.optimization_barrier(
-        (tail_down, late_up, late_down, rows, neighbour)
-    )
+    tail_down, late_up, late_down, rows = lax.optimization_barrier((tail_down, late_up, late_down, rows))
     far_down = shift(tail_down, dx=-1)
     late_far = [shift(late_up[:16], dy=1), shift(late_down[16:], dy=-1)]
-    sides = [head_up, tail_up, head_down, tail_down, late_up, late_down, neighbour]
+    sides = [head_up, tail_up, head_down, tail_down, late_up, late_down]
     swapped_sides = swap(sides)
     far, swapped_sides = lax.optimization_barrier(([far_up, far_down, *late_far], swapped_sides))
-    swapped_far = swap(far)
-    diagonals = [quarter, neighbour, swapped[3], swapped_sides[6]]
+    swapped_far = swap([*far, neighbour])
+    diagonals = [quarter, neighbour, swapped[3], swapped_far[4]]
     arrays = [head, tail, *sides[:4], *far[:2], *swapped[:2], *swapped_sides[:4], *swapped_far[:2]]
-    late_arrays = [whole, *sides[4:6], *far[2:], swapped[2], *swapped_sides[4:6], *swapped_far[2:]]
+    late_arrays = [whole, *sides[4:], *far[2:], swapped[2], *swapped_sides[4:], *swapped_far[2:4]]
     return rows, diagonals + arrays + late_arrays
 
 

time: 267 us -> 276 us (1.034)
  waiting for transfers between devices: 140 us -> 146 us
  blocking collectives: 22.4 us -> 25.6 us
    ppermute x44, waiting for transfers between devices: 130 us -> 136 us  [shift(): return lax.ppermute(value, ALL, pairs)]
    ppermute x44, starting transfers between devices: 38.9 us -> 42.8 us  [shift(): return lax.ppermute(value, ALL, pairs)]
    all_to_all x1, blocking collectives: 22.4 us -> 25.6 us  [local(): result = lax.all_to_all(solved, 'aux', 0, 0, tiled=True)]
    unnamed x38 -> x48, local copies, waits for them, and re-layouts: 8.42 us -> 8.17 us
  transfers between devices with their start and end apart: 47 -> 47, of which waited for: 19 -> 22; matrix products, arithmetic and copies ran while one was open for 5% -> 4% of each run, Pallas kernels for 0% -> 0%
where the time goes in v3:
time: 276 us; the launch traced here: 273 us
  waiting for transfers between devices  146 us (53%)
  starting transfers between devices  58.4 us (21%)
  Pallas kernels  26.2 us (9%)
  blocking collectives  25.6 us (9%)
  local copies, waits for them, and re-layouts  13 us (5%)
  other arithmetic  3.56 us (1%)
    ppermute x44, waiting for transfers between devices, shift(): return lax.ppermute(value, ALL, pairs)  136 us
    ppermute x44, starting transfers between devices, shift(): return lax.ppermute(value, ALL, pairs)  42.8 us
    pallas_call x1, Pallas kernels, solve(): pl.pallas_call(kernel, out_shape=jax.ShapeDtypeStruct((PANELS, ROWS, PANE...  26.2 us
    all_to_all x1, blocking collectives, local(): result = lax.all_to_all(solved, 'aux', 0, 0, tiled=True)  25.6 us
    all_to_all x1, starting transfers between devices, spread(): lax.all_to_all(halves, ALL, 0, 0, axis_index_groups=groups, tiled=True)  10.9 us
    all_to_all x1, waiting for transfers between devices, spread(): lax.all_to_all(halves, ALL, 0, 0, axis_index_groups=groups, tiled=True)  9.65 us
    unnamed x48, local copies, waits for them, and re-layouts  8.17 us
  transfers between devices with their start and end apart: 47, of which 22 were waited for; matrix products, arithmetic and copies ran while one was open for 4% of the time, Pallas kernels for 0%

profile of v3, /device:TPU:56, one launch (start us, length us, event | category | flops | bytes accessed | tf_op | source)
XLA Modules:
  0.0 273.2 jit_solution(9073274888909149943)
XLA Ops:
  2.1 2.5 collective-permute-start
  4.6 1.8 reverse_select_fusion
  6.4 10.9 %all-to-all-start = ((f32[16,32,128]{2,1,0:T(8,128)}), f32[16,32,128]{2,1,0:T(8,128)S(1)}, u32[]{:S(2)}, u32[]{:S(2)}) async-start(f32[16,32,128]{2,1,0:T(8,128)} %bitcast.5), calls=%async_computation | async-start | bytes 524288 | tf_op jit(solution)/shard_map/all_to_all | solution.py:43
  17.3 9.6 %all-to-all-done = f32[16,32,128]{2,1,0:T(8,128)S(1)} async-done(((f32[16,32,128]{2,1,0:T(8,128)}), f32[16,32,128]{2,1,0:T(8,128)S(1)}, u32[]{:S(2)}, u32[]{:S(2)}) %all-to-all-start) | async-done | bytes 262176 | tf_op jit(solution)/shard_map/all_to_all | solution.py:43
  28.4 1.6 collective-permute-start.4
  30.0 2.0 collective-permute-start.2
  34.5 1.9 collective-permute-start.9
  36.4 1.8 collective-permute-done.4
  39.2 2.2 collective-permute-start.7
  41.4 3.7 %collective-permute-start.6 = (f32[7,32,128]{2,1,0:T(8,128)S(1)}, f32[7,32,128]{2,1,0:T(8,128)S(1)}, u32[]{:S(2)}, u32[]{:S(2)}) collective-permute-start(f32[7,32,128]{2,1,0:T(8,128)S(1)} %collective-permute-done.4), channel_id=1, source_target_pairs={{0,4},{8,12},{4,16},{12,24},{16,20},{24,28},{20,32},{28,40},{32,36... | collective-permute-start | bytes 344072 | tf_op jit(solution)/shard_map/ppermute | solution.py:28
  45.1 6.0 %collective-permute-done.6 = f32[7,32,128]{2,1,0:T(8,128)S(1)} collective-permute-done((f32[7,32,128]{2,1,0:T(8,128)S(1)}, f32[7,32,128]{2,1,0:T(8,128)S(1)}, u32[]{:S(2)}, u32[]{:S(2)}) %collective-permute-start.6) | collective-permute-done | bytes 114720 | tf_op jit(solution)/shard_map/ppermute | solution.py:28
  51.4 3.2 %collective-permute-start.11 = (f32[8,4,32,128]{3,2,1,0:T(8,128)S(1)}, f32[8,4,32,128]{3,2,1,0:T(8,128)S(1)}, u32[]{:S(2)}, u32[]{:S(2)}) collective-permute-start(f32[8,4,32,128]{3,2,1,0:T(8,128)S(1)} %slice.32), channel_id=1, source_target_pairs={{0,1},{8,9},{4,5},{12,13},{16,17},{24,25},{20,21},{28,29},{32,33},... | collective-permute-start | bytes 1572872 | tf_op jit(solution)/shard_map/ppermute | solution.py:28
  55.4 2.0 collective-permute-start.13
  59.0 6.9 %collective-permute-done.14 = f32[8,3,32,128]{3,2,1,0:T(8,128)S(1)} collective-permute-done((f32[8,3,32,128]{3,2,1,0:T(8,128)S(1)}, f32[8,3,32,128]{3,2,1,0:T(8,128)S(1)}, u32[]{:S(2)}, u32[]{:S(2)}) %collective-permute-start.14) | collective-permute-done | bytes 393248 | tf_op jit(solution)/shard_map/ppermute | solution.py:28
  68.4 2.0 collective-permute-start.15
  70.4 2.1 collective-permute-start.17
  72.5 2.2 collective-permute-done.18
  76.9 1.8 collective-permute-done.17
  79.4 4.7 %all-to-all-start.1 = ((f32[32,80,128]{2,1,0:T(8,128)}), f32[32,80,128]{2,1,0:T(8,128)}, u32[]{:S(2)}, u32[]{:S(2)}) async-start(f32[32,80,128]{2,1,0:T(8,128)} %param.3), calls=%async_computation.1 | async-start | bytes 2621440 | tf_op jit(solution)/shard_map/all_to_all | solution.py:63
  84.2 1.7 collective-permute-start.24
  91.5 19.0 %collective-permute-done.30 = f32[16,4,32,128]{3,2,1,0:T(8,128)} collective-permute-done((f32[16,4,32,128]{3,2,1,0:T(8,128)S(1)}, f32[16,4,32,128]{3,2,1,0:T(8,128)}, u32[]{:S(2)}, u32[]{:S(2)}) %collective-permute-start.30) | collective-permute-done | bytes 1048608 | tf_op jit(solution)/shard_map/ppermute | solution.py:28
  110.5 14.7 %collective-permute-done.24 = f32[16,4,32,128]{3,2,1,0:T(8,128)S(1)} collective-permute-done((f32[16,4,32,128]{3,2,1,0:T(8,128)S(1)}, f32[16,4,32,128]{3,2,1,0:T(8,128)S(1)}, u32[]{:S(2)}, u32[]{:S(2)}) %collective-permute-start.24) | collective-permute-done | bytes 1048608 | tf_op jit(solution)/shard_map/ppermute | solution.py:28
  126.0 3.2 %collective-permute-start.21 = (f32[32,3,32,128]{3,2,1,0:T(8,128)}, f32[32,3,32,128]{3,2,1,0:T(8,128)}, u32[]{:S(2)}, u32[]{:S(2)}) collective-permute-start(f32[32,3,32,128]{3,2,1,0:T(8,128)} %constant_dynamic-update-slice_fusion.10), channel_id=1, source_target_pairs={{0,1},{8,9},{4,5},{12,13},{16,17},{24,25},{20,21},{28,29},{32,33},... | collective-permute-start | bytes 4718600 | tf_op jit(solution)/shard_map/ppermute | solution.py:28
  129.2 18.0 %collective-permute-done.29 = f32[16,4,32,128]{3,2,1,0:T(8,128)} collective-permute-done((f32[16,4,32,128]{3,2,1,0:T(8,128)S(1)}, f32[16,4,32,128]{3,2,1,0:T(8,128)}, u32[]{:S(2)}, u32[]{:S(2)}) %collective-permute-start.29) | collective-permute-done | bytes 1048608 | tf_op jit(solution)/shard_map/ppermute | solution.py:28
  147.2 2.1 collective-permute-done.20
  150.4 11.8 %collective-permute-done.21 = f32[32,3,32,128]{3,2,1,0:T(8,128)} collective-permute-done((f32[32,3,32,128]{3,2,1,0:T(8,128)}, f32[32,3,32,128]{3,2,1,0:T(8,128)}, u32[]{:S(2)}, u32[]{:S(2)}) %collective-permute-start.21) | collective-permute-done | bytes 1572896 | tf_op jit(solution)/shard_map/ppermute | solution.py:28
  166.1 3.8 %collective-permute-start.33 = (f32[16,3,32,128]{3,2,1,0:T(8,128)S(1)}, f32[16,3,32,128]{3,2,1,0:T(8,128)}, u32[]{:S(2)}, u32[]{:S(2)}) collective-permute-start(f32[16,3,32,128]{3,2,1,0:T(8,128)S(1)} %slice.38), channel_id=1, source_target_pairs={{0,1},{8,9},{4,5},{12,13},{16,17},{24,25},{20,21},{28,29},{32,33},... | collective-permute-start | bytes 2359304 | tf_op jit(solution)/shard_map/ppermute | solution.py:28
  169.9 15.7 %collective-permute-done.34 = f32[16,3,32,128]{3,2,1,0:T(8,128)} collective-permute-done((f32[16,3,32,128]{3,2,1,0:T(8,128)S(1)}, f32[16,3,32,128]{3,2,1,0:T(8,128)}, u32[]{:S(2)}, u32[]{:S(2)}) %collective-permute-start.34) | collective-permute-done | bytes 786464 | tf_op jit(solution)/shard_map/ppermute | solution.py:28
  190.7 22.8 %collective-permute-done.31 = f32[16,4,32,128]{3,2,1,0:T(8,128)} collective-permute-done((f32[16,4,32,128]{3,2,1,0:T(8,128)S(1)}, f32[16,4,32,128]{3,2,1,0:T(8,128)}, u32[]{:S(2)}, u32[]{:S(2)}) %collective-permute-start.31) | collective-permute-done | bytes 1048608 | tf_op jit(solution)/shard_map/ppermute | solution.py:28
  214.8 4.5 %collective-permute-done.43 = f32[16,3,32,128]{3,2,1,0:T(8,128)} collective-permute-done((f32[16,3,32,128]{3,2,1,0:T(8,128)}, f32[16,3,32,128]{3,2,1,0:T(8,128)}, u32[]{:S(2)}, u32[]{:S(2)}) %collective-permute-start.43) | collective-permute-done | bytes 786464 | tf_op jit(solution)/shard_map/ppermute | solution.py:28
  220.4 26.2 %shard_map.37 = f32[8,80,512]{2,1,0:T(8,128)} custom-call(s32[4]{0:T(128)S(1)} %pad_add_fusion.refs_0_, f32[32,80,128]{2,1,0:T(8,128)} %all-to-all-done.1.refs_1_, f32[4,256,512]{2,1,0:T(8,128)} %pad_maximum_fusion.refs_2_, f32[4,256,512]{2,1,0:T(8,128)} %collective-permute-done.23.refs_3_, f32[4,256,512]{2,1,0:T(8,128)} %collective-permute-done.27.refs_4_, ...), custom_call_target="tpu_custom_call" | custom-call | flops 16000000000 | bytes 40000000 | tf_op jit(solution)/shard_map/pallas_call | solution.py:195
  246.6 25.6 %all_to_all.15 = f32[8,80,512]{2,1,0:T(8,128)S(1)} all-to-all(f32[8,80,512]{2,1,0:T(8,128)} %shard_map.37), channel_id=1, replica_groups=mesh['pair'=32,'aux'=8] {'aux'}, dimensions={0} | all-to-all | bytes 2621440 | tf_op jit(solution)/shard_map/all_to_all | solution.py:226
  (132 shorter events, 34.8 us)
Async XLA Ops:
  1.3 25.7 %collective-permute-start.1 = (f32[256,512]{1,0:T(8,128)S(1)}, f32[256,512]{1,0:T(8,128)S(1)}, u32[]{:S(2)}, u32[]{:S(2)}) collective-permute-start(f32[256,512]{1,0:T(8,128)S(1)} %fusion), channel_id=1, source_target_pairs={{0,3},{8,11},{4,7},{12,15},{16,19},{24,27},{20,23},{28,31},{32,35}... | collective-permute-start | bytes 1572872 | tf_op jit(solution)/shard_map/ppermute | solution.py:28
  2.1 24.8 %collective-permute-start = (f32[256,512]{1,0:T(8,128)S(1)}, f32[256,512]{1,0:T(8,128)S(1)}, u32[]{:S(2)}, u32[]{:S(2)}) collective-permute-start(f32[256,512]{1,0:T(8,128)S(1)} %fusion), channel_id=1, source_target_pairs={{0,1},{8,9},{4,5},{12,13},{16,17},{24,25},{20,21},{28,29},{32,33},... | collective-permute-start | bytes 1572872 | tf_op jit(solution)/shard_map/ppermute | solution.py:28
  6.4 20.5 %all-to-all-start = ((f32[16,32,128]{2,1,0:T(8,128)}), f32[16,32,128]{2,1,0:T(8,128)S(1)}, u32[]{:S(2)}, u32[]{:S(2)}) async-start(f32[16,32,128]{2,1,0:T(8,128)} %bitcast.5), calls=%async_computation | async-start | bytes 524288 | tf_op jit(solution)/shard_map/all_to_all | solution.py:43
  32.1 19.0 %collective-permute-start.10 = (f32[128,512]{1,0:T(8,128)S(1)}, f32[128,512]{1,0:T(8,128)S(1)}, u32[]{:S(2)}, u32[]{:S(2)}) collective-permute-start(f32[128,512]{1,0:T(8,128)S(1)} %slice.31), channel_id=1, source_target_pairs={{0,3},{8,11},{4,7},{12,15},{16,19},{24,27},{20,23},{28,31},{32,35}... | collective-permute-start | bytes 786440 | tf_op jit(solution)/shard_map/ppermute | solution.py:28
  34.5 16.7 %collective-permute-start.9 = (f32[128,512]{1,0:T(8,128)S(1)}, f32[128,512]{1,0:T(8,128)S(1)}, u32[]{:S(2)}, u32[]{:S(2)}) collective-permute-start(f32[128,512]{1,0:T(8,128)S(1)} %slice.30), channel_id=1, source_target_pairs={{0,1},{8,9},{4,5},{12,13},{16,17},{24,25},{20,21},{28,29},{32,33},... | collective-permute-start | bytes 786440 | tf_op jit(solution)/shard_map/ppermute | solution.py:28
  39.2 11.9 %collective-permute-start.7 = (f32[7,32,128]{2,1,0:T(8,128)S(1)}, f32[7,32,128]{2,1,0:T(8,128)S(1)}, u32[]{:S(2)}, u32[]{:S(2)}) collective-permute-start(f32[7,32,128]{2,1,0:T(8,128)S(1)} %collective-permute-done.4), channel_id=1, source_target_pairs={{0,16},{8,24},{4,20},{12,28},{16,32},{24,40},{20,36},{28,44},{32,4... | collective-permute-start | bytes 344072 | tf_op jit(solution)/shard_map/ppermute | solution.py:28
  51.3 15.8 %collective-permute-start.12 = (f32[8,4,32,128]{3,2,1,0:T(8,128)S(1)}, f32[8,4,32,128]{3,2,1,0:T(8,128)S(1)}, u32[]{:S(2)}, u32[]{:S(2)}) collective-permute-start(f32[8,4,32,128]{3,2,1,0:T(8,128)S(1)} %slice.32), channel_id=1, source_target_pairs={{0,3},{8,11},{4,7},{12,15},{16,19},{24,27},{20,23},{28,31},{32,35}... | collective-permute-start | bytes 1572872 | tf_op jit(solution)/shard_map/ppermute | solution.py:28
  51.4 15.7 %collective-permute-start.11 = (f32[8,4,32,128]{3,2,1,0:T(8,128)S(1)}, f32[8,4,32,128]{3,2,1,0:T(8,128)S(1)}, u32[]{:S(2)}, u32[]{:S(2)}) collective-permute-start(f32[8,4,32,128]{3,2,1,0:T(8,128)S(1)} %slice.32), channel_id=1, source_target_pairs={{0,1},{8,9},{4,5},{12,13},{16,17},{24,25},{20,21},{28,29},{32,33},... | collective-permute-start | bytes 1572872 | tf_op jit(solution)/shard_map/ppermute | solution.py:28
  55.4 10.5 %collective-permute-start.14 = (f32[8,3,32,128]{3,2,1,0:T(8,128)S(1)}, f32[8,3,32,128]{3,2,1,0:T(8,128)S(1)}, u32[]{:S(2)}, u32[]{:S(2)}) collective-permute-start(f32[8,3,32,128]{3,2,1,0:T(8,128)S(1)} %get-tuple-element.80), channel_id=1, source_target_pairs={{0,192},{8,200},{4,196},{12,204},{16,208},{24,216},{20,212},{28,22... | collective-permute-start | bytes 1179656 | tf_op jit(solution)/shard_map/ppermute | solution.py:28
  55.4 11.7 %collective-permute-start.13 = (f32[8,3,32,128]{3,2,1,0:T(8,128)S(1)}, f32[8,3,32,128]{3,2,1,0:T(8,128)S(1)}, u32[]{:S(2)}, u32[]{:S(2)}) collective-permute-start(f32[8,3,32,128]{3,2,1,0:T(8,128)S(1)} %get-tuple-element.80), channel_id=1, source_target_pairs={{0,64},{8,72},{4,68},{12,76},{16,80},{24,88},{20,84},{28,92},{32,9... | collective-permute-start | bytes 1179656 | tf_op jit(solution)/shard_map/ppermute | solution.py:28
  59.0 67.0 %collective-permute-start.27 = (f32[4,256,512]{2,1,0:T(8,128)}, f32[4,256,512]{2,1,0:T(8,128)}, u32[]{:S(2)}, u32[]{:S(2)}) collective-permute-start(f32[4,256,512]{2,1,0:T(8,128)} %pad_maximum_fusion.refs_2_), channel_id=1, source_target_pairs={{0,8},{8,0},{4,12},{12,4},{16,24},{24,16},{20,28},{28,20},{32,40},... | collective-permute-start | bytes 6291464 | tf_op jit(solution)/shard_map/ppermute | solution.py:28
  67.2 21.2 %collective-permute-start.19 = (f32[16,4,32,128]{3,2,1,0:T(8,128)S(1)}, f32[16,4,32,128]{3,2,1,0:T(8,128)}, u32[]{:S(2)}, u32[]{:S(2)}) collective-permute-start(f32[16,4,32,128]{3,2,1,0:T(8,128)S(1)} %pad_maximum_fusion.1), channel_id=1, source_target_pairs={{0,8},{8,0},{4,12},{12,4},{16,24},{24,16},{20,28},{28,20},{32,40},... | collective-permute-start | bytes 3145736 | tf_op jit(solution)/shard_map/ppermute | solution.py:28
  68.4 15.7 %collective-permute-start.15 = (f32[4,4,32,128]{3,2,1,0:T(8,128)}, f32[4,4,32,128]{3,2,1,0:T(8,128)S(1)}, u32[]{:S(2)}, u32[]{:S(2)}) collective-permute-start(f32[4,4,32,128]{3,2,1,0:T(8,128)} %slice.34), channel_id=1, source_target_pairs={{0,1},{8,9},{4,5},{12,13},{16,17},{24,25},{20,21},{28,29},{32,33},... | collective-permute-start | bytes 786440 | tf_op jit(solution)/shard_map/ppermute | solution.py:28
  74.7 35.8 %collective-permute-start.30 = (f32[16,4,32,128]{3,2,1,0:T(8,128)S(1)}, f32[16,4,32,128]{3,2,1,0:T(8,128)}, u32[]{:S(2)}, u32[]{:S(2)}) collective-permute-start(f32[16,4,32,128]{3,2,1,0:T(8,128)S(1)} %pad_maximum_fusion.1), channel_id=1, source_target_pairs={{0,192},{8,200},{4,196},{12,204},{16,208},{24,216},{20,212},{28,22... | collective-permute-start | bytes 3145736 | tf_op jit(solution)/shard_map/ppermute | solution.py:28
  79.4 82.8 %all-to-all-start.1 = ((f32[32,80,128]{2,1,0:T(8,128)}), f32[32,80,128]{2,1,0:T(8,128)}, u32[]{:S(2)}, u32[]{:S(2)}) async-start(f32[32,80,128]{2,1,0:T(8,128)} %param.3), calls=%async_computation.1 | async-start | bytes 2621440 | tf_op jit(solution)/shard_map/all_to_all | solution.py:63
  84.2 41.0 %collective-permute-start.24 = (f32[16,4,32,128]{3,2,1,0:T(8,128)S(1)}, f32[16,4,32,128]{3,2,1,0:T(8,128)S(1)}, u32[]{:S(2)}, u32[]{:S(2)}) collective-permute-start(f32[16,4,32,128]{3,2,1,0:T(8,128)S(1)} %pad_maximum_fusion.1), channel_id=1, source_target_pairs={{0,64},{8,72},{4,68},{12,76},{16,80},{24,88},{20,84},{28,92},{32,9... | collective-permute-start | bytes 3145736 | tf_op jit(solution)/shard_map/ppermute | solution.py:28
  89.9 59.5 %collective-permute-start.22 = (f32[32,3,32,128]{3,2,1,0:T(8,128)}, f32[32,3,32,128]{3,2,1,0:T(8,128)}, u32[]{:S(2)}, u32[]{:S(2)}) collective-permute-start(f32[32,3,32,128]{3,2,1,0:T(8,128)} %constant_dynamic-update-slice_fusion.10), channel_id=1, source_target_pairs={{0,3},{8,11},{4,7},{12,15},{16,19},{24,27},{20,23},{28,31},{32,35}... | collective-permute-start | bytes 4718600 | tf_op jit(solution)/shard_map/ppermute | solution.py:28
  90.8 56.4 %collective-permute-start.29 = (f32[16,4,32,128]{3,2,1,0:T(8,128)S(1)}, f32[16,4,32,128]{3,2,1,0:T(8,128)}, u32[]{:S(2)}, u32[]{:S(2)}) collective-permute-start(f32[16,4,32,128]{3,2,1,0:T(8,128)S(1)} %constant_dynamic-update-slice_fusion.7), channel_id=1, source_target_pairs={{0,64},{8,72},{4,68},{12,76},{16,80},{24,88},{20,84},{28,92},{32,9... | collective-permute-start | bytes 3145736 | tf_op jit(solution)/shard_map/ppermute | solution.py:28
  110.5 53.0 %collective-permute-start.23 = (f32[4,256,512]{2,1,0:T(8,128)}, f32[4,256,512]{2,1,0:T(8,128)}, u32[]{:S(2)}, u32[]{:S(2)}) collective-permute-start(f32[4,256,512]{2,1,0:T(8,128)} %pad_maximum_fusion.refs_2_), channel_id=1, source_target_pairs={{0,4},{1,5},{2,6},{3,7},{4,0},{5,1},{6,2},{7,3},{8,12},{9,13},{10,... | collective-permute-start | bytes 6291464 | tf_op jit(solution)/shard_map/ppermute | solution.py:64
  125.2 24.2 %collective-permute-start.20 = (f32[16,4,32,128]{3,2,1,0:T(8,128)S(1)}, f32[16,4,32,128]{3,2,1,0:T(8,128)S(1)}, u32[]{:S(2)}, u32[]{:S(2)}) collective-permute-start(f32[16,4,32,128]{3,2,1,0:T(8,128)S(1)} %constant_dynamic-update-slice_fusion.7), channel_id=1, source_target_pairs={{0,192},{8,200},{4,196},{12,204},{16,208},{24,216},{20,212},{28,22... | collective-permute-start | bytes 3145736 | tf_op jit(solution)/shard_map/ppermute | solution.py:28
  126.0 36.2 %collective-permute-start.21 = (f32[32,3,32,128]{3,2,1,0:T(8,128)}, f32[32,3,32,128]{3,2,1,0:T(8,128)}, u32[]{:S(2)}, u32[]{:S(2)}) collective-permute-start(f32[32,3,32,128]{3,2,1,0:T(8,128)} %constant_dynamic-update-slice_fusion.10), channel_id=1, source_target_pairs={{0,1},{8,9},{4,5},{12,13},{16,17},{24,25},{20,21},{28,29},{32,33},... | collective-permute-start | bytes 4718600 | tf_op jit(solution)/shard_map/ppermute | solution.py:28
  147.2 18.9 %collective-permute-start.26 = (f32[32,3,32,128]{3,2,1,0:T(8,128)}, f32[32,3,32,128]{3,2,1,0:T(8,128)}, u32[]{:S(2)}, u32[]{:S(2)}) collective-permute-start(f32[32,3,32,128]{3,2,1,0:T(8,128)} %constant_dynamic-update-slice_fusion.10), channel_id=1, source_target_pairs={{0,8},{8,0},{4,12},{12,4},{16,24},{24,16},{20,28},{28,20},{32,40},... | collective-permute-start | bytes 4718600 | tf_op jit(solution)/shard_map/ppermute | solution.py:28
  149.4 14.2 %collective-permute-start.37 = (f32[16,4,32,128]{3,2,1,0:T(8,128)}, f32[16,4,32,128]{3,2,1,0:T(8,128)}, u32[]{:S(2)}, u32[]{:S(2)}) collective-permute-start(f32[16,4,32,128]{3,2,1,0:T(8,128)} %collective-permute-done.30), channel_id=1, source_target_pairs={{0,8},{8,0},{4,12},{12,4},{16,24},{24,16},{20,28},{28,20},{32,40},... | collective-permute-start | bytes 3145736 | tf_op jit(solution)/shard_map/ppermute | solution.py:28
  150.4 13.8 %collective-permute-start.25 = (f32[16,4,32,128]{3,2,1,0:T(8,128)S(1)}, f32[16,4,32,128]{3,2,1,0:T(8,128)}, u32[]{:S(2)}, u32[]{:S(2)}) collective-permute-start(f32[16,4,32,128]{3,2,1,0:T(8,128)S(1)} %constant_dynamic-update-slice_fusion.7), channel_id=1, source_target_pairs={{0,8},{8,0},{4,12},{12,4},{16,24},{24,16},{20,28},{28,20},{32,40},... | collective-permute-start | bytes 3145736 | tf_op jit(solution)/shard_map/ppermute | solution.py:28
  163.5 22.1 %collective-permute-start.34 = (f32[16,3,32,128]{3,2,1,0:T(8,128)S(1)}, f32[16,3,32,128]{3,2,1,0:T(8,128)}, u32[]{:S(2)}, u32[]{:S(2)}) collective-permute-start(f32[16,3,32,128]{3,2,1,0:T(8,128)S(1)} %slice.39), channel_id=1, source_target_pairs={{0,3},{8,11},{4,7},{12,15},{16,19},{24,27},{20,23},{28,31},{32,35}... | collective-permute-start | bytes 2359304 | tf_op jit(solution)/shard_map/ppermute | solution.py:28
  163.6 23.1 %collective-permute-start.38 = (f32[16,4,32,128]{3,2,1,0:T(8,128)}, f32[16,4,32,128]{3,2,1,0:T(8,128)S(1)}, u32[]{:S(2)}, u32[]{:S(2)}) collective-permute-start(f32[16,4,32,128]{3,2,1,0:T(8,128)} %copy-done.11), channel_id=1, source_target_pairs={{0,8},{8,0},{4,12},{12,4},{16,24},{24,16},{20,28},{28,20},{32,40},... | collective-permute-start | bytes 3145736 | tf_op jit(solution)/shard_map/ppermute | solution.py:28
  164.2 25.5 %collective-permute-start.32 = (f32[16,4,32,128]{3,2,1,0:T(8,128)}, f32[16,4,32,128]{3,2,1,0:T(8,128)}, u32[]{:S(2)}, u32[]{:S(2)}) collective-permute-start(f32[16,4,32,128]{3,2,1,0:T(8,128)} %copy-done.11), channel_id=1, source_target_pairs={{0,192},{8,200},{4,196},{12,204},{16,208},{24,216},{20,212},{28,22... | collective-permute-start | bytes 3145736 | tf_op jit(solution)/shard_map/ppermute | solution.py:28
  166.1 20.6 %collective-permute-start.33 = (f32[16,3,32,128]{3,2,1,0:T(8,128)S(1)}, f32[16,3,32,128]{3,2,1,0:T(8,128)}, u32[]{:S(2)}, u32[]{:S(2)}) collective-permute-start(f32[16,3,32,128]{3,2,1,0:T(8,128)S(1)} %slice.38), channel_id=1, source_target_pairs={{0,1},{8,9},{4,5},{12,13},{16,17},{24,25},{20,21},{28,29},{32,33},... | collective-permute-start | bytes 2359304 | tf_op jit(solution)/shard_map/ppermute | solution.py:28
  169.9 43.7 %collective-permute-start.39 = (f32[32,3,32,128]{3,2,1,0:T(8,128)}, f32[32,3,32,128]{3,2,1,0:T(8,128)}, u32[]{:S(2)}, u32[]{:S(2)}) collective-permute-start(f32[32,3,32,128]{3,2,1,0:T(8,128)} %collective-permute-done.21), channel_id=1, source_target_pairs={{0,8},{8,0},{4,12},{12,4},{16,24},{24,16},{20,28},{28,20},{32,40},... | collective-permute-start | bytes 4718600 | tf_op jit(solution)/shard_map/ppermute | solution.py:28
  185.6 28.0 %collective-permute-start.40 = (f32[32,3,32,128]{3,2,1,0:T(8,128)}, f32[32,3,32,128]{3,2,1,0:T(8,128)}, u32[]{:S(2)}, u32[]{:S(2)}) collective-permute-start(f32[32,3,32,128]{3,2,1,0:T(8,128)} %collective-permute-done.22), channel_id=1, source_target_pairs={{0,8},{8,0},{4,12},{12,4},{16,24},{24,16},{20,28},{28,20},{32,40},... | collective-permute-start | bytes 4718600 | tf_op jit(solution)/shard_map/ppermute | solution.py:28
  186.7 26.9 %collective-permute-start.31 = (f32[16,4,32,128]{3,2,1,0:T(8,128)S(1)}, f32[16,4,32,128]{3,2,1,0:T(8,128)}, u32[]{:S(2)}, u32[]{:S(2)}) collective-permute-start(f32[16,4,32,128]{3,2,1,0:T(8,128)S(1)} %copy-done.10), channel_id=1, source_target_pairs={{0,64},{8,72},{4,68},{12,76},{16,80},{24,88},{20,84},{28,92},{32,9... | collective-permute-start | bytes 3145736 | tf_op jit(solution)/shard_map/ppermute | solution.py:28
  189.7 25.1 %collective-permute-start.28 = (f32[4,256,512]{2,1,0:T(8,128)}, f32[4,256,512]{2,1,0:T(8,128)}, u32[]{:S(2)}, u32[]{:S(2)}) collective-permute-start(f32[4,256,512]{2,1,0:T(8,128)} %collective-permute-done.23.refs_3_), channel_id=1, source_target_pairs={{0,8},{8,0},{4,12},{12,4},{16,24},{24,16},{20,28},{28,20},{32,40},... | collective-permute-start | bytes 6291464 | tf_op jit(solution)/shard_map/ppermute | solution.py:28
  (29 other events, 241.5 us)

commit v4 on v3

--- a/solution.py
+++ b/solution.py
@@ -101,7 +101,7 @@
 def kernel(*refs):
     place_ref, x_ref = refs[:2]
     diagonals, arrays, late_arrays = refs[2:6], refs[6:22], refs[22:32]
-    out_ref, held, inverses, remain, parts, inverse_sem, first_sem, second_sem, late_sem = refs[32:]
+    out_ref, held, inverses, remain, parts, firsts, inverse_sem, first_sem, second_sem, late_sem = refs[32:]
     x, y, z, core = (place_ref[i] for i in range(4))
 
     for other in range(2):
@@ -119,37 +119,40 @@
             to = held.at[other, second, pl.ds(block, count), :, pl.ds(EARLY, LATE)]
             pltpu.make_async_copy(late_arrays[5 * other + number], to, late_sem).start()
     parts[...] = jnp.zeros_like(parts)
-    y_positions = [position(sy - y) for sy in range(NY)]
+    y_offsets = [position(sy - y) * (4 * NZ * SLOTS) for sy in range(NY)]
+    flat = held.reshape(256 * SLOTS, 32, LANES)
+
+    @pl.loop(0, 32)
+    def _(p):
+        base = (lax.rem(p + core, 2) * 16 + position(lax.div(p, 8) - x)) * NZ
+        for z_lo in range(2):
+            d = lax.rem(z - 2 * lax.rem(lax.div(p, 2), 4) - z_lo + NZ, NZ)
+            firsts[2 * p + z_lo] = (base + d) * SLOTS
 
     def slab(p, slot):
-        x_position = position(lax.div(p, 8) - x)
-        other = lax.rem(p + core, 2)
-        sz = 2 * lax.rem(lax.div(p, 2), 4)
         rows = []
         for z_lo in range(2):
-            d = lax.rem(z - sz - z_lo + NZ, NZ)
-            rows += [held[other, y_positions[sy], x_position, d, slot] for sy in range(NY)]
+            at = firsts[2 * p + z_lo] + slot
+            rows += [flat[at + y_offsets[sy]] for sy in range(NY)]
         return jnp.concatenate(rows)
 
-    def product(left, loads):
-        dims = (((1,), (1,)), ((), ()))
+    def product(right, load):
         halves = []
         for half in range(2):
-            weight = jnp.concatenate([load(half, side) for load in loads for side in range(2)], axis=1)
+            weight = jnp.concatenate([load(half, side) for side in range(2)], axis=1)
             high = weight.astype(jnp.bfloat16)
             low = (weight - high.astype(jnp.float32)).astype(jnp.bfloat16)
-            twice = lax.dot_general(left, high, dims, preferred_element_type=jnp.float32)
-            once = lax.dot_general(left[:ROWS], low, dims, preferred_element_type=jnp.float32)
-            halves.append(twice[:ROWS] + (twice[ROWS:] + once))
-        return jnp.concatenate(halves, axis=1)
-
-    def split(value):
+            both = jnp.dot(jnp.concatenate([high, low]), right, preferred_element_type=jnp.float32)
+            halves.append(both[:256, :ROWS] + (both[:256, LANES : LANES + ROWS] + both[256:, :ROWS]))
+        return jnp.concatenate(halves)
+
+    def split(value, to):
         high = value.astype(jnp.bfloat16)
-        low = (value - high.astype(jnp.float32)).astype(jnp.bfloat16)
-        return jnp.concatenate([high, low], axis=0)
+        to[:, :ROWS] = high
+        to[:, LANES : LANES + ROWS] = (value - high.astype(jnp.float32)).astype(jnp.bfloat16)
 
     def block(j, k):
-        low_slot = jnp.where(j < 8 - k, jnp.maximum(j - k - 1, 0), 2 * j - 9)
+        low_slot = jnp.where(j < 8 - k, j - k - 1, 2 * j - 9)
         slot = jnp.where(k < 4, low_slot, 2 * j - 8)
 
         def load(half, side):
@@ -166,24 +169,23 @@
                 arrived = held.at[:, :, :, :, slots]
                 pltpu.make_async_copy(arrived, arrived, sem).wait()
 
-        remain[...] = jnp.concatenate([x_ref[4 * j + s] for s in range(4)], axis=1)
-
-        def update(pair, carry):
-            k = 2 * pair
-            left = jnp.concatenate([parts[k], parts[k + 1]], axis=1)
-            remain[...] -= product(left, [block(j, k), block(j, k + 1)])
+        remain[...] = jnp.concatenate([x_ref[4 * j + s].T for s in range(4)])
+
+        def update(k, carry):
+            remain[...] -= product(parts[k], block(j, k))
             return carry
 
-        lax.fori_loop(0, lax.div(j + 1, 2), update, 0)
+        lax.fori_loop(0, j, update, 0)
 
         def load(half, side):
             other, z_lo = lax.rem(core + half, 2), lax.rem(z + lax.div(j, 4), 2)
             at = position(lax.rem(j, 4) - y)
             return inverses[other, z_lo, at, :, 256 * side : 256 * (side + 1)]
 
-        solved = product(split(remain[...]), [load])
-        out_ref[j] = solved
-        parts[j] = split(solved)
+        split(remain[...], parts.at[j])
+        solved = product(parts[j], load)
+        out_ref[j] = solved.T
+        split(solved, parts.at[j])
         return carry
 
     pltpu.make_async_copy(inverses, inverses, inverse_sem).wait()
@@ -201,8 +203,9 @@
         scratch_shapes=[
             pltpu.VMEM((2, 4, 4, NZ, SLOTS, 32, LANES), jnp.float32),
             pltpu.VMEM((2, 2, 4, 256, PANEL), jnp.float32),
-            pltpu.VMEM((ROWS, PANEL), jnp.float32),
-            pltpu.VMEM((PANELS, 2 * ROWS, PANEL), jnp.bfloat16),
+            pltpu.VMEM((PANEL, ROWS), jnp.float32),
+            pltpu.VMEM((PANELS, PANEL, 2 * LANES), jnp.bfloat16),
+            pltpu.SMEM((64,), jnp.int32),
         ]
         + [pltpu.SemaphoreType.DMA] * 4,
         compiler_params=pltpu.CompilerParams(vmem_limit_bytes=48 * 2**20),

time: 276 us -> 275 us (level)
  no operation moved by 1% of the time
where the time goes in v4:
time: 275 us; the launch traced here: 272 us
  waiting for transfers between devices  146 us (53%)
  starting transfers between devices  58.4 us (21%)
  blocking collectives  25.6 us (9%)
  Pallas kernels  25 us (9%)
  local copies, waits for them, and re-layouts  13 us (5%)
  other arithmetic  3.56 us (1%)
    ppermute x44, waiting for transfers between devices, shift(): return lax.ppermute(value, ALL, pairs)  136 us
    ppermute x44, starting transfers between devices, shift(): return lax.ppermute(value, ALL, pairs)  42.8 us
    all_to_all x1, blocking collectives, local(): result = lax.all_to_all(solved, 'aux', 0, 0, tiled=True)  25.6 us
    pallas_call x1, Pallas kernels, solve(): pl.pallas_call(kernel, out_shape=jax.ShapeDtypeStruct((PANELS, ROWS, PANE...  25 us
    all_to_all x1, starting transfers between devices, spread(): lax.all_to_all(halves, ALL, 0, 0, axis_index_groups=groups, tiled=True)  10.9 us
    all_to_all x1, waiting for transfers between devices, spread(): lax.all_to_all(halves, ALL, 0, 0, axis_index_groups=groups, tiled=True)  9.65 us
    unnamed x48, local copies, waits for them, and re-layouts  8.17 us
  transfers between devices with their start and end apart: 47, of which 22 were waited for; matrix products, arithmetic and copies ran while one was open for 4% of the time, Pallas kernels for 0%

profile of v4, /device:TPU:56, one launch (start us, length us, event | category | flops | bytes accessed | tf_op | source)
XLA Modules:
  0.0 272.1 jit_solution(5888060162128945714)
XLA Ops:
  2.1 2.5 collective-permute-start
  4.6 1.8 reverse_select_fusion
  6.4 10.9 %all-to-all-start = ((f32[16,32,128]{2,1,0:T(8,128)}), f32[16,32,128]{2,1,0:T(8,128)S(1)}, u32[]{:S(2)}, u32[]{:S(2)}) async-start(f32[16,32,128]{2,1,0:T(8,128)} %bitcast.5), calls=%async_computation | async-start | bytes 524288 | tf_op jit(solution)/shard_map/all_to_all | solution.py:43
  17.3 9.6 %all-to-all-done = f32[16,32,128]{2,1,0:T(8,128)S(1)} async-done(((f32[16,32,128]{2,1,0:T(8,128)}), f32[16,32,128]{2,1,0:T(8,128)S(1)}, u32[]{:S(2)}, u32[]{:S(2)}) %all-to-all-start) | async-done | bytes 262176 | tf_op jit(solution)/shard_map/all_to_all | solution.py:43
  28.4 1.6 collective-permute-start.4
  30.0 2.0 collective-permute-start.2
  34.5 1.9 collective-permute-start.9
  36.4 1.8 collective-permute-done.4
  39.2 2.2 collective-permute-start.7
  41.4 3.7 %collective-permute-start.6 = (f32[7,32,128]{2,1,0:T(8,128)S(1)}, f32[7,32,128]{2,1,0:T(8,128)S(1)}, u32[]{:S(2)}, u32[]{:S(2)}) collective-permute-start(f32[7,32,128]{2,1,0:T(8,128)S(1)} %collective-permute-done.4), channel_id=1, source_target_pairs={{0,4},{8,12},{4,16},{12,24},{16,20},{24,28},{20,32},{28,40},{32,36... | collective-permute-start | bytes 344072 | tf_op jit(solution)/shard_map/ppermute | solution.py:28
  45.1 6.0 %collective-permute-done.6 = f32[7,32,128]{2,1,0:T(8,128)S(1)} collective-permute-done((f32[7,32,128]{2,1,0:T(8,128)S(1)}, f32[7,32,128]{2,1,0:T(8,128)S(1)}, u32[]{:S(2)}, u32[]{:S(2)}) %collective-permute-start.6) | collective-permute-done | bytes 114720 | tf_op jit(solution)/shard_map/ppermute | solution.py:28
  51.4 3.2 %collective-permute-start.11 = (f32[8,4,32,128]{3,2,1,0:T(8,128)S(1)}, f32[8,4,32,128]{3,2,1,0:T(8,128)S(1)}, u32[]{:S(2)}, u32[]{:S(2)}) collective-permute-start(f32[8,4,32,128]{3,2,1,0:T(8,128)S(1)} %slice.32), channel_id=1, source_target_pairs={{0,1},{8,9},{4,5},{12,13},{16,17},{24,25},{20,21},{28,29},{32,33},... | collective-permute-start | bytes 1572872 | tf_op jit(solution)/shard_map/ppermute | solution.py:28
  55.4 2.0 collective-permute-start.13
  59.0 6.9 %collective-permute-done.14 = f32[8,3,32,128]{3,2,1,0:T(8,128)S(1)} collective-permute-done((f32[8,3,32,128]{3,2,1,0:T(8,128)S(1)}, f32[8,3,32,128]{3,2,1,0:T(8,128)S(1)}, u32[]{:S(2)}, u32[]{:S(2)}) %collective-permute-start.14) | collective-permute-done | bytes 393248 | tf_op jit(solution)/shard_map/ppermute | solution.py:28
  68.4 2.0 collective-permute-start.15
  70.4 2.1 collective-permute-start.17
  72.5 2.2 collective-permute-done.18
  76.9 1.8 collective-permute-done.17
  79.4 4.7 %all-to-all-start.1 = ((f32[32,80,128]{2,1,0:T(8,128)}), f32[32,80,128]{2,1,0:T(8,128)}, u32[]{:S(2)}, u32[]{:S(2)}) async-start(f32[32,80,128]{2,1,0:T(8,128)} %param.3), calls=%async_computation.1 | async-start | bytes 2621440 | tf_op jit(solution)/shard_map/all_to_all | solution.py:63
  84.2 1.7 collective-permute-start.24
  91.5 19.0 %collective-permute-done.30 = f32[16,4,32,128]{3,2,1,0:T(8,128)} collective-permute-done((f32[16,4,32,128]{3,2,1,0:T(8,128)S(1)}, f32[16,4,32,128]{3,2,1,0:T(8,128)}, u32[]{:S(2)}, u32[]{:S(2)}) %collective-permute-start.30) | collective-permute-done | bytes 1048608 | tf_op jit(solution)/shard_map/ppermute | solution.py:28
  110.5 14.7 %collective-permute-done.24 = f32[16,4,32,128]{3,2,1,0:T(8,128)S(1)} collective-permute-done((f32[16,4,32,128]{3,2,1,0:T(8,128)S(1)}, f32[16,4,32,128]{3,2,1,0:T(8,128)S(1)}, u32[]{:S(2)}, u32[]{:S(2)}) %collective-permute-start.24) | collective-permute-done | bytes 1048608 | tf_op jit(solution)/shard_map/ppermute | solution.py:28
  126.0 3.2 %collective-permute-start.21 = (f32[32,3,32,128]{3,2,1,0:T(8,128)}, f32[32,3,32,128]{3,2,1,0:T(8,128)}, u32[]{:S(2)}, u32[]{:S(2)}) collective-permute-start(f32[32,3,32,128]{3,2,1,0:T(8,128)} %constant_dynamic-update-slice_fusion.10), channel_id=1, source_target_pairs={{0,1},{8,9},{4,5},{12,13},{16,17},{24,25},{20,21},{28,29},{32,33},... | collective-permute-start | bytes 4718600 | tf_op jit(solution)/shard_map/ppermute | solution.py:28
  129.2 18.0 %collective-permute-done.29 = f32[16,4,32,128]{3,2,1,0:T(8,128)} collective-permute-done((f32[16,4,32,128]{3,2,1,0:T(8,128)S(1)}, f32[16,4,32,128]{3,2,1,0:T(8,128)}, u32[]{:S(2)}, u32[]{:S(2)}) %collective-permute-start.29) | collective-permute-done | bytes 1048608 | tf_op jit(solution)/shard_map/ppermute | solution.py:28
  147.2 2.1 collective-permute-done.20
  150.4 11.8 %collective-permute-done.21 = f32[32,3,32,128]{3,2,1,0:T(8,128)} collective-permute-done((f32[32,3,32,128]{3,2,1,0:T(8,128)}, f32[32,3,32,128]{3,2,1,0:T(8,128)}, u32[]{:S(2)}, u32[]{:S(2)}) %collective-permute-start.21) | collective-permute-done | bytes 1572896 | tf_op jit(solution)/shard_map/ppermute | solution.py:28
  166.1 3.8 %collective-permute-start.33 = (f32[16,3,32,128]{3,2,1,0:T(8,128)S(1)}, f32[16,3,32,128]{3,2,1,0:T(8,128)}, u32[]{:S(2)}, u32[]{:S(2)}) collective-permute-start(f32[16,3,32,128]{3,2,1,0:T(8,128)S(1)} %slice.38), channel_id=1, source_target_pairs={{0,1},{8,9},{4,5},{12,13},{16,17},{24,25},{20,21},{28,29},{32,33},... | collective-permute-start | bytes 2359304 | tf_op jit(solution)/shard_map/ppermute | solution.py:28
  169.9 15.7 %collective-permute-done.34 = f32[16,3,32,128]{3,2,1,0:T(8,128)} collective-permute-done((f32[16,3,32,128]{3,2,1,0:T(8,128)S(1)}, f32[16,3,32,128]{3,2,1,0:T(8,128)}, u32[]{:S(2)}, u32[]{:S(2)}) %collective-permute-start.34) | collective-permute-done | bytes 786464 | tf_op jit(solution)/shard_map/ppermute | solution.py:28
  190.7 22.8 %collective-permute-done.31 = f32[16,4,32,128]{3,2,1,0:T(8,128)} collective-permute-done((f32[16,4,32,128]{3,2,1,0:T(8,128)S(1)}, f32[16,4,32,128]{3,2,1,0:T(8,128)}, u32[]{:S(2)}, u32[]{:S(2)}) %collective-permute-start.31) | collective-permute-done | bytes 1048608 | tf_op jit(solution)/shard_map/ppermute | solution.py:28
  214.8 4.5 %collective-permute-done.43 = f32[16,3,32,128]{3,2,1,0:T(8,128)} collective-permute-done((f32[16,3,32,128]{3,2,1,0:T(8,128)}, f32[16,3,32,128]{3,2,1,0:T(8,128)}, u32[]{:S(2)}, u32[]{:S(2)}) %collective-permute-start.43) | collective-permute-done | bytes 786464 | tf_op jit(solution)/shard_map/ppermute | solution.py:28
  220.4 25.0 %shard_map.37 = f32[8,80,512]{2,1,0:T(8,128)} custom-call(s32[4]{0:T(128)S(1)} %pad_add_fusion.refs_0_, f32[32,80,128]{2,1,0:T(8,128)} %all-to-all-done.1.refs_1_, f32[4,256,512]{2,1,0:T(8,128)} %pad_maximum_fusion.refs_2_, f32[4,256,512]{2,1,0:T(8,128)} %collective-permute-done.23.refs_3_, f32[4,256,512]{2,1,0:T(8,128)} %collective-permute-done.27.refs_4_, ...), custom_call_target="tpu_custom_call" | custom-call | flops 16000000000 | bytes 40000000 | tf_op jit(solution)/shard_map/pallas_call | solution.py:197
  245.5 25.6 %all_to_all.15 = f32[8,80,512]{2,1,0:T(8,128)S(1)} all-to-all(f32[8,80,512]{2,1,0:T(8,128)} %shard_map.37), channel_id=1, replica_groups=mesh['pair'=32,'aux'=8] {'aux'}, dimensions={0} | all-to-all | bytes 2621440 | tf_op jit(solution)/shard_map/all_to_all | solution.py:229
  (132 shorter events, 34.8 us)
Async XLA Ops:
  1.3 25.7 %collective-permute-start.1 = (f32[256,512]{1,0:T(8,128)S(1)}, f32[256,512]{1,0:T(8,128)S(1)}, u32[]{:S(2)}, u32[]{:S(2)}) collective-permute-start(f32[256,512]{1,0:T(8,128)S(1)} %fusion), channel_id=1, source_target_pairs={{0,3},{8,11},{4,7},{12,15},{16,19},{24,27},{20,23},{28,31},{32,35}... | collective-permute-start | bytes 1572872 | tf_op jit(solution)/shard_map/ppermute | solution.py:28
  2.1 24.8 %collective-permute-start = (f32[256,512]{1,0:T(8,128)S(1)}, f32[256,512]{1,0:T(8,128)S(1)}, u32[]{:S(2)}, u32[]{:S(2)}) collective-permute-start(f32[256,512]{1,0:T(8,128)S(1)} %fusion), channel_id=1, source_target_pairs={{0,1},{8,9},{4,5},{12,13},{16,17},{24,25},{20,21},{28,29},{32,33},... | collective-permute-start | bytes 1572872 | tf_op jit(solution)/shard_map/ppermute | solution.py:28
  6.4 20.5 %all-to-all-start = ((f32[16,32,128]{2,1,0:T(8,128)}), f32[16,32,128]{2,1,0:T(8,128)S(1)}, u32[]{:S(2)}, u32[]{:S(2)}) async-start(f32[16,32,128]{2,1,0:T(8,128)} %bitcast.5), calls=%async_computation | async-start | bytes 524288 | tf_op jit(solution)/shard_map/all_to_all | solution.py:43
  32.1 19.0 %collective-permute-start.10 = (f32[128,512]{1,0:T(8,128)S(1)}, f32[128,512]{1,0:T(8,128)S(1)}, u32[]{:S(2)}, u32[]{:S(2)}) collective-permute-start(f32[128,512]{1,0:T(8,128)S(1)} %slice.31), channel_id=1, source_target_pairs={{0,3},{8,11},{4,7},{12,15},{16,19},{24,27},{20,23},{28,31},{32,35}... | collective-permute-start | bytes 786440 | tf_op jit(solution)/shard_map/ppermute | solution.py:28
  34.5 16.7 %collective-permute-start.9 = (f32[128,512]{1,0:T(8,128)S(1)}, f32[128,512]{1,0:T(8,128)S(1)}, u32[]{:S(2)}, u32[]{:S(2)}) collective-permute-start(f32[128,512]{1,0:T(8,128)S(1)} %slice.30), channel_id=1, source_target_pairs={{0,1},{8,9},{4,5},{12,13},{16,17},{24,25},{20,21},{28,29},{32,33},... | collective-permute-start | bytes 786440 | tf_op jit(solution)/shard_map/ppermute | solution.py:28
  39.2 11.9 %collective-permute-start.7 = (f32[7,32,128]{2,1,0:T(8,128)S(1)}, f32[7,32,128]{2,1,0:T(8,128)S(1)}, u32[]{:S(2)}, u32[]{:S(2)}) collective-permute-start(f32[7,32,128]{2,1,0:T(8,128)S(1)} %collective-permute-done.4), channel_id=1, source_target_pairs={{0,16},{8,24},{4,20},{12,28},{16,32},{24,40},{20,36},{28,44},{32,4... | collective-permute-start | bytes 344072 | tf_op jit(solution)/shard_map/ppermute | solution.py:28
  51.3 15.8 %collective-permute-start.12 = (f32[8,4,32,128]{3,2,1,0:T(8,128)S(1)}, f32[8,4,32,128]{3,2,1,0:T(8,128)S(1)}, u32[]{:S(2)}, u32[]{:S(2)}) collective-permute-start(f32[8,4,32,128]{3,2,1,0:T(8,128)S(1)} %slice.32), channel_id=1, source_target_pairs={{0,3},{8,11},{4,7},{12,15},{16,19},{24,27},{20,23},{28,31},{32,35}... | collective-permute-start | bytes 1572872 | tf_op jit(solution)/shard_map/ppermute | solution.py:28
  51.4 15.7 %collective-permute-start.11 = (f32[8,4,32,128]{3,2,1,0:T(8,128)S(1)}, f32[8,4,32,128]{3,2,1,0:T(8,128)S(1)}, u32[]{:S(2)}, u32[]{:S(2)}) collective-permute-start(f32[8,4,32,128]{3,2,1,0:T(8,128)S(1)} %slice.32), channel_id=1, source_target_pairs={{0,1},{8,9},{4,5},{12,13},{16,17},{24,25},{20,21},{28,29},{32,33},... | collective-permute-start | bytes 1572872 | tf_op jit(solution)/shard_map/ppermute | solution.py:28
  55.4 10.5 %collective-permute-start.14 = (f32[8,3,32,128]{3,2,1,0:T(8,128)S(1)}, f32[8,3,32,128]{3,2,1,0:T(8,128)S(1)}, u32[]{:S(2)}, u32[]{:S(2)}) collective-permute-start(f32[8,3,32,128]{3,2,1,0:T(8,128)S(1)} %get-tuple-element.80), channel_id=1, source_target_pairs={{0,192},{8,200},{4,196},{12,204},{16,208},{24,216},{20,212},{28,22... | collective-permute-start | bytes 1179656 | tf_op jit(solution)/shard_map/ppermute | solution.py:28
  55.4 11.7 %collective-permute-start.13 = (f32[8,3,32,128]{3,2,1,0:T(8,128)S(1)}, f32[8,3,32,128]{3,2,1,0:T(8,128)S(1)}, u32[]{:S(2)}, u32[]{:S(2)}) collective-permute-start(f32[8,3,32,128]{3,2,1,0:T(8,128)S(1)} %get-tuple-element.80), channel_id=1, source_target_pairs={{0,64},{8,72},{4,68},{12,76},{16,80},{24,88},{20,84},{28,92},{32,9... | collective-permute-start | bytes 1179656 | tf_op jit(solution)/shard_map/ppermute | solution.py:28
  59.0 67.0 %collective-permute-start.27 = (f32[4,256,512]{2,1,0:T(8,128)}, f32[4,256,512]{2,1,0:T(8,128)}, u32[]{:S(2)}, u32[]{:S(2)}) collective-permute-start(f32[4,256,512]{2,1,0:T(8,128)} %pad_maximum_fusion.refs_2_), channel_id=1, source_target_pairs={{0,8},{8,0},{4,12},{12,4},{16,24},{24,16},{20,28},{28,20},{32,40},... | collective-permute-start | bytes 6291464 | tf_op jit(solution)/shard_map/ppermute | solution.py:28
  67.2 21.2 %collective-permute-start.19 = (f32[16,4,32,128]{3,2,1,0:T(8,128)S(1)}, f32[16,4,32,128]{3,2,1,0:T(8,128)}, u32[]{:S(2)}, u32[]{:S(2)}) collective-permute-start(f32[16,4,32,128]{3,2,1,0:T(8,128)S(1)} %pad_maximum_fusion.1), channel_id=1, source_target_pairs={{0,8},{8,0},{4,12},{12,4},{16,24},{24,16},{20,28},{28,20},{32,40},... | collective-permute-start | bytes 3145736 | tf_op jit(solution)/shard_map/ppermute | solution.py:28
  68.4 15.7 %collective-permute-start.15 = (f32[4,4,32,128]{3,2,1,0:T(8,128)}, f32[4,4,32,128]{3,2,1,0:T(8,128)S(1)}, u32[]{:S(2)}, u32[]{:S(2)}) collective-permute-start(f32[4,4,32,128]{3,2,1,0:T(8,128)} %slice.34), channel_id=1, source_target_pairs={{0,1},{8,9},{4,5},{12,13},{16,17},{24,25},{20,21},{28,29},{32,33},... | collective-permute-start | bytes 786440 | tf_op jit(solution)/shard_map/ppermute | solution.py:28
  74.7 35.8 %collective-permute-start.30 = (f32[16,4,32,128]{3,2,1,0:T(8,128)S(1)}, f32[16,4,32,128]{3,2,1,0:T(8,128)}, u32[]{:S(2)}, u32[]{:S(2)}) collective-permute-start(f32[16,4,32,128]{3,2,1,0:T(8,128)S(1)} %pad_maximum_fusion.1), channel_id=1, source_target_pairs={{0,192},{8,200},{4,196},{12,204},{16,208},{24,216},{20,212},{28,22... | collective-permute-start | bytes 3145736 | tf_op jit(solution)/shard_map/ppermute | solution.py:28
  79.4 82.8 %all-to-all-start.1 = ((f32[32,80,128]{2,1,0:T(8,128)}), f32[32,80,128]{2,1,0:T(8,128)}, u32[]{:S(2)}, u32[]{:S(2)}) async-start(f32[32,80,128]{2,1,0:T(8,128)} %param.3), calls=%async_computation.1 | async-start | bytes 2621440 | tf_op jit(solution)/shard_map/all_to_all | solution.py:63
  84.2 41.0 %collective-permute-start.24 = (f32[16,4,32,128]{3,2,1,0:T(8,128)S(1)}, f32[16,4,32,128]{3,2,1,0:T(8,128)S(1)}, u32[]{:S(2)}, u32[]{:S(2)}) collective-permute-start(f32[16,4,32,128]{3,2,1,0:T(8,128)S(1)} %pad_maximum_fusion.1), channel_id=1, source_target_pairs={{0,64},{8,72},{4,68},{12,76},{16,80},{24,88},{20,84},{28,92},{32,9... | collective-permute-start | bytes 3145736 | tf_op jit(solution)/shard_map/ppermute | solution.py:28
  89.9 59.5 %collective-permute-start.22 = (f32[32,3,32,128]{3,2,1,0:T(8,128)}, f32[32,3,32,128]{3,2,1,0:T(8,128)}, u32[]{:S(2)}, u32[]{:S(2)}) collective-permute-start(f32[32,3,32,128]{3,2,1,0:T(8,128)} %constant_dynamic-update-slice_fusion.10), channel_id=1, source_target_pairs={{0,3},{8,11},{4,7},{12,15},{16,19},{24,27},{20,23},{28,31},{32,35}... | collective-permute-start | bytes 4718600 | tf_op jit(solution)/shard_map/ppermute | solution.py:28
  90.8 56.4 %collective-permute-start.29 = (f32[16,4,32,128]{3,2,1,0:T(8,128)S(1)}, f32[16,4,32,128]{3,2,1,0:T(8,128)}, u32[]{:S(2)}, u32[]{:S(2)}) collective-permute-start(f32[16,4,32,128]{3,2,1,0:T(8,128)S(1)} %constant_dynamic-update-slice_fusion.7), channel_id=1, source_target_pairs={{0,64},{8,72},{4,68},{12,76},{16,80},{24,88},{20,84},{28,92},{32,9... | collective-permute-start | bytes 3145736 | tf_op jit(solution)/shard_map/ppermute | solution.py:28
  110.5 53.0 %collective-permute-start.23 = (f32[4,256,512]{2,1,0:T(8,128)}, f32[4,256,512]{2,1,0:T(8,128)}, u32[]{:S(2)}, u32[]{:S(2)}) collective-permute-start(f32[4,256,512]{2,1,0:T(8,128)} %pad_maximum_fusion.refs_2_), channel_id=1, source_target_pairs={{0,4},{1,5},{2,6},{3,7},{4,0},{5,1},{6,2},{7,3},{8,12},{9,13},{10,... | collective-permute-start | bytes 6291464 | tf_op jit(solution)/shard_map/ppermute | solution.py:64
  125.2 24.2 %collective-permute-start.20 = (f32[16,4,32,128]{3,2,1,0:T(8,128)S(1)}, f32[16,4,32,128]{3,2,1,0:T(8,128)S(1)}, u32[]{:S(2)}, u32[]{:S(2)}) collective-permute-start(f32[16,4,32,128]{3,2,1,0:T(8,128)S(1)} %constant_dynamic-update-slice_fusion.7), channel_id=1, source_target_pairs={{0,192},{8,200},{4,196},{12,204},{16,208},{24,216},{20,212},{28,22... | collective-permute-start | bytes 3145736 | tf_op jit(solution)/shard_map/ppermute | solution.py:28
  126.0 36.2 %collective-permute-start.21 = (f32[32,3,32,128]{3,2,1,0:T(8,128)}, f32[32,3,32,128]{3,2,1,0:T(8,128)}, u32[]{:S(2)}, u32[]{:S(2)}) collective-permute-start(f32[32,3,32,128]{3,2,1,0:T(8,128)} %constant_dynamic-update-slice_fusion.10), channel_id=1, source_target_pairs={{0,1},{8,9},{4,5},{12,13},{16,17},{24,25},{20,21},{28,29},{32,33},... | collective-permute-start | bytes 4718600 | tf_op jit(solution)/shard_map/ppermute | solution.py:28
  147.2 18.9 %collective-permute-start.26 = (f32[32,3,32,128]{3,2,1,0:T(8,128)}, f32[32,3,32,128]{3,2,1,0:T(8,128)}, u32[]{:S(2)}, u32[]{:S(2)}) collective-permute-start(f32[32,3,32,128]{3,2,1,0:T(8,128)} %constant_dynamic-update-slice_fusion.10), channel_id=1, source_target_pairs={{0,8},{8,0},{4,12},{12,4},{16,24},{24,16},{20,28},{28,20},{32,40},... | collective-permute-start | bytes 4718600 | tf_op jit(solution)/shard_map/ppermute | solution.py:28
  149.4 14.2 %collective-permute-start.37 = (f32[16,4,32,128]{3,2,1,0:T(8,128)}, f32[16,4,32,128]{3,2,1,0:T(8,128)}, u32[]{:S(2)}, u32[]{:S(2)}) collective-permute-start(f32[16,4,32,128]{3,2,1,0:T(8,128)} %collective-permute-done.30), channel_id=1, source_target_pairs={{0,8},{8,0},{4,12},{12,4},{16,24},{24,16},{20,28},{28,20},{32,40},... | collective-permute-start | bytes 3145736 | tf_op jit(solution)/shard_map/ppermute | solution.py:28
  150.4 13.8 %collective-permute-start.25 = (f32[16,4,32,128]{3,2,1,0:T(8,128)S(1)}, f32[16,4,32,128]{3,2,1,0:T(8,128)}, u32[]{:S(2)}, u32[]{:S(2)}) collective-permute-start(f32[16,4,32,128]{3,2,1,0:T(8,128)S(1)} %constant_dynamic-update-slice_fusion.7), channel_id=1, source_target_pairs={{0,8},{8,0},{4,12},{12,4},{16,24},{24,16},{20,28},{28,20},{32,40},... | collective-permute-start | bytes 3145736 | tf_op jit(solution)/shard_map/ppermute | solution.py:28
  163.5 22.1 %collective-permute-start.34 = (f32[16,3,32,128]{3,2,1,0:T(8,128)S(1)}, f32[16,3,32,128]{3,2,1,0:T(8,128)}, u32[]{:S(2)}, u32[]{:S(2)}) collective-permute-start(f32[16,3,32,128]{3,2,1,0:T(8,128)S(1)} %slice.39), channel_id=1, source_target_pairs={{0,3},{8,11},{4,7},{12,15},{16,19},{24,27},{20,23},{28,31},{32,35}... | collective-permute-start | bytes 2359304 | tf_op jit(solution)/shard_map/ppermute | solution.py:28
  163.6 23.1 %collective-permute-start.38 = (f32[16,4,32,128]{3,2,1,0:T(8,128)}, f32[16,4,32,128]{3,2,1,0:T(8,128)S(1)}, u32[]{:S(2)}, u32[]{:S(2)}) collective-permute-start(f32[16,4,32,128]{3,2,1,0:T(8,128)} %copy-done.11), channel_id=1, source_target_pairs={{0,8},{8,0},{4,12},{12,4},{16,24},{24,16},{20,28},{28,20},{32,40},... | collective-permute-start | bytes 3145736 | tf_op jit(solution)/shard_map/ppermute | solution.py:28
  164.2 25.5 %collective-permute-start.32 = (f32[16,4,32,128]{3,2,1,0:T(8,128)}, f32[16,4,32,128]{3,2,1,0:T(8,128)}, u32[]{:S(2)}, u32[]{:S(2)}) collective-permute-start(f32[16,4,32,128]{3,2,1,0:T(8,128)} %copy-done.11), channel_id=1, source_target_pairs={{0,192},{8,200},{4,196},{12,204},{16,208},{24,216},{20,212},{28,22... | collective-permute-start | bytes 3145736 | tf_op jit(solution)/shard_map/ppermute | solution.py:28
  166.1 20.6 %collective-permute-start.33 = (f32[16,3,32,128]{3,2,1,0:T(8,128)S(1)}, f32[16,3,32,128]{3,2,1,0:T(8,128)}, u32[]{:S(2)}, u32[]{:S(2)}) collective-permute-start(f32[16,3,32,128]{3,2,1,0:T(8,128)S(1)} %slice.38), channel_id=1, source_target_pairs={{0,1},{8,9},{4,5},{12,13},{16,17},{24,25},{20,21},{28,29},{32,33},... | collective-permute-start | bytes 2359304 | tf_op jit(solution)/shard_map/ppermute | solution.py:28
  169.9 43.7 %collective-permute-start.39 = (f32[32,3,32,128]{3,2,1,0:T(8,128)}, f32[32,3,32,128]{3,2,1,0:T(8,128)}, u32[]{:S(2)}, u32[]{:S(2)}) collective-permute-start(f32[32,3,32,128]{3,2,1,0:T(8,128)} %collective-permute-done.21), channel_id=1, source_target_pairs={{0,8},{8,0},{4,12},{12,4},{16,24},{24,16},{20,28},{28,20},{32,40},... | collective-permute-start | bytes 4718600 | tf_op jit(solution)/shard_map/ppermute | solution.py:28
  185.6 28.0 %collective-permute-start.40 = (f32[32,3,32,128]{3,2,1,0:T(8,128)}, f32[32,3,32,128]{3,2,1,0:T(8,128)}, u32[]{:S(2)}, u32[]{:S(2)}) collective-permute-start(f32[32,3,32,128]{3,2,1,0:T(8,128)} %collective-permute-done.22), channel_id=1, source_target_pairs={{0,8},{8,0},{4,12},{12,4},{16,24},{24,16},{20,28},{28,20},{32,40},... | collective-permute-start | bytes 4718600 | tf_op jit(solution)/shard_map/ppermute | solution.py:28
  186.7 26.9 %collective-permute-start.31 = (f32[16,4,32,128]{3,2,1,0:T(8,128)S(1)}, f32[16,4,32,128]{3,2,1,0:T(8,128)}, u32[]{:S(2)}, u32[]{:S(2)}) collective-permute-start(f32[16,4,32,128]{3,2,1,0:T(8,128)S(1)} %copy-done.10), channel_id=1, source_target_pairs={{0,64},{8,72},{4,68},{12,76},{16,80},{24,88},{20,84},{28,92},{32,9... | collective-permute-start | bytes 3145736 | tf_op jit(solution)/shard_map/ppermute | solution.py:28
  189.7 25.1 %collective-permute-start.28 = (f32[4,256,512]{2,1,0:T(8,128)}, f32[4,256,512]{2,1,0:T(8,128)}, u32[]{:S(2)}, u32[]{:S(2)}) collective-permute-start(f32[4,256,512]{2,1,0:T(8,128)} %collective-permute-done.23.refs_3_), channel_id=1, source_target_pairs={{0,8},{8,0},{4,12},{12,4},{16,24},{24,16},{20,28},{28,20},{32,40},... | collective-permute-start | bytes 6291464 | tf_op jit(solution)/shard_map/ppermute | solution.py:28
  (29 other events, 241.5 us)

commit v5 on v4

--- a/solution.py
+++ b/solution.py
@@ -76,11 +76,12 @@
     swapped = [swapped_head, *swap([tail, whole, quarter])]
     head_up, swapped = lax.optimization_barrier((head_up, swapped))
     far_up = shift(head_up, dx=1)
-    tail_down, late_up, late_down, rows = lax.optimization_barrier((tail_down, late_up, late_down, rows))
+    swapped_up = shift(head_up, core=1)
+    late_up, late_down, rows, swapped_up = lax.optimization_barrier((late_up, late_down, rows, swapped_up))
     far_down = shift(tail_down, dx=-1)
     late_far = [shift(late_up[:16], dy=1), shift(late_down[16:], dy=-1)]
     sides = [head_up, tail_up, head_down, tail_down, late_up, late_down]
-    swapped_sides = swap(sides)
+    swapped_sides = [swapped_up, *swap(sides[1:])]
     far, swapped_sides = lax.optimization_barrier(([far_up, far_down, *late_far], swapped_sides))
     swapped_far = swap([*far, neighbour])
     diagonals = [quarter, neighbour, swapped[3], swapped_far[4]]

time: 275 us -> 260 us (0.945)
  waiting for transfers between devices: 146 us -> 138 us
  blocking collectives: 25.6 us -> 21.9 us
  local copies, waits for them, and re-layouts: 13 us -> 9.89 us
    ppermute x44, waiting for transfers between devices: 136 us -> 106 us  [shift(): return lax.ppermute(value, ALL, pairs)]
    ppermute x1, waiting for transfers between devices: 0.01 us -> 18.1 us  [gather(): lax.ppermute(quarter, 'aux', [(a, (a + 4) % 8) for a in range(8)])]
    all_to_all x1, waiting for transfers between devices: 0.01 us -> 4.08 us  [gather(): rows = lax.all_to_all(integrals, 'pair', 0, 0, tiled=True)]
    all_to_all x1, blocking collectives: 25.6 us -> 21.9 us  [local(): result = lax.all_to_all(solved, 'aux', 0, 0, tiled=True)]
    unnamed x48 -> x25, local copies, waits for them, and re-layouts: 8.17 us -> 5.77 us
where the time goes in v5:
time: 260 us; the launch traced here: 258 us
  waiting for transfers between devices  138 us (53%)
  starting transfers between devices  59.4 us (23%)
  Pallas kernels  25.1 us (10%)
  blocking collectives  21.9 us (8%)
  local copies, waits for them, and re-layouts  9.89 us (4%)
  other arithmetic  3.54 us (1%)
    ppermute x44, waiting for transfers between devices, shift(): return lax.ppermute(value, ALL, pairs)  106 us
    ppermute x44, starting transfers between devices, shift(): return lax.ppermute(value, ALL, pairs)  41.5 us
    pallas_call x1, Pallas kernels, solve(): pl.pallas_call(kernel, out_shape=jax.ShapeDtypeStruct((PANELS, ROWS, PANE...  25.1 us
    all_to_all x1, blocking collectives, local(): result = lax.all_to_all(solved, 'aux', 0, 0, tiled=True)  21.9 us
    ppermute x1, waiting for transfers between devices, gather(): lax.ppermute(quarter, 'aux', [(a, (a + 4) % 8) for a in range(8)])  18.1 us
    all_to_all x1, starting transfers between devices, spread(): lax.all_to_all(halves, ALL, 0, 0, axis_index_groups=groups, tiled=True)  10.9 us
    all_to_all x1, waiting for transfers between devices, spread(): lax.all_to_all(halves, ALL, 0, 0, axis_index_groups=groups, tiled=True)  9.65 us
    all_to_all x1, starting transfers between devices, gather(): rows = lax.all_to_all(integrals, 'pair', 0, 0, tiled=True)  5.87 us
  transfers between devices with their start and end apart: 47, of which 22 were waited for; matrix products, arithmetic and copies ran while one was open for 4% of the time, Pallas kernels for 0%

profile of v5, /device:TPU:56, one launch (start us, length us, event | category | flops | bytes accessed | tf_op | source)
XLA Modules:
  0.0 257.7 jit_solution(504318211000685923)
XLA Ops:
  2.1 2.5 collective-permute-start
  4.6 1.8 reverse_select_fusion
  6.4 10.9 %all-to-all-start = ((f32[16,32,128]{2,1,0:T(8,128)}), f32[16,32,128]{2,1,0:T(8,128)S(1)}, u32[]{:S(2)}, u32[]{:S(2)}) async-start(f32[16,32,128]{2,1,0:T(8,128)} %bitcast.5), calls=%async_computation | async-start | bytes 524288 | tf_op jit(solution)/shard_map/all_to_all | solution.py:43
  17.3 9.6 %all-to-all-done = f32[16,32,128]{2,1,0:T(8,128)S(1)} async-done(((f32[16,32,128]{2,1,0:T(8,128)}), f32[16,32,128]{2,1,0:T(8,128)S(1)}, u32[]{:S(2)}, u32[]{:S(2)}) %all-to-all-start) | async-done | bytes 262176 | tf_op jit(solution)/shard_map/all_to_all | solution.py:43
  30.0 2.0 collective-permute-start.2
  34.5 1.9 collective-permute-start.9
  36.4 1.8 collective-permute-done.4
  39.2 2.2 collective-permute-start.7
  41.4 3.7 %collective-permute-start.6 = (f32[7,32,128]{2,1,0:T(8,128)S(1)}, f32[7,32,128]{2,1,0:T(8,128)S(1)}, u32[]{:S(2)}, u32[]{:S(2)}) collective-permute-start(f32[7,32,128]{2,1,0:T(8,128)S(1)} %collective-permute-done.4), channel_id=1, source_target_pairs={{0,4},{8,12},{4,16},{12,24},{16,20},{24,28},{20,32},{28,40},{32,36... | collective-permute-start | bytes 344072 | tf_op jit(solution)/shard_map/ppermute | solution.py:28
  45.1 6.0 %collective-permute-done.6 = f32[7,32,128]{2,1,0:T(8,128)S(1)} collective-permute-done((f32[7,32,128]{2,1,0:T(8,128)S(1)}, f32[7,32,128]{2,1,0:T(8,128)S(1)}, u32[]{:S(2)}, u32[]{:S(2)}) %collective-permute-start.6) | collective-permute-done | bytes 114720 | tf_op jit(solution)/shard_map/ppermute | solution.py:28
  51.4 3.2 %collective-permute-start.11 = (f32[8,4,32,128]{3,2,1,0:T(8,128)S(1)}, f32[8,4,32,128]{3,2,1,0:T(8,128)S(1)}, u32[]{:S(2)}, u32[]{:S(2)}) collective-permute-start(f32[8,4,32,128]{3,2,1,0:T(8,128)S(1)} %slice.33), channel_id=1, source_target_pairs={{0,1},{8,9},{4,5},{12,13},{16,17},{24,25},{20,21},{28,29},{32,33},... | collective-permute-start | bytes 1572872 | tf_op jit(solution)/shard_map/ppermute | solution.py:28
  55.4 2.0 collective-permute-start.13
  57.4 8.5 %collective-permute-done.14 = f32[8,3,32,128]{3,2,1,0:T(8,128)S(1)} collective-permute-done((f32[8,3,32,128]{3,2,1,0:T(8,128)S(1)}, f32[8,3,32,128]{3,2,1,0:T(8,128)S(1)}, u32[]{:S(2)}, u32[]{:S(2)}) %collective-permute-start.14) | collective-permute-done | bytes 393248 | tf_op jit(solution)/shard_map/ppermute | solution.py:28
  67.8 1.7 collective-permute-start.17
  72.6 2.7 %collective-permute-done.18 = f32[4,3,32,128]{3,2,1,0:T(8,128)S(1)} collective-permute-done((f32[4,3,32,128]{3,2,1,0:T(8,128)S(1)}, f32[4,3,32,128]{3,2,1,0:T(8,128)S(1)}, u32[]{:S(2)}, u32[]{:S(2)}) %collective-permute-start.18) | collective-permute-done | bytes 196640 | tf_op jit(solution)/shard_map/ppermute | solution.py:28
  76.1 2.4 collective-permute-start.15
  80.1 3.8 %collective-permute-done.16 = f32[4,4,32,128]{3,2,1,0:T(8,128)S(1)} collective-permute-done((f32[4,4,32,128]{3,2,1,0:T(8,128)S(1)}, f32[4,4,32,128]{3,2,1,0:T(8,128)S(1)}, u32[]{:S(2)}, u32[]{:S(2)}) %collective-permute-start.16) | collective-permute-done | bytes 262176 | tf_op jit(solution)/shard_map/ppermute | solution.py:28
  87.0 10.2 %collective-permute-done.30 = f32[16,4,32,128]{3,2,1,0:T(8,128)S(1)} collective-permute-done((f32[16,4,32,128]{3,2,1,0:T(8,128)S(1)}, f32[16,4,32,128]{3,2,1,0:T(8,128)S(1)}, u32[]{:S(2)}, u32[]{:S(2)}) %collective-permute-start.30) | collective-permute-done | bytes 1048608 | tf_op jit(solution)/shard_map/ppermute | solution.py:28
  98.2 5.9 %all-to-all-start.1 = ((f32[32,80,128]{2,1,0:T(8,128)}), f32[32,80,128]{2,1,0:T(8,128)}, u32[]{:S(2)}, u32[]{:S(2)}) async-start(f32[32,80,128]{2,1,0:T(8,128)} %param.3), calls=%async_computation.1 | async-start | bytes 2621440 | tf_op jit(solution)/shard_map/all_to_all | solution.py:63
  104.1 13.1 %collective-permute-done.22 = f32[16,4,32,128]{3,2,1,0:T(8,128)} collective-permute-done((f32[16,4,32,128]{3,2,1,0:T(8,128)S(1)}, f32[16,4,32,128]{3,2,1,0:T(8,128)}, u32[]{:S(2)}, u32[]{:S(2)}) %collective-permute-start.22) | collective-permute-done | bytes 1048608 | tf_op jit(solution)/shard_map/ppermute | solution.py:28
  117.2 2.0 collective-permute-start.29
  119.2 3.7 %collective-permute-start.20 = (f32[32,3,32,128]{3,2,1,0:T(8,128)}, f32[32,3,32,128]{3,2,1,0:T(8,128)}, u32[]{:S(2)}, u32[]{:S(2)}) collective-permute-start(f32[32,3,32,128]{3,2,1,0:T(8,128)} %constant_dynamic-update-slice_fusion.7), channel_id=1, source_target_pairs={{0,1},{8,9},{4,5},{12,13},{16,17},{24,25},{20,21},{28,29},{32,33},... | collective-permute-start | bytes 4718600 | tf_op jit(solution)/shard_map/ppermute | solution.py:28
  122.9 18.1 %collective-permute-done.27.refs_3_ = f32[4,256,512]{2,1,0:T(8,128)} collective-permute-done((f32[4,256,512]{2,1,0:T(8,128)}, f32[4,256,512]{2,1,0:T(8,128)}, u32[]{:S(2)}, u32[]{:S(2)}) %collective-permute-start.27) | collective-permute-done | bytes 2097184 | tf_op jit(solution)/shard_map/ppermute | solution.py:64
  141.5 3.5 %collective-permute-done.29 = f32[16,4,32,128]{3,2,1,0:T(8,128)} collective-permute-done((f32[16,4,32,128]{3,2,1,0:T(8,128)S(1)}, f32[16,4,32,128]{3,2,1,0:T(8,128)}, u32[]{:S(2)}, u32[]{:S(2)}) %collective-permute-start.29) | collective-permute-done | bytes 1048608 | tf_op jit(solution)/shard_map/ppermute | solution.py:28
  145.0 9.1 %collective-permute-done.21 = f32[32,3,32,128]{3,2,1,0:T(8,128)} collective-permute-done((f32[32,3,32,128]{3,2,1,0:T(8,128)}, f32[32,3,32,128]{3,2,1,0:T(8,128)}, u32[]{:S(2)}, u32[]{:S(2)}) %collective-permute-start.21) | collective-permute-done | bytes 1572896 | tf_op jit(solution)/shard_map/ppermute | solution.py:28
  156.3 4.1 %all-to-all-done.1.refs_1_ = f32[32,80,128]{2,1,0:T(8,128)} async-done(((f32[32,80,128]{2,1,0:T(8,128)}), f32[32,80,128]{2,1,0:T(8,128)}, u32[]{:S(2)}, u32[]{:S(2)}) %all-to-all-start.1) | async-done | bytes 1310752 | tf_op jit(solution)/shard_map/all_to_all | solution.py:63
  161.7 15.9 %collective-permute-done.33 = f32[16,4,32,128]{3,2,1,0:T(8,128)} collective-permute-done((f32[16,4,32,128]{3,2,1,0:T(8,128)}, f32[16,4,32,128]{3,2,1,0:T(8,128)}, u32[]{:S(2)}, u32[]{:S(2)}) %collective-permute-start.33) | collective-permute-done | bytes 1048608 | tf_op jit(solution)/shard_map/ppermute | solution.py:28
  180.0 3.6 %collective-permute-done.32 = f32[16,4,32,128]{3,2,1,0:T(8,128)} collective-permute-done((f32[16,4,32,128]{3,2,1,0:T(8,128)}, f32[16,4,32,128]{3,2,1,0:T(8,128)}, u32[]{:S(2)}, u32[]{:S(2)}) %collective-permute-start.32) | collective-permute-done | bytes 1048608 | tf_op jit(solution)/shard_map/ppermute | solution.py:28
  185.0 16.2 %collective-permute-done.35 = f32[16,3,32,128]{3,2,1,0:T(8,128)} collective-permute-done((f32[16,3,32,128]{3,2,1,0:T(8,128)S(1)}, f32[16,3,32,128]{3,2,1,0:T(8,128)}, u32[]{:S(2)}, u32[]{:S(2)}) %collective-permute-start.35) | collective-permute-done | bytes 786464 | tf_op jit(solution)/shard_map/ppermute | solution.py:28
  203.9 4.5 %collective-permute-done.43 = f32[16,3,32,128]{3,2,1,0:T(8,128)} collective-permute-done((f32[16,3,32,128]{3,2,1,0:T(8,128)}, f32[16,3,32,128]{3,2,1,0:T(8,128)}, u32[]{:S(2)}, u32[]{:S(2)}) %collective-permute-start.43) | collective-permute-done | bytes 786464 | tf_op jit(solution)/shard_map/ppermute | solution.py:28
  209.6 25.1 %shard_map.37 = f32[8,80,512]{2,1,0:T(8,128)} custom-call(s32[4]{0:T(128)S(1)} %pad_add_fusion.refs_0_, f32[32,80,128]{2,1,0:T(8,128)} %all-to-all-done.1.refs_1_, f32[4,256,512]{2,1,0:T(8,128)} %pad_maximum_fusion.refs_2_, f32[4,256,512]{2,1,0:T(8,128)} %collective-permute-done.27.refs_3_, f32[4,256,512]{2,1,0:T(8,128)} %collective-permute-done.25.refs_4_, ...), custom_call_target="tpu_custom_call" | custom-call | flops 16000000000 | bytes 40000000 | tf_op jit(solution)/shard_map/pallas_call | solution.py:198
  234.7 21.9 %all_to_all.15 = f32[8,80,512]{2,1,0:T(8,128)S(1)} all-to-all(f32[8,80,512]{2,1,0:T(8,128)} %shard_map.37), channel_id=1, replica_groups=mesh['pair'=32,'aux'=8] {'aux'}, dimensions={0} | all-to-all | bytes 2621440 | tf_op jit(solution)/shard_map/all_to_all | solution.py:230
  (110 shorter events, 33.8 us)
Async XLA Ops:
  1.3 25.7 %collective-permute-start.1 = (f32[256,512]{1,0:T(8,128)S(1)}, f32[256,512]{1,0:T(8,128)S(1)}, u32[]{:S(2)}, u32[]{:S(2)}) collective-permute-start(f32[256,512]{1,0:T(8,128)S(1)} %fusion.1), channel_id=1, source_target_pairs={{0,3},{8,11},{4,7},{12,15},{16,19},{24,27},{20,23},{28,31},{32,35}... | collective-permute-start | bytes 1572872 | tf_op jit(solution)/shard_map/ppermute | solution.py:28
  2.1 24.8 %collective-permute-start = (f32[256,512]{1,0:T(8,128)S(1)}, f32[256,512]{1,0:T(8,128)S(1)}, u32[]{:S(2)}, u32[]{:S(2)}) collective-permute-start(f32[256,512]{1,0:T(8,128)S(1)} %fusion.1), channel_id=1, source_target_pairs={{0,1},{8,9},{4,5},{12,13},{16,17},{24,25},{20,21},{28,29},{32,33},... | collective-permute-start | bytes 1572872 | tf_op jit(solution)/shard_map/ppermute | solution.py:28
  6.4 20.5 %all-to-all-start = ((f32[16,32,128]{2,1,0:T(8,128)}), f32[16,32,128]{2,1,0:T(8,128)S(1)}, u32[]{:S(2)}, u32[]{:S(2)}) async-start(f32[16,32,128]{2,1,0:T(8,128)} %bitcast.5), calls=%async_computation | async-start | bytes 524288 | tf_op jit(solution)/shard_map/all_to_all | solution.py:43
  32.1 19.0 %collective-permute-start.10 = (f32[128,512]{1,0:T(8,128)S(1)}, f32[128,512]{1,0:T(8,128)S(1)}, u32[]{:S(2)}, u32[]{:S(2)}) collective-permute-start(f32[128,512]{1,0:T(8,128)S(1)} %slice.31), channel_id=1, source_target_pairs={{0,3},{8,11},{4,7},{12,15},{16,19},{24,27},{20,23},{28,31},{32,35}... | collective-permute-start | bytes 786440 | tf_op jit(solution)/shard_map/ppermute | solution.py:28
  34.5 16.7 %collective-permute-start.9 = (f32[128,512]{1,0:T(8,128)S(1)}, f32[128,512]{1,0:T(8,128)S(1)}, u32[]{:S(2)}, u32[]{:S(2)}) collective-permute-start(f32[128,512]{1,0:T(8,128)S(1)} %slice.30), channel_id=1, source_target_pairs={{0,1},{8,9},{4,5},{12,13},{16,17},{24,25},{20,21},{28,29},{32,33},... | collective-permute-start | bytes 786440 | tf_op jit(solution)/shard_map/ppermute | solution.py:28
  39.2 11.9 %collective-permute-start.7 = (f32[7,32,128]{2,1,0:T(8,128)S(1)}, f32[7,32,128]{2,1,0:T(8,128)S(1)}, u32[]{:S(2)}, u32[]{:S(2)}) collective-permute-start(f32[7,32,128]{2,1,0:T(8,128)S(1)} %collective-permute-done.4), channel_id=1, source_target_pairs={{0,16},{8,24},{4,20},{12,28},{16,32},{24,40},{20,36},{28,44},{32,4... | collective-permute-start | bytes 344072 | tf_op jit(solution)/shard_map/ppermute | solution.py:28
  51.3 15.8 %collective-permute-start.12 = (f32[8,4,32,128]{3,2,1,0:T(8,128)S(1)}, f32[8,4,32,128]{3,2,1,0:T(8,128)S(1)}, u32[]{:S(2)}, u32[]{:S(2)}) collective-permute-start(f32[8,4,32,128]{3,2,1,0:T(8,128)S(1)} %slice.33), channel_id=1, source_target_pairs={{0,3},{8,11},{4,7},{12,15},{16,19},{24,27},{20,23},{28,31},{32,35}... | collective-permute-start | bytes 1572872 | tf_op jit(solution)/shard_map/ppermute | solution.py:28
  51.4 15.7 %collective-permute-start.11 = (f32[8,4,32,128]{3,2,1,0:T(8,128)S(1)}, f32[8,4,32,128]{3,2,1,0:T(8,128)S(1)}, u32[]{:S(2)}, u32[]{:S(2)}) collective-permute-start(f32[8,4,32,128]{3,2,1,0:T(8,128)S(1)} %slice.33), channel_id=1, source_target_pairs={{0,1},{8,9},{4,5},{12,13},{16,17},{24,25},{20,21},{28,29},{32,33},... | collective-permute-start | bytes 1572872 | tf_op jit(solution)/shard_map/ppermute | solution.py:28
  55.4 11.7 %collective-permute-start.13 = (f32[8,3,32,128]{3,2,1,0:T(8,128)S(1)}, f32[8,3,32,128]{3,2,1,0:T(8,128)S(1)}, u32[]{:S(2)}, u32[]{:S(2)}) collective-permute-start(f32[8,3,32,128]{3,2,1,0:T(8,128)S(1)} %get-tuple-element.79), channel_id=1, source_target_pairs={{0,64},{8,72},{4,68},{12,76},{16,80},{24,88},{20,84},{28,92},{32,9... | collective-permute-start | bytes 1179656 | tf_op jit(solution)/shard_map/ppermute | solution.py:28
  67.2 17.7 %collective-permute-start.19 = (f32[16,4,32,128]{3,2,1,0:T(8,128)S(1)}, f32[16,4,32,128]{3,2,1,0:T(8,128)S(1)}, u32[]{:S(2)}, u32[]{:S(2)}) collective-permute-start(f32[16,4,32,128]{3,2,1,0:T(8,128)S(1)} %pad_maximum_fusion.1), channel_id=1, source_target_pairs={{0,8},{8,0},{4,12},{12,4},{16,24},{24,16},{20,28},{28,20},{32,40},... | collective-permute-start | bytes 3145736 | tf_op jit(solution)/shard_map/ppermute | solution.py:28
  71.0 46.2 %collective-permute-start.25 = (f32[4,256,512]{2,1,0:T(8,128)}, f32[4,256,512]{2,1,0:T(8,128)}, u32[]{:S(2)}, u32[]{:S(2)}) collective-permute-start(f32[4,256,512]{2,1,0:T(8,128)} %pad_maximum_fusion.refs_2_), channel_id=1, source_target_pairs={{0,8},{8,0},{4,12},{12,4},{16,24},{24,16},{20,28},{28,20},{32,40},... | collective-permute-start | bytes 6291464 | tf_op jit(solution)/shard_map/ppermute | solution.py:28
  71.0 26.2 %collective-permute-start.30 = (f32[16,4,32,128]{3,2,1,0:T(8,128)S(1)}, f32[16,4,32,128]{3,2,1,0:T(8,128)S(1)}, u32[]{:S(2)}, u32[]{:S(2)}) collective-permute-start(f32[16,4,32,128]{3,2,1,0:T(8,128)S(1)} %pad_maximum_fusion.1), channel_id=1, source_target_pairs={{0,192},{8,200},{4,196},{12,204},{16,208},{24,216},{20,212},{28,22... | collective-permute-start | bytes 3145736 | tf_op jit(solution)/shard_map/ppermute | solution.py:28
  83.8 57.2 %collective-permute-start.27 = (f32[4,256,512]{2,1,0:T(8,128)}, f32[4,256,512]{2,1,0:T(8,128)}, u32[]{:S(2)}, u32[]{:S(2)}) collective-permute-start(f32[4,256,512]{2,1,0:T(8,128)} %pad_maximum_fusion.refs_2_), channel_id=1, source_target_pairs={{0,4},{1,5},{2,6},{3,7},{4,0},{5,1},{6,2},{7,3},{8,12},{9,13},{10,... | collective-permute-start | bytes 6291464 | tf_op jit(solution)/shard_map/ppermute | solution.py:64
  86.3 32.9 %collective-permute-start.24 = (f32[32,3,32,128]{3,2,1,0:T(8,128)}, f32[32,3,32,128]{3,2,1,0:T(8,128)}, u32[]{:S(2)}, u32[]{:S(2)}) collective-permute-start(f32[32,3,32,128]{3,2,1,0:T(8,128)} %constant_dynamic-update-slice_fusion.7), channel_id=1, source_target_pairs={{0,8},{8,0},{4,12},{12,4},{16,24},{24,16},{20,28},{28,20},{32,40},... | collective-permute-start | bytes 4718600 | tf_op jit(solution)/shard_map/ppermute | solution.py:28
  86.4 30.8 %collective-permute-start.22 = (f32[16,4,32,128]{3,2,1,0:T(8,128)S(1)}, f32[16,4,32,128]{3,2,1,0:T(8,128)}, u32[]{:S(2)}, u32[]{:S(2)}) collective-permute-start(f32[16,4,32,128]{3,2,1,0:T(8,128)S(1)} %pad_maximum_fusion.1), channel_id=1, source_target_pairs={{0,64},{8,72},{4,68},{12,76},{16,80},{24,88},{20,84},{28,92},{32,9... | collective-permute-start | bytes 3145736 | tf_op jit(solution)/shard_map/ppermute | solution.py:28
  98.2 21.0 %collective-permute-start.23 = (f32[16,4,32,128]{3,2,1,0:T(8,128)S(1)}, f32[16,4,32,128]{3,2,1,0:T(8,128)}, u32[]{:S(2)}, u32[]{:S(2)}) collective-permute-start(f32[16,4,32,128]{3,2,1,0:T(8,128)S(1)} %constant_dynamic-update-slice_fusion.12), channel_id=1, source_target_pairs={{0,8},{8,0},{4,12},{12,4},{16,24},{24,16},{20,28},{28,20},{32,40},... | collective-permute-start | bytes 3145736 | tf_op jit(solution)/shard_map/ppermute | solution.py:28
  98.2 62.1 %all-to-all-start.1 = ((f32[32,80,128]{2,1,0:T(8,128)}), f32[32,80,128]{2,1,0:T(8,128)}, u32[]{:S(2)}, u32[]{:S(2)}) async-start(f32[32,80,128]{2,1,0:T(8,128)} %param.3), calls=%async_computation.1 | async-start | bytes 2621440 | tf_op jit(solution)/shard_map/all_to_all | solution.py:63
  117.2 23.8 %collective-permute-start.31 = (f32[16,4,32,128]{3,2,1,0:T(8,128)S(1)}, f32[16,4,32,128]{3,2,1,0:T(8,128)}, u32[]{:S(2)}, u32[]{:S(2)}) collective-permute-start(f32[16,4,32,128]{3,2,1,0:T(8,128)S(1)} %constant_dynamic-update-slice_fusion.12), channel_id=1, source_target_pairs={{0,192},{8,200},{4,196},{12,204},{16,208},{24,216},{20,212},{28,22... | collective-permute-start | bytes 3145736 | tf_op jit(solution)/shard_map/ppermute | solution.py:28
  117.2 27.8 %collective-permute-start.29 = (f32[16,4,32,128]{3,2,1,0:T(8,128)S(1)}, f32[16,4,32,128]{3,2,1,0:T(8,128)}, u32[]{:S(2)}, u32[]{:S(2)}) collective-permute-start(f32[16,4,32,128]{3,2,1,0:T(8,128)S(1)} %constant_dynamic-update-slice_fusion.12), channel_id=1, source_target_pairs={{0,64},{8,72},{4,68},{12,76},{16,80},{24,88},{20,84},{28,92},{32,9... | collective-permute-start | bytes 3145736 | tf_op jit(solution)/shard_map/ppermute | solution.py:28
  119.2 34.9 %collective-permute-start.21 = (f32[32,3,32,128]{3,2,1,0:T(8,128)}, f32[32,3,32,128]{3,2,1,0:T(8,128)}, u32[]{:S(2)}, u32[]{:S(2)}) collective-permute-start(f32[32,3,32,128]{3,2,1,0:T(8,128)} %constant_dynamic-update-slice_fusion.7), channel_id=1, source_target_pairs={{0,3},{8,11},{4,7},{12,15},{16,19},{24,27},{20,23},{28,31},{32,35}... | collective-permute-start | bytes 4718600 | tf_op jit(solution)/shard_map/ppermute | solution.py:28
  119.2 36.4 %collective-permute-start.20 = (f32[32,3,32,128]{3,2,1,0:T(8,128)}, f32[32,3,32,128]{3,2,1,0:T(8,128)}, u32[]{:S(2)}, u32[]{:S(2)}) collective-permute-start(f32[32,3,32,128]{3,2,1,0:T(8,128)} %constant_dynamic-update-slice_fusion.7), channel_id=1, source_target_pairs={{0,1},{8,9},{4,5},{12,13},{16,17},{24,25},{20,21},{28,29},{32,33},... | collective-permute-start | bytes 4718600 | tf_op jit(solution)/shard_map/ppermute | solution.py:28
  141.0 14.7 %collective-permute-start.26 = (f32[16,4,32,128]{3,2,1,0:T(8,128)}, f32[16,4,32,128]{3,2,1,0:T(8,128)}, u32[]{:S(2)}, u32[]{:S(2)}) collective-permute-start(f32[16,4,32,128]{3,2,1,0:T(8,128)} %collective-permute-done.22), channel_id=1, source_target_pairs={{0,8},{8,0},{4,12},{12,4},{16,24},{24,16},{20,28},{28,20},{32,40},... | collective-permute-start | bytes 3145736 | tf_op jit(solution)/shard_map/ppermute | solution.py:28
  141.0 19.4 %collective-permute-start.37 = (f32[16,4,32,128]{3,2,1,0:T(8,128)}, f32[16,4,32,128]{3,2,1,0:T(8,128)}, u32[]{:S(2)}, u32[]{:S(2)}) collective-permute-start(f32[16,4,32,128]{3,2,1,0:T(8,128)} %copy-done.2), channel_id=1, source_target_pairs={{0,8},{8,0},{4,12},{12,4},{16,24},{24,16},{20,28},{28,20},{32,40},... | collective-permute-start | bytes 3145736 | tf_op jit(solution)/shard_map/ppermute | solution.py:28
  145.0 16.5 %collective-permute-start.38 = (f32[16,4,32,128]{3,2,1,0:T(8,128)}, f32[16,4,32,128]{3,2,1,0:T(8,128)}, u32[]{:S(2)}, u32[]{:S(2)}) collective-permute-start(f32[16,4,32,128]{3,2,1,0:T(8,128)} %collective-permute-done.31), channel_id=1, source_target_pairs={{0,8},{8,0},{4,12},{12,4},{16,24},{24,16},{20,28},{28,20},{32,40},... | collective-permute-start | bytes 3145736 | tf_op jit(solution)/shard_map/ppermute | solution.py:28
  154.1 23.4 %collective-permute-start.33 = (f32[16,4,32,128]{3,2,1,0:T(8,128)}, f32[16,4,32,128]{3,2,1,0:T(8,128)}, u32[]{:S(2)}, u32[]{:S(2)}) collective-permute-start(f32[16,4,32,128]{3,2,1,0:T(8,128)} %collective-permute-done.31), channel_id=1, source_target_pairs={{0,192},{8,200},{4,196},{12,204},{16,208},{24,216},{20,212},{28,22... | collective-permute-start | bytes 3145736 | tf_op jit(solution)/shard_map/ppermute | solution.py:28
  155.6 24.3 %collective-permute-start.36 = (f32[16,4,32,128]{3,2,1,0:T(8,128)}, f32[16,4,32,128]{3,2,1,0:T(8,128)}, u32[]{:S(2)}, u32[]{:S(2)}) collective-permute-start(f32[16,4,32,128]{3,2,1,0:T(8,128)} %collective-permute-done.29), channel_id=1, source_target_pairs={{0,8},{8,0},{4,12},{12,4},{16,24},{24,16},{20,28},{28,20},{32,40},... | collective-permute-start | bytes 3145736 | tf_op jit(solution)/shard_map/ppermute | solution.py:28
  155.7 28.0 %collective-permute-start.32 = (f32[16,4,32,128]{3,2,1,0:T(8,128)}, f32[16,4,32,128]{3,2,1,0:T(8,128)}, u32[]{:S(2)}, u32[]{:S(2)}) collective-permute-start(f32[16,4,32,128]{3,2,1,0:T(8,128)} %collective-permute-done.22), channel_id=1, source_target_pairs={{0,64},{8,72},{4,68},{12,76},{16,80},{24,88},{20,84},{28,92},{32,9... | collective-permute-start | bytes 3145736 | tf_op jit(solution)/shard_map/ppermute | solution.py:28
  160.3 42.5 %collective-permute-start.39 = (f32[32,3,32,128]{3,2,1,0:T(8,128)}, f32[32,3,32,128]{3,2,1,0:T(8,128)}, u32[]{:S(2)}, u32[]{:S(2)}) collective-permute-start(f32[32,3,32,128]{3,2,1,0:T(8,128)} %collective-permute-done.20), channel_id=1, source_target_pairs={{0,8},{8,0},{4,12},{12,4},{16,24},{24,16},{20,28},{28,20},{32,40},... | collective-permute-start | bytes 4718600 | tf_op jit(solution)/shard_map/ppermute | solution.py:28
  161.6 41.3 %collective-permute-start.40 = (f32[32,3,32,128]{3,2,1,0:T(8,128)}, f32[32,3,32,128]{3,2,1,0:T(8,128)}, u32[]{:S(2)}, u32[]{:S(2)}) collective-permute-start(f32[32,3,32,128]{3,2,1,0:T(8,128)} %collective-permute-done.21), channel_id=1, source_target_pairs={{0,8},{8,0},{4,12},{12,4},{16,24},{24,16},{20,28},{28,20},{32,40},... | collective-permute-start | bytes 4718600 | tf_op jit(solution)/shard_map/ppermute | solution.py:28
  177.6 26.4 %collective-permute-start.28 = (f32[4,256,512]{2,1,0:T(8,128)}, f32[4,256,512]{2,1,0:T(8,128)}, u32[]{:S(2)}, u32[]{:S(2)}) collective-permute-start(f32[4,256,512]{2,1,0:T(8,128)} %collective-permute-done.27.refs_3_), channel_id=1, source_target_pairs={{0,8},{8,0},{4,12},{12,4},{16,24},{24,16},{20,28},{28,20},{32,40},... | collective-permute-start | bytes 6291464 | tf_op jit(solution)/shard_map/ppermute | solution.py:28
  179.9 21.3 %collective-permute-start.35 = (f32[16,3,32,128]{3,2,1,0:T(8,128)S(1)}, f32[16,3,32,128]{3,2,1,0:T(8,128)}, u32[]{:S(2)}, u32[]{:S(2)}) collective-permute-start(f32[16,3,32,128]{3,2,1,0:T(8,128)S(1)} %slice.39), channel_id=1, source_target_pairs={{0,3},{8,11},{4,7},{12,15},{16,19},{24,27},{20,23},{28,31},{32,35}... | collective-permute-start | bytes 2359304 | tf_op jit(solution)/shard_map/ppermute | solution.py:28
  183.7 19.2 %collective-permute-start.34 = (f32[16,3,32,128]{3,2,1,0:T(8,128)S(1)}, f32[16,3,32,128]{3,2,1,0:T(8,128)}, u32[]{:S(2)}, u32[]{:S(2)}) collective-permute-start(f32[16,3,32,128]{3,2,1,0:T(8,128)S(1)} %slice.38), channel_id=1, source_target_pairs={{0,1},{8,9},{4,5},{12,13},{16,17},{24,25},{20,21},{28,29},{32,33},... | collective-permute-start | bytes 2359304 | tf_op jit(solution)/shard_map/ppermute | solution.py:28
  (18 other events, 133.6 us)
